TPU v7x, 8 devices: a whole 2x2x1 slice. The times are simulated.
8 devices in a mesh: dp: 1 (over z), tp: 2 (over y), sq: 4 (over x, core).
Axes of the slice: x: 2, y: 2, z: 1, core: 2. Of those that a mesh axis runs over, the one named last changes fastest.
Arguments:
- x_steps: bfloat16 [4, 48, 4608], P(None, 'dp')
- positions: int32 [48], P('dp')
- k_cache: bfloat16 [48, 4096, 4, 128], P('dp', 'sq', 'tp')
- v_cache: bfloat16 [48, 4096, 4, 128], P('dp', 'sq', 'tp')
- w_q: bfloat16 [4608, 4608], P(None, 'tp')
- b_q: bfloat16 [4608], P('tp')
- w_k: bfloat16 [4608, 512], P(None, 'tp')
- b_k: bfloat16 [512], P('tp')
- w_v: bfloat16 [4608, 512], P(None, 'tp')
- b_v: bfloat16 [512], P('tp')
- w_o: bfloat16 [4608, 4608], P('tp')
- b_o: bfloat16 [4608], replicated
- ln1_gain: bfloat16 [4608], replicated
- ln1_bias: bfloat16 [4608], replicated
- ln2_gain: bfloat16 [4608], replicated
- ln2_bias: bfloat16 [4608], replicated
- w_fc: bfloat16 [4608, 18432], P(None, 'tp')
- b_fc: bfloat16 [18432], P('tp')
- w_proj: bfloat16 [18432, 4608], P('tp')
- b_proj: bfloat16 [4608], replicated
Outputs:
- output 1: bfloat16 [4, 48, 4608], P(None, 'dp')
- output 2: bfloat16 [48, 4096, 4, 128], P('dp', 'sq', 'tp')
- output 3: bfloat16 [48, 4096, 4, 128], P('dp', 'sq', 'tp')
All inputs are finite; a program needn't handle non-finite values.
Results may differ from a plain program's by a relative error of at most 0.0162477.
Values sent between devices are 32-bit elements.
A program may use at most 1.25 GiB of HBM per device.

v0:
```python
import jax
import jax.numpy as jnp
from jax import lax
from jax.sharding import PartitionSpec as P

ROPE_BASE = 1000000.0
LN_EPS = 1e-5
NEG_BIG = -1e30


def layer_norm(vectors, gain, shift):
    row_mean = jnp.mean(vectors, axis=-1, keepdims=True)
    centered = vectors - row_mean
    row_var = jnp.mean(centered * centered, axis=-1, keepdims=True)
    return centered * lax.rsqrt(row_var + LN_EPS) * gain.astype(jnp.float32) + shift.astype(jnp.float32)


def rope_tables(positions, head_dim):
    half_dim = head_dim // 2
    inv_freq = jnp.power(jnp.float32(ROPE_BASE), -2.0 * jnp.arange(half_dim, dtype=jnp.float32) / head_dim)
    angle = positions.astype(jnp.float32)[..., None] * inv_freq
    return jnp.cos(angle), jnp.sin(angle)


def apply_rope(vectors, cos_t, sin_t):
    half_dim = vectors.shape[-1] // 2
    first = vectors[..., :half_dim]
    second = vectors[..., half_dim:]
    return jnp.concatenate([first * cos_t - second * sin_t, second * cos_t + first * sin_t], axis=-1)


def linear(rows_in, weight, bias):
    return jnp.dot(rows_in, weight, preferred_element_type=jnp.float32) + bias.astype(jnp.float32)


def new_entries(x_in, cur_pos, ln1_gain, ln1_bias, w_q, b_q, w_k, b_k, w_v, b_v, kv_count, head_dim):
    batch = x_in.shape[0]
    group = w_q.shape[1] // (kv_count * head_dim)
    hidden = layer_norm(x_in.astype(jnp.float32), ln1_gain, ln1_bias).astype(jnp.bfloat16)
    query = linear(hidden, w_q, b_q).astype(jnp.bfloat16)
    key_new = linear(hidden, w_k, b_k).astype(jnp.bfloat16)
    val_new = linear(hidden, w_v, b_v).astype(jnp.bfloat16)
    cos_t, sin_t = rope_tables(cur_pos, head_dim)
    q_rot = apply_rope(query.reshape(batch, kv_count, group, head_dim).astype(jnp.float32), cos_t[:, None, None, :], sin_t[:, None, None, :]).astype(jnp.bfloat16)
    k_rot = apply_rope(key_new.reshape(batch, kv_count, head_dim).astype(jnp.float32), cos_t[:, None, :], sin_t[:, None, :]).astype(jnp.bfloat16)
    return q_rot, k_rot, val_new.reshape(batch, kv_count, head_dim)


def partial_attention(q_rot, key_buf, val_buf, slot_ok, head_dim):
    slot_mask = slot_ok[:, None, None, :]
    scores = jnp.einsum("bgrd,bwgd->bgrw", q_rot, key_buf, preferred_element_type=jnp.float32) * head_dim ** -0.5
    scores = jnp.where(slot_mask, scores, NEG_BIG)
    part_max = jnp.max(scores, axis=-1)
    weights = jnp.where(slot_mask, jnp.exp(scores - part_max[..., None]), 0.0)
    part_sum = jnp.sum(weights, axis=-1)
    part_out = jnp.einsum("bgrw,bwgd->bgrd", weights.astype(jnp.bfloat16), val_buf, preferred_element_type=jnp.float32)
    return part_max, part_sum, part_out


def layer_tail(x_in, attn_out, w_o, b_o, ln2_gain, ln2_bias, w_fc, b_fc, w_proj, b_proj):
    attn_proj = lax.psum(jnp.dot(attn_out, w_o, preferred_element_type=jnp.float32), "tp")
    x_mid = (x_in.astype(jnp.float32) + attn_proj + b_o.astype(jnp.float32)).astype(jnp.bfloat16)
    hidden = layer_norm(x_mid.astype(jnp.float32), ln2_gain, ln2_bias).astype(jnp.bfloat16)
    gelu_out = jax.nn.gelu(linear(hidden, w_fc, b_fc), approximate=True).astype(jnp.bfloat16)
    mlp_out = lax.psum(jnp.dot(gelu_out, w_proj, preferred_element_type=jnp.float32), "tp")
    return (x_mid.astype(jnp.float32) + mlp_out + b_proj.astype(jnp.float32)).astype(jnp.bfloat16)


def solution(mesh):
    sq_size = mesh.shape["sq"]
    act_spec = P(None, "dp", None)
    cache_spec = P("dp", "sq", "tp", None)
    col_spec = P(None, "tp")
    row_spec = P("tp", None)
    vec_spec = P("tp")
    rep_spec = P(None)
    in_specs = (act_spec, P("dp"), cache_spec, cache_spec, col_spec, vec_spec, col_spec, vec_spec,
                col_spec, vec_spec, row_spec, rep_spec, rep_spec, rep_spec, rep_spec, rep_spec,
                col_spec, vec_spec, row_spec, rep_spec)
    out_specs = (act_spec, cache_spec, cache_spec)

    def per_device(x_steps, positions, key_buf, val_buf, w_q, b_q, w_k, b_k, w_v, b_v, w_o, b_o,
                   ln1_gain, ln1_bias, ln2_gain, ln2_bias, w_fc, b_fc, w_proj, b_proj):
        steps, batch = x_steps.shape[0], x_steps.shape[1]
        slots_local, kv_local, head_dim = key_buf.shape[1], key_buf.shape[2], key_buf.shape[3]
        slots = slots_local * sq_size
        first_slot = lax.axis_index("sq") * slots_local
        slot_ids = first_slot + jnp.arange(slots_local, dtype=jnp.int32)
        batch_ids = jnp.arange(batch, dtype=jnp.int32)
        outputs = []
        for step_idx in range(steps):
            x_in = x_steps[step_idx]
            cur_pos = positions + step_idx
            q_rot, k_rot, v_heads = new_entries(x_in, cur_pos, ln1_gain, ln1_bias, w_q, b_q, w_k, b_k, w_v, b_v, kv_local, head_dim)
            local_slot = cur_pos % slots - first_slot
            local_slot = jnp.where((local_slot >= 0) & (local_slot < slots_local), local_slot, slots_local)
            key_buf = key_buf.at[batch_ids, local_slot].set(k_rot, mode="drop")
            val_buf = val_buf.at[batch_ids, local_slot].set(v_heads, mode="drop")
            held_pos = cur_pos[:, None] - (cur_pos[:, None] - slot_ids[None, :]) % slots
            part_max, part_sum, part_out = partial_attention(q_rot, key_buf, val_buf, held_pos >= 0, head_dim)
            stats = jnp.concatenate([part_out, part_sum[..., None], part_max[..., None]], axis=-1)
            gathered = lax.all_gather(stats, "sq")
            all_max = gathered[..., head_dim + 1]
            glob_max = jnp.max(all_max, axis=0)
            rescale = jnp.exp(all_max - glob_max)
            total_sum = jnp.sum(rescale * gathered[..., head_dim], axis=0)
            total_out = jnp.sum(rescale[..., None] * gathered[..., :head_dim], axis=0)
            attn_out = (total_out / total_sum[..., None]).astype(jnp.bfloat16).reshape(batch, -1)
            outputs.append(layer_tail(x_in, attn_out, w_o, b_o, ln2_gain, ln2_bias, w_fc, b_fc, w_proj, b_proj))
        return jnp.stack(outputs), key_buf, val_buf

    return jax.shard_map(per_device, mesh=mesh, in_specs=in_specs, out_specs=out_specs, check_vma=False)
```

profile of v0, /device:TPU:0, one launch (start us, length us, event | category | flops | bytes accessed | tf_op | source)
XLA Modules:
  0.0 839.2 jit_solution(13471597563522008926)
XLA Ops:
  7.2 20.4 %copy.269 = bf16[48,1024,2,128]{3,2,1,0:T(2,128)(2,1)} copy(bf16[48,1024,2,128]{3,2,1,0:T(2,128)(2,1)} %param.22) | data formatting | bytes 50331648
  87.9 14.7 %fusion.16 = (f32[48,2,9]{2,1,0:T(2,128)}, f32[48,2,9,1024]{3,2,1,0:T(8,128)}) fusion(pred[48,1024]{1,0:T(8,128)(4,1)} %get-tuple-element.65, bf16[48,1024,2,128]{3,2,1,0:T(2,128)(2,1)} %scatter_fusion, bf16[48,2,9,64]{3,2,1,0:T(8,128)(2,1)} %get-tuple-element.46, bf16[48,2,9,64]{3,2,1,0:T(8,128)(2,1)S(1)} %get-tuple-element.45), kind=kOutput, calls=%fused_computation.36 | convolution fusion | flops 229588128 | bytes 28978560 | tf_op jit(solution)/shard_map/bgrd,bwgd->bgrw/dot_general | solution.py:51
  109.1 19.2 %fusion.17 = (f32[48,2,9]{2,1,0:T(2,128)S(1)}, f32[48,2,9,1024]{3,2,1,0:T(8,128)}) fusion(pred[48,1024]{1,0:T(8,128)(4,1)} %get-tuple-element.66, bf16[48,1024,2,128]{3,2,1,0:T(2,128)(2,1)} %scatter_fusion.2, bf16[48,2,9,64]{3,2,1,0:T(8,128)(2,1)S(1)} %copy-done.15, bf16[48,2,9,64]{3,2,1,0:T(8,128)(2,1)S(1)} %copy-done.14), kind=kOutput, calls=%fused_computation.37 | convolution fusion | flops 229588128 | bytes 28978560 | tf_op jit(solution)/shard_map/bgrd,bwgd->bgrw/dot_general | solution.py:51
  145.8 14.3 %fusion.12 = f32[48,2,9,128]{3,2,1,0:T(8,128)} fusion(bf16[48,1024,2,128]{3,2,1,0:T(2,128)(2,1)} %scatter_fusion.1, f32[48,2,9,1024]{3,2,1,0:T(8,128)} %get-tuple-element.101, f32[48,2,9]{2,1,0:T(2,128)S(1)} %copy-done.24, pred[48,1024]{1,0:T(8,128)(4,1)S(1)} %copy-done.19), kind=kOutput, calls=%fused_computation.20 | convolution fusion | flops 230916096 | bytes 29199744 | tf_op jit(solution)/shard_map/bgrw,bwgd->bgrd/dot_general | solution.py:56
  176.9 14.4 %fusion.8 = f32[48,2,9,128]{3,2,1,0:T(8,128)S(1)} fusion(bf16[48,1024,2,128]{3,2,1,0:T(2,128)(2,1)} %scatter_fusion.3, f32[48,2,9,1024]{3,2,1,0:T(8,128)} %get-tuple-element.99, f32[48,2,9]{2,1,0:T(2,128)S(1)} %get-tuple-element.98, pred[48,1024]{1,0:T(8,128)(4,1)S(1)} %copy-done.18), kind=kOutput, calls=%fused_computation.16 | convolution fusion | flops 230916096 | bytes 29199744 | tf_op jit(solution)/shard_map/bgrw,bwgd->bgrd/dot_general | solution.py:56
  195.1 11.9 %fusion.33 = f32[48,2304]{1,0:T(8,128)} fusion(bf16[4608,2304]{1,0:T(8,128)(2,1)} %param.24, f32[2304]{0:T(1024)S(1)} %copy-done.26, f32[48]{0:T(128)S(1)} %add_rsqrt_fusion.3, f32[48]{0:T(128)S(1)} %copy-done.42, f32[4608]{0:T(1024)S(1)} %copy-done.23, f32[4608]{0:T(1024)S(1)} %copy-done.21, bf16[4,48,4608]{2,1,0:T(8,128)(2,1)} %param.20), kind=kOutput, calls=%fused_computation.57 | convolution fusion | flops 1020874752 | bytes 22164864 | tf_op jit(solution)/shard_map/dot_general | solution.py:33
  225.5 15.9 %fusion.18 = (f32[48,2,9]{2,1,0:T(2,128)S(1)}, f32[48,2,9,1024]{3,2,1,0:T(8,128)}) fusion(pred[48,1024]{1,0:T(8,128)(4,1)S(1)} %copy-done.17, bf16[48,1024,2,128]{3,2,1,0:T(2,128)(2,1)} %scatter_fusion.4, bf16[48,2,9,64]{3,2,1,0:T(8,128)(2,1)S(1)} %get-tuple-element.50, bf16[48,2,9,64]{3,2,1,0:T(8,128)(2,1)S(1)} %get-tuple-element.49), kind=kOutput, calls=%fused_computation.38 | convolution fusion | flops 229588128 | bytes 28978560 | tf_op jit(solution)/shard_map/bgrd,bwgd->bgrw/dot_general | solution.py:51
  248.3 16.4 %fusion.19 = (f32[48,2,9]{2,1,0:T(2,128)S(1)}, f32[48,2,9,1024]{3,2,1,0:T(8,128)}) fusion(pred[48,1024]{1,0:T(8,128)(4,1)S(1)} %copy-done.16, bf16[48,1024,2,128]{3,2,1,0:T(2,128)(2,1)} %scatter_fusion.6, bf16[48,2,9,64]{3,2,1,0:T(8,128)(2,1)S(1)} %get-tuple-element.52, bf16[48,2,9,64]{3,2,1,0:T(8,128)(2,1)S(1)} %get-tuple-element.51), kind=kOutput, calls=%fused_computation.39 | convolution fusion | flops 229588128 | bytes 28978560 | tf_op jit(solution)/shard_map/bgrd,bwgd->bgrw/dot_general | solution.py:51
  282.0 14.5 %fusion.4 = f32[48,2,9,128]{3,2,1,0:T(8,128)S(1)} fusion(bf16[48,1024,2,128]{3,2,1,0:T(2,128)(2,1)} %scatter_fusion.5, f32[48,2,9,1024]{3,2,1,0:T(8,128)} %get-tuple-element.97, f32[48,2,9]{2,1,0:T(2,128)S(1)} %get-tuple-element.96, pred[48,1024]{1,0:T(8,128)(4,1)S(1)} %copy-done.17), kind=kOutput, calls=%fused_computation.12 | convolution fusion | flops 230916096 | bytes 29199744 | tf_op jit(solution)/shard_map/bgrw,bwgd->bgrd/dot_general | solution.py:56
  310.0 14.4 %fusion = f32[48,2,9,128]{3,2,1,0:T(8,128)S(1)} fusion(bf16[48,1024,2,128]{3,2,1,0:T(2,128)(2,1)} %scatter_fusion.7, f32[48,2,9,1024]{3,2,1,0:T(8,128)} %get-tuple-element.95, f32[48,2,9]{2,1,0:T(2,128)S(1)} %get-tuple-element.94, pred[48,1024]{1,0:T(8,128)(4,1)S(1)} %copy-done.16), kind=kOutput, calls=%fused_computation.8 | convolution fusion | flops 230916096 | bytes 29199744 | tf_op jit(solution)/shard_map/bgrw,bwgd->bgrd/dot_general | solution.py:56
  345.2 12.1 %fusion.344 = f32[48,4608]{1,0:T(8,128)} fusion(bf16[48,2304]{1,0:T(8,128)(2,1)S(1)} %convert_element_type.326, bf16[2304,4608]{1,0:T(8,128)(2,1)} %param.30), kind=kOutput, calls=%fused_computation.488 | convolution fusion | flops 1019215872 | bytes 22339584 | tf_op jit(solution)/shard_map/dot_general | solution.py:61
  357.8 11.7 %fusion.345 = f32[48,4608]{1,0:T(8,128)} fusion(bf16[48,2304]{1,0:T(8,128)(2,1)S(1)} %convert_element_type.350, bf16[2304,4608]{1,0:T(8,128)(2,1)} %param.30), kind=kOutput, calls=%fused_computation.489 | convolution fusion | flops 1019215872 | bytes 22339584 | tf_op jit(solution)/shard_map/dot_general | solution.py:61
  369.5 11.7 %fusion.346 = f32[48,4608]{1,0:T(8,128)} fusion(bf16[48,2304]{1,0:T(8,128)(2,1)S(1)} %convert_element_type.369, bf16[2304,4608]{1,0:T(8,128)(2,1)} %param.30), kind=kOutput, calls=%fused_computation.490 | convolution fusion | flops 1019215872 | bytes 22339584 | tf_op jit(solution)/shard_map/dot_general | solution.py:61
  387.5 11.7 %fusion.347 = f32[48,4608]{1,0:T(8,128)} fusion(bf16[48,2304]{1,0:T(8,128)(2,1)S(1)} %convert_element_type.388, bf16[2304,4608]{1,0:T(8,128)(2,1)} %param.30), kind=kOutput, calls=%fused_computation.491 | convolution fusion | flops 1019215872 | bytes 22339584 | tf_op jit(solution)/shard_map/dot_general | solution.py:61
  400.0 92.7 %all-reduce.7.cloned.1.call-done = (f32[48,4608]{1,0:T(8,128)}, f32[48,4608]{1,0:T(8,128)}, f32[48,4608]{1,0:T(8,128)}, f32[48,4608]{1,0:T(8,128)}) async-done(((f32[48,4608]{1,0:T(8,128)}, f32[48,4608]{1,0:T(8,128)}, f32[48,4608]{1,0:T(8,128)}, f32[48,4608]{1,0:T(8,128)}), (f32[48,4608]{1,0:T(8,128)}, f32[48,4608]{1,0:T(8,128)}, f32[48,4608]{1,0:T(8,128)}, ...) | async-done | bytes 3538960 | tf_op jit(solution)/shard_map/psum | solution.py:61
  495.9 30.1 %fusion.67.clone.4 = bf16[48,9216]{1,0:T(8,128)(2,1)S(1)} fusion(bf16[4608,9216]{1,0:T(8,128)(2,1)} %param.36, f32[9216]{0:T(1024)S(1)} %convert_element_type.333, bf16[48,4608]{1,0:T(8,128)(2,1)S(1)} %get-tuple-element.32, f32[4608]{0:T(1024)S(1)} %convert_element_type.331, f32[4608]{0:T(1024)S(1)} %convert_element_type.330, ...), kind=kOutput, calls=%fused_computation.91.clone.clone.clone.1 | convolution fusion | flops 4082614272 | bytes 86335872 | tf_op jit(solution)/shard_map/dot_general | solution.py:33
  526.1 30.1 %fusion.76.clone.4 = bf16[48,9216]{1,0:T(8,128)(2,1)S(1)} fusion(bf16[4608,9216]{1,0:T(8,128)(2,1)} %param.36, f32[9216]{0:T(1024)S(1)} %convert_element_type.333, bf16[48,4608]{1,0:T(8,128)(2,1)S(1)} %get-tuple-element.40, f32[48]{0:T(128)S(1)} %add_rsqrt_fusion.4, f32[48]{0:T(128)S(1)} %broadcast_multiply_fusion.4, ...), kind=kOutput, calls=%fused_computation.100.clone.clone.clone.1 | convolution fusion | flops 4082614272 | bytes 86335872 | tf_op jit(solution)/shard_map/dot_general | solution.py:33
  556.2 30.4 %fusion.68 = f32[48,4608]{1,0:T(8,128)} fusion(bf16[9216,4608]{1,0:T(8,128)(2,1)} %param.38, bf16[48,9216]{1,0:T(8,128)(2,1)S(1)} %fusion.67.clone.4), kind=kOutput, calls=%fused_computation.92 | convolution fusion | flops 4076863488 | bytes 86704128 | tf_op jit(solution)/shard_map/dot_general | solution.py:65
  586.6 30.5 %fusion.77 = f32[48,4608]{1,0:T(8,128)} fusion(bf16[9216,4608]{1,0:T(8,128)(2,1)} %param.38, bf16[48,9216]{1,0:T(8,128)(2,1)S(1)} %fusion.76.clone.4), kind=kOutput, calls=%fused_computation.101 | convolution fusion | flops 4076863488 | bytes 86704128 | tf_op jit(solution)/shard_map/dot_general | solution.py:65
  617.4 30.1 %fusion.85.clone.2 = bf16[48,9216]{1,0:T(8,128)(2,1)S(1)} fusion(bf16[4608,9216]{1,0:T(8,128)(2,1)} %param.36, f32[9216]{0:T(1024)S(1)} %convert_element_type.333, bf16[48,4608]{1,0:T(8,128)(2,1)S(1)} %get-tuple-element.42, f32[48]{0:T(128)S(1)} %add_rsqrt_fusion.2, f32[48]{0:T(128)S(1)} %broadcast_multiply_fusion.2, ...), kind=kOutput, calls=%fused_computation.109.clone.clone.clone | convolution fusion | flops 4082614272 | bytes 86335872 | tf_op jit(solution)/shard_map/dot_general | solution.py:33
  647.6 30.4 %fusion.86 = f32[48,4608]{1,0:T(8,128)} fusion(bf16[9216,4608]{1,0:T(8,128)(2,1)} %param.38, bf16[48,9216]{1,0:T(8,128)(2,1)S(1)} %fusion.85.clone.2), kind=kOutput, calls=%fused_computation.110 | convolution fusion | flops 4076863488 | bytes 86704128 | tf_op jit(solution)/shard_map/dot_general | solution.py:65
  678.2 30.4 %fusion.94.clone.2 = bf16[48,9216]{1,0:T(8,128)(2,1)S(1)} fusion(bf16[4608,9216]{1,0:T(8,128)(2,1)} %param.36, f32[9216]{0:T(1024)S(1)} %convert_element_type.333, bf16[48,4608]{1,0:T(8,128)(2,1)S(1)} %get-tuple-element.44, f32[48]{0:T(128)S(1)} %add_rsqrt_fusion, f32[48]{0:T(128)S(1)} %broadcast_multiply_fusion, ...), kind=kOutput, calls=%fused_computation.118.clone.clone.clone | convolution fusion | flops 4082614272 | bytes 86335872 | tf_op jit(solution)/shard_map/dot_general | solution.py:33
  708.6 30.3 %fusion.95 = f32[48,4608]{1,0:T(8,128)} fusion(bf16[9216,4608]{1,0:T(8,128)(2,1)} %param.38, bf16[48,9216]{1,0:T(8,128)(2,1)S(1)} %fusion.94.clone.2), kind=kOutput, calls=%fused_computation.119 | convolution fusion | flops 4076863488 | bytes 86704128 | tf_op jit(solution)/shard_map/dot_general | solution.py:65
  739.7 88.0 %all-reduce.5.cloned.1.call-done = (f32[48,4608]{1,0:T(8,128)}, f32[48,4608]{1,0:T(8,128)}, f32[48,4608]{1,0:T(8,128)}, f32[48,4608]{1,0:T(8,128)}) async-done(((f32[48,4608]{1,0:T(8,128)}, f32[48,4608]{1,0:T(8,128)}, f32[48,4608]{1,0:T(8,128)}, f32[48,4608]{1,0:T(8,128)}), (f32[48,4608]{1,0:T(8,128)}, f32[48,4608]{1,0:T(8,128)}, f32[48,4608]{1,0:T(8,128)}, ...) | async-done | bytes 3538960 | tf_op jit(solution)/shard_map/psum | solution.py:65
  (269 shorter events, 197.0 us)
Async XLA Ops:
  7.2 39.2 %copy-start = (bf16[4608,256]{1,0:T(8,128)(2,1)S(1)}, bf16[4608,256]{1,0:T(8,128)(2,1)}, u32[]{:S(2)}) copy-start(bf16[4608,256]{1,0:T(8,128)(2,1)} %param.26) | copy-start | bytes 7077892
  7.2 319.5 %all-gather.9.cloned.1.call-start = ((), (), s32[]{:S(2)}) async-start(), calls=%async_computation | async-start | bytes 4423680 | tf_op jit(solution)/shard_map/all_gather | solution.py:102
  7.2 24.3 %copy-start.5 = (bf16[48,1024,2,128]{3,2,1,0:T(2,128)(2,1)S(1)}, bf16[48,1024,2,128]{3,2,1,0:T(2,128)(2,1)}, u32[]{:S(2)}) copy-start(bf16[48,1024,2,128]{3,2,1,0:T(2,128)(2,1)} %param.23) | copy-start | bytes 75497472
  43.6 14.5 %copy-start.43 = (f32[48]{0:T(128)}, f32[48]{0:T(128)S(1)}, u32[]{:S(2)}) copy-start(f32[48]{0:T(128)S(1)} %broadcast_multiply_fusion.5) | copy-start | bytes 580
  87.9 21.2 %copy-start.14 = (bf16[48,2,9,64]{3,2,1,0:T(8,128)(2,1)S(1)}, bf16[48,2,9,64]{3,2,1,0:T(8,128)(2,1)}, u32[]{:S(2)}) copy-start(bf16[48,2,9,64]{3,2,1,0:T(8,128)(2,1)} %get-tuple-element.47) | copy-start | bytes 331780
  87.9 21.2 %copy-start.15 = (bf16[48,2,9,64]{3,2,1,0:T(8,128)(2,1)S(1)}, bf16[48,2,9,64]{3,2,1,0:T(8,128)(2,1)}, u32[]{:S(2)}) copy-start(bf16[48,2,9,64]{3,2,1,0:T(8,128)(2,1)} %get-tuple-element.48) | copy-start | bytes 331780
  109.1 19.2 %copy-start.18 = (pred[48,1024]{1,0:T(8,128)(4,1)S(1)}, pred[48,1024]{1,0:T(8,128)(4,1)}, u32[]{:S(2)}) copy-start(pred[48,1024]{1,0:T(8,128)(4,1)} %get-tuple-element.66) | copy-start | bytes 147460
  109.1 19.2 %copy-start.19 = (pred[48,1024]{1,0:T(8,128)(4,1)S(1)}, pred[48,1024]{1,0:T(8,128)(4,1)}, u32[]{:S(2)}) copy-start(pred[48,1024]{1,0:T(8,128)(4,1)} %get-tuple-element.65) | copy-start | bytes 147460
  109.1 19.2 %copy-start.24 = (f32[48,2,9]{2,1,0:T(2,128)S(1)}, f32[48,2,9]{2,1,0:T(2,128)}, u32[]{:S(2)}) copy-start(f32[48,2,9]{2,1,0:T(2,128)} %get-tuple-element.100) | copy-start | bytes 10372
  165.1 167.9 %all-gather.11.cloned.1.call-start = ((), (), s32[]{:S(2)}) async-start(), calls=%async_computation.1 | async-start | bytes 4423680 | tf_op jit(solution)/shard_map/all_gather | solution.py:102
  176.9 14.4 %copy-start.10 = (f32[48,2,9,1]{3,2,1,0:T(8,128)S(1)}, f32[48,2,9,1]{3,2,1,0:T(8,128)}, u32[]{:S(2)}) copy-start(f32[48,2,9,1]{3,2,1,0:T(8,128)} %copy.189) | copy-start | bytes 10372
  193.4 146.0 %all-gather.13.cloned.1.call-start = ((), (), s32[]{:S(2)}) async-start(), calls=%async_computation.2 | async-start | bytes 4423680 | tf_op jit(solution)/shard_map/all_gather | solution.py:102
  195.1 12.0 %copy-start.52 = (f32[48]{0:T(128)S(1)}, f32[48]{0:T(128)}, u32[]{:S(2)}) copy-start(f32[48]{0:T(128)} %get-tuple-element.15) | copy-start | bytes 580
  195.1 12.0 %copy-start.3 = (bf16[4,48,4608]{2,1,0:T(8,128)(2,1)S(1)}, bf16[4,48,4608]{2,1,0:T(8,128)(2,1)}, u32[]{:S(2)}) copy-start(bf16[4,48,4608]{2,1,0:T(8,128)(2,1)} %param.20) | copy-start | bytes 5308420
  225.5 22.8 %copy-start.16 = (pred[48,1024]{1,0:T(8,128)(4,1)S(1)}, pred[48,1024]{1,0:T(8,128)(4,1)}, u32[]{:S(2)}) copy-start(pred[48,1024]{1,0:T(8,128)(4,1)} %get-tuple-element.68) | copy-start | bytes 147460
  282.0 14.5 %copy-start.11 = (f32[48,2,9,1]{3,2,1,0:T(8,128)S(1)}, f32[48,2,9,1]{3,2,1,0:T(8,128)}, u32[]{:S(2)}) copy-start(f32[48,2,9,1]{3,2,1,0:T(8,128)} %copy.198) | copy-start | bytes 10372
  298.6 82.6 %all-gather.15.cloned.1.call-start = ((), (), s32[]{:S(2)}) async-start(), calls=%async_computation.3 | async-start | bytes 4423680 | tf_op jit(solution)/shard_map/all_gather | solution.py:102
  310.0 14.4 %copy-start.12 = (f32[48,2,9,1]{3,2,1,0:T(8,128)S(1)}, f32[48,2,9,1]{3,2,1,0:T(8,128)}, u32[]{:S(2)}) copy-start(f32[48,2,9,1]{3,2,1,0:T(8,128)} %copy.207) | copy-start | bytes 10372
  326.4 166.2 %all-reduce.7.cloned.1.call-start = ((), (), s32[]{:S(2)}) async-start(), calls=%async_computation.5 | async-start | bytes 7077888 | tf_op jit(solution)/shard_map/psum | solution.py:61
  399.2 428.5 %all-reduce.5.cloned.1.call-start = ((), (), s32[]{:S(2)}) async-start(), calls=%async_computation.4 | async-start | bytes 7077888 | tf_op jit(solution)/shard_map/psum | solution.py:65
  495.3 30.8 %copy-start.6 = (bf16[48,4608]{1,0:T(8,128)(2,1)}, bf16[48,4608]{1,0:T(8,128)(2,1)S(1)}, u32[]{:S(2)}) copy-start(bf16[48,4608]{1,0:T(8,128)(2,1)S(1)} %get-tuple-element.32) | copy-start | bytes 1327108
  495.3 122.1 %copy-start.8 = (bf16[48,4608]{1,0:T(8,128)(2,1)}, bf16[48,4608]{1,0:T(8,128)(2,1)S(1)}, u32[]{:S(2)}) copy-start(bf16[48,4608]{1,0:T(8,128)(2,1)S(1)} %get-tuple-element.42) | copy-start | bytes 1327108
  495.3 182.9 %copy-start.9 = (bf16[48,4608]{1,0:T(8,128)(2,1)}, bf16[48,4608]{1,0:T(8,128)(2,1)S(1)}, u32[]{:S(2)}) copy-start(bf16[48,4608]{1,0:T(8,128)(2,1)S(1)} %get-tuple-element.44) | copy-start | bytes 1327108
  739.0 88.7 %copy-start.7 = (bf16[48,4608]{1,0:T(8,128)(2,1)S(1)}, bf16[48,4608]{1,0:T(8,128)(2,1)}, u32[]{:S(2)}) copy-start(bf16[48,4608]{1,0:T(8,128)(2,1)} %copy-done.6) | copy-start | bytes 1327108
  (41 other events, 248.9 us)
Sparse Core Ops, SparseCore 0:
  165.2 31.1 all-gather.8
  197.9 27.7 all-gather.10
  298.7 32.1 all-gather.12
  332.8 27.7 all-gather.14
  399.3 93.2 all-reduce.6
  739.1 88.5 all-reduce.4
where the time goes:
time: 849 us; the launch traced here: 839 us
  matrix products  466 us (55%)
  waiting for transfers between devices  181 us (21%)
  local copies, waits for them, and re-layouts  120 us (14%)
  other arithmetic  56.2 us (7%)
  between operations  15.8 us (2%)
    dot_general x16, matrix products, linear(): jnp.dot(rows_in, weight, preferred_element_type=jnp.float32)  173 us
    dot_general x4, matrix products, layer_tail(): jnp.dot(gelu_out, w_proj, preferred_element_type=jnp.float32)  122 us
    psum x1, waiting for transfers between devices, layer_tail(): lax.psum(jnp.dot(attn_out, w_o, preferred_element_type=jnp.float32), 'tp')  92.7 us
    psum x1, waiting for transfers between devices, layer_tail(): lax.psum(jnp.dot(gelu_out, w_proj, preferred_element_type=jnp.float32), '...  88 us
    dot_general x4, matrix products, partial_attention(): jnp.einsum('bgrd,bwgd->bgrw', q_rot, key_buf, preferred_element_type=jnp....  66.2 us
    dot_general x4, matrix products, partial_attention(): jnp.einsum('bgrw,bwgd->bgrd', weights.astype(jnp.bfloat16), val_buf, pref...  57.6 us
    dot_general x4, matrix products, layer_tail(): jnp.dot(attn_out, w_o, preferred_element_type=jnp.float32)  47.2 us
    unnamed x120, local copies, waits for them, and re-layouts  34.6 us
  transfers between devices with their start and end apart: 6, of which 2 were waited for; matrix products, arithmetic and copies ran while one was open for 26% of the time, Pallas kernels for 0%

commit v1 on v0

v1 whole, which is shorter than its diff:
```python
import functools
import math

import jax
import jax.numpy as jnp
from jax import lax
from jax.experimental import pallas as pl
from jax.experimental.pallas import tpu as pltpu
from jax.sharding import PartitionSpec as P

ROPE_BASE = 1000000.0
LN_EPS = 1e-5
NEG_BIG = -1e30
NEG_HALF = -1e29
LOG2E = 1.4426950408889634
VMEM_CAP = 67_043_328
F32 = jnp.float32
BF16 = jnp.bfloat16
LANES = 128


def layer_norm(vectors, gain, shift):
    row_mean = jnp.mean(vectors, axis=-1, keepdims=True)
    centered = vectors - row_mean
    row_var = jnp.mean(centered * centered, axis=-1, keepdims=True)
    return centered * lax.rsqrt(row_var + LN_EPS) * gain.astype(F32) + shift.astype(F32)


def rope_tables(positions, head_dim):
    half_dim = head_dim // 2
    inv_freq = jnp.power(F32(ROPE_BASE), -2.0 * jnp.arange(half_dim, dtype=F32) / head_dim)
    angle = positions.astype(F32)[..., None] * inv_freq
    return jnp.cos(angle), jnp.sin(angle)


def apply_rope(vectors, cos_t, sin_t):
    half_dim = vectors.shape[-1] // 2
    first = vectors[..., :half_dim]
    second = vectors[..., half_dim:]
    return jnp.concatenate([first * cos_t - second * sin_t, second * cos_t + first * sin_t], axis=-1)


def linear(rows_in, weight, bias):
    return jnp.einsum("sbd,dn->sbn", rows_in, weight, preferred_element_type=F32) + bias.astype(F32)


def attend_kernel(cfg, meta, q_ref, kn_ref, vn_ref, k_ref, v_ref, ko_ref, vo_ref, o_ref, lse_ref, o_rows, stat_rows):
    steps, kvs, group, per, slots = cfg
    rows = k_ref.shape[1]
    tile = steps * kvs
    inner = pl.program_id(1)
    base = (pl.program_id(0) * pl.num_programs(1) + inner) * per
    first = meta[0]
    coef = LANES ** -0.5 * LOG2E
    contract_last = (((1,), (1,)), ((), ()))

    sub = lax.broadcasted_iota(jnp.int32, (tile, rows), 0)
    lane = lax.broadcasted_iota(jnp.int32, (tile, rows), 1)
    own_head = (lane % kvs) == (sub // steps)
    slot = first + lane // kvs
    sub2 = lax.broadcasted_iota(jnp.int32, (tile, kn_ref.shape[1]), 0)
    lane2 = lax.broadcasted_iota(jnp.int32, (tile, kn_ref.shape[1]), 1)
    new_head = (lane2 % kvs) == (sub2 // steps)
    new_step = lane2 // kvs
    stat_sub = lax.broadcasted_iota(jnp.int32, (tile, LANES), 0)
    stat_lane = lax.broadcasted_iota(jnp.int32, (tile, LANES), 1) - (stat_sub // steps) * group
    win_row = lax.broadcasted_iota(jnp.int32, (16, LANES), 0)

    for one in range(per):
        pos = meta[1 + base + one]
        q = q_ref[one]
        for src, dst, new in ((k_ref, ko_ref, kn_ref), (v_ref, vo_ref, vn_ref)):
            dst[one] = src[one]
            fresh = new[one].astype(F32)
            for t in range(steps):
                row = kvs * ((pos + t) % slots - first)
                start = pl.multiple_of(jnp.clip(row // 16, 0, rows // 16 - 1) * 16, 16)
                window = dst[one, pl.ds(start, 16), :].astype(F32)
                offset = win_row + (start - row)
                for h in range(kvs):
                    window = jnp.where(offset == h, fresh[t * kvs + h:t * kvs + h + 1, :], window)
                dst[one, pl.ds(start, 16), :] = window.astype(BF16)
        ahead = (slot - pos) & (slots - 1)
        bias = jnp.where(own_head & (slot < pos) & (ahead > sub % steps), 0.0, NEG_BIG).astype(F32)
        new_slot = ((pos + new_step) & (slots - 1)) - first
        here = (new_slot >= 0) & (new_slot < rows // kvs)
        bias2 = jnp.where(new_head & (new_step <= sub2 % steps) & here, 0.0, NEG_BIG).astype(F32)
        raw = lax.dot_general(q, k_ref[one], contract_last, preferred_element_type=F32)
        raw2 = lax.dot_general(q, kn_ref[one], contract_last, preferred_element_type=F32)
        score = raw.reshape(group, tile, rows) * coef + bias[None]
        score2 = raw2.reshape(group, tile, -1) * coef + bias2[None]
        top = jnp.maximum(jnp.max(score, axis=-1, keepdims=True), jnp.max(score2, axis=-1, keepdims=True))
        top = jnp.maximum(top, NEG_HALF)
        w = jnp.exp2(score - top)
        w2 = jnp.exp2(score2 - top)
        total = jnp.sum(w, axis=-1, keepdims=True) + jnp.sum(w2, axis=-1, keepdims=True)
        out = jnp.dot(w.reshape(group * tile, rows).astype(BF16), v_ref[one], preferred_element_type=F32)
        out = out + jnp.dot(w2.reshape(group * tile, -1).astype(BF16), vn_ref[one], preferred_element_type=F32)
        some = total > 0.0
        safe = jnp.where(some, total, 1.0)
        lse = jnp.where(some, top + jnp.log2(safe), NEG_BIG)
        out = out.reshape(group, tile, LANES) * (1.0 / safe)
        stats = jnp.zeros((tile, LANES), F32)
        for i in range(group):
            stats = jnp.where(stat_lane == i, lse[i], stats)
        seat = inner * per + one
        o_rows[pl.ds(pl.multiple_of(seat * (group * tile), 8), group * tile), :] = out.reshape(group * tile, LANES)
        stat_rows[pl.ds(pl.multiple_of(seat * tile, 8), tile), :] = stats

    @pl.when(inner == pl.num_programs(1) - 1)
    def _():
        for s in range(steps):
            lse_ref[s] = sum(stat_rows[pl.ds(h * steps + s, 8, stride=tile), :] for h in range(kvs))
            for h in range(kvs):
                for i in range(group):
                    col = (h * group + i) * LANES
                    o_ref[s, :, col:col + LANES] = o_rows[pl.ds(i * tile + h * steps + s, 8, stride=group * tile), :]


def attend(meta, q, k_new, v_new, k_rows, v_rows, steps, kvs, group, slots):
    batch, rows, dim = k_rows.shape
    per, eight = 2, 8
    inner = eight // per
    cfg = (steps, kvs, group, per, slots)
    seq = lambda g, j, meta: (g * inner + j, 0, 0)
    wide = lambda g, j, meta: (0, g, 0)
    cache_spec = pl.BlockSpec((per, rows, dim), seq)
    return pl.pallas_call(
        functools.partial(attend_kernel, cfg),
        grid_spec=pltpu.PrefetchScalarGridSpec(
            num_scalar_prefetch=1,
            grid=(batch // eight, inner),
            in_specs=[
                pl.BlockSpec((per, q.shape[1], dim), seq),
                pl.BlockSpec((per, k_new.shape[1], dim), seq),
                pl.BlockSpec((per, v_new.shape[1], dim), seq),
                cache_spec,
                cache_spec,
            ],
            out_specs=[
                cache_spec,
                cache_spec,
                pl.BlockSpec((steps, eight, kvs * group * dim), wide),
                pl.BlockSpec((steps, eight, LANES), wide),
            ],
            scratch_shapes=[
                pltpu.VMEM((eight * q.shape[1], dim), F32),
                pltpu.VMEM((eight * steps * kvs, dim), F32),
            ],
        ),
        out_shape=[
            jax.ShapeDtypeStruct(k_rows.shape, BF16),
            jax.ShapeDtypeStruct(v_rows.shape, BF16),
            jax.ShapeDtypeStruct((steps, batch, kvs * group * dim), F32),
            jax.ShapeDtypeStruct((steps, batch, LANES), F32),
        ],
        compiler_params=pltpu.CompilerParams(dimension_semantics=("arbitrary", "arbitrary")),
        cost_estimate=pl.CostEstimate(flops=4 * batch * rows * q.shape[1] * dim, bytes_accessed=8 * batch * rows * dim,
                                      transcendentals=batch * rows * q.shape[1]),
        name="attend",
    )(meta, q, k_new, v_new, k_rows, v_rows)


CHUNK = 512
RING = 6
(C_PEER_O, C_STAT, C_OWN_O, C_X_O, C_X_E, C_RS_CORE, C_RS_Y, C_AG_Y, C_AG_OWN, C_AG_FWD) = range(10)
(J_RS_CORE, J_RS_Y, J_OWN_Y, J_OWN_X, J_OWN_C, J_FWD_X, J_FWD_C, J_XOWN_C, J_XFWD_C) = range(9)


def tail_kernel(cfg, o_ref, lse_ref, x_ref, wo_hbm, wfc_hbm, wproj_hbm, bo_ref, gain_ref, shift_ref, bfc_ref, bproj_ref,
                y_ref,
                in_o_peer, in_o_own, in_lse, to_x, to_x_e, mine, in_x, in_x_e, a_buf,
                wo_buf, part, in_part, half_sum, in_y, x_buf, x_mid, hid, hid_b,
                ring, g_buf, p_chunk, in_rc, p_half, in_ry, y_all,
                send_a, recv_a, send_j, recv_j, wo_sem, x_sem, ring_sem):
    steps, batch, group, chunks, kvs = cfg
    half = batch // 2
    quarter = half
    d_model = wo_hbm.shape[1]
    head_cols = group * LANES
    ff_own = wfc_hbm.shape[1] // 2
    y = lax.axis_index("tp")
    sq = lax.axis_index("sq")
    x, c = sq // 2, sq % 2
    sib = {"sq": x * 2 + 1 - c}
    xpeer = {"sq": (1 - x) * 2 + c}
    ypeer = {"tp": 1 - y}
    MESH = pl.DeviceIdType.MESH
    my_step = 2 * c + y

    def load_item(item, slot):
        @pl.when(item < chunks)
        def _():
            col = pl.multiple_of(c * ff_own + item * CHUNK, CHUNK)
            pltpu.make_async_copy(wfc_hbm.at[:, pl.ds(col, CHUNK)], ring.at[slot], ring_sem.at[slot]).start()

        @pl.when(item >= chunks)
        def _():
            col = pl.multiple_of((item - chunks) * CHUNK, CHUNK)
            row = pl.multiple_of(c * ff_own, CHUNK)
            pltpu.make_async_copy(wproj_hbm.at[pl.ds(row, ff_own), pl.ds(col, CHUNK)], ring.at[slot], ring_sem.at[slot]).start()

    def wait_item(slot):
        pltpu.make_async_copy(wfc_hbm.at[:, pl.ds(0, CHUNK)], ring.at[slot], ring_sem.at[slot]).wait()

    wo_copy = pltpu.make_async_copy(wo_hbm.at[pl.ds(pl.multiple_of(c * head_cols, LANES), head_cols), :], wo_buf, wo_sem)
    wo_copy.start()
    x_copy = pltpu.make_async_copy(x_ref.at[my_step, pl.ds(pl.multiple_of(x * half, 8), half), :], x_buf, x_sem)
    x_copy.start()
    for k in range(RING):
        load_item(jnp.int32(k), k)

    barrier = pltpu.get_barrier_semaphore()
    for who in (sib, xpeer, ypeer):
        pl.semaphore_signal(barrier, inc=1, device_id=who, device_id_type=MESH)
    pl.semaphore_wait(barrier, 3)

    def remote(src, dst, kind, who):
        return pltpu.make_async_remote_copy(src_ref=src, dst_ref=dst, send_sem=send_a.at[kind], recv_sem=recv_a.at[kind],
                                            device_id=who, device_id_type=MESH)

    peer_rows = pl.ds(pl.multiple_of((1 - x) * half, 8), half)
    own_rows = pl.ds(pl.multiple_of(x * half, 8), half)
    sib_cols = pl.ds(pl.multiple_of((1 - c) * head_cols, LANES), head_cols)
    cp_stat = remote(lse_ref, in_lse, C_STAT, sib)
    cp_peer = remote(o_ref.at[:, peer_rows, sib_cols], in_o_peer, C_PEER_O, sib)
    cp_own = remote(o_ref.at[:, own_rows, sib_cols], in_o_own, C_OWN_O, sib)
    cp_stat.start()
    cp_peer.start()
    cp_own.start()

    def my_lanes(stat):
        return jnp.where(c == 0, stat, pltpu.roll(stat, LANES - group, 1))

    def weights_of(e1, e2):
        top = jnp.maximum(e1, e2)
        w1 = jnp.exp2(e1 - top)
        w2 = jnp.exp2(e2 - top)
        tot = w1 + w2
        inv = 1.0 / tot
        return w1 * inv, w2 * inv, top + jnp.log2(tot)

    def merge_core(rows, incoming, out, keep_e):
        for s in range(steps):
            w1, w2, e = weights_of(my_lanes(lse_ref[s, rows, :]), my_lanes(in_lse[s, rows, :]))
            keep_e[s] = e
            for i in range(group):
                col = pl.ds(pl.multiple_of(c * head_cols + i * LANES, LANES), LANES)
                out[s, :, i * LANES:(i + 1) * LANES] = (w1[:, i:i + 1] * o_ref[s, rows, col]
                                                        + w2[:, i:i + 1] * incoming[s, :, i * LANES:(i + 1) * LANES])

    mine_e = hid.at[pl.ds(0, steps * half), pl.ds(0, LANES)]
    cp_stat.wait_recv()
    cp_peer.wait_recv()
    merge_core(peer_rows, in_o_peer, to_x, to_x_e)
    cp_xe = remote(to_x_e, in_x_e, C_X_E, xpeer)
    cp_xo = remote(to_x, in_x, C_X_O, xpeer)
    cp_xe.start()
    cp_xo.start()
    cp_own.wait_recv()
    for s in range(steps):
        w1, w2, e = weights_of(my_lanes(lse_ref[s, own_rows, :]), my_lanes(in_lse[s, own_rows, :]))
        mine_e[s * half:(s + 1) * half, :] = e
        for i in range(group):
            col = pl.ds(pl.multiple_of(c * head_cols + i * LANES, LANES), LANES)
            mine[s, :, i * LANES:(i + 1) * LANES] = (w1[:, i:i + 1] * o_ref[s, own_rows, col]
                                                     + w2[:, i:i + 1] * in_o_own[s, :, i * LANES:(i + 1) * LANES])
    x_copy.wait()
    cp_xe.wait_recv()
    cp_xo.wait_recv()
    w1, w2, _ = weights_of(mine_e[...], in_x_e[...].reshape(steps * half, LANES))
    for i in range(group):
        cols = slice(i * LANES, (i + 1) * LANES)
        a_buf[:, cols] = (w1[:, i:i + 1] * mine[:, :, cols].reshape(steps * half, LANES)
                          + w2[:, i:i + 1] * in_x[:, :, cols].reshape(steps * half, LANES)).astype(BF16)

    wo_copy.wait()

    @pl.loop(0, chunks)
    def _(j):
        cols = pl.ds(pl.multiple_of(j * CHUNK, CHUNK), CHUNK)
        part[:, cols] = jnp.dot(a_buf[...], wo_buf[:, cols], preferred_element_type=F32)

    def step_rows(s, n=1):
        return pl.ds(pl.multiple_of(s * half, 8), n * half)

    cp_rs = remote(part.at[step_rows(2 * (1 - c), 2), :], in_part, C_RS_CORE, sib)
    cp_rs.start()
    cp_rs.wait_recv()
    half_sum[...] = part[step_rows(2 * c, 2), :] + in_part[...]
    cp_ry = remote(half_sum.at[step_rows(1 - y), :], in_y, C_RS_Y, ypeer)
    cp_ry.start()
    cp_ry.wait_recv()
    x_new = (x_buf[...] + (half_sum[step_rows(y), :] + in_y[...]) + bo_ref[...]).astype(BF16).astype(F32)
    x_mid[...] = x_new
    mean = jnp.mean(x_new, axis=-1, keepdims=True)
    cent = x_new - mean
    var = jnp.mean(cent * cent, axis=-1, keepdims=True)
    normed = cent * lax.rsqrt(var + LN_EPS) * gain_ref[...] + shift_ref[...]
    hid[step_rows(my_step), :] = normed.astype(BF16).astype(F32)

    own_h = hid.at[step_rows(my_step), :]
    peer_h = hid.at[step_rows(2 * c + 1 - y), :]
    cp_ay = remote(own_h, own_h, C_AG_Y, ypeer)
    cp_ac = remote(own_h, own_h, C_AG_OWN, sib)
    cp_ay.start()
    cp_ac.start()
    cp_ay.wait_recv()
    cp_af = remote(peer_h, peer_h, C_AG_FWD, sib)
    cp_af.start()
    cp_ac.wait_recv()
    cp_af.wait_recv()
    hid_b[...] = hid[...].astype(BF16)

    @pl.loop(0, chunks)
    def _(j):
        slot = lax.rem(j, RING)
        wait_item(slot)
        pre = jnp.dot(hid_b[...], ring[slot], preferred_element_type=F32) + bfc_ref[pl.ds(c * chunks + j, 1), :]
        cube = pre * pre * pre
        act = 0.5 * pre * (1.0 + jnp.tanh(math.sqrt(2.0 / math.pi) * (pre + 0.044715 * cube)))
        g_buf[:, pl.ds(pl.multiple_of(j * CHUNK, CHUNK), CHUNK)] = act.astype(BF16)
        load_item(j + RING, slot)

    def jcopy(src, dst, kind, j, who):
        return pltpu.make_async_remote_copy(src_ref=src, dst_ref=dst, send_sem=send_j.at[kind, j], recv_sem=recv_j.at[kind, j],
                                            device_id=who, device_id_type=MESH)

    def rs_core(j):
        return jcopy(p_chunk.at[j, step_rows(2 * (1 - c), 2), :], in_rc.at[j], J_RS_CORE, j, sib)

    def rs_y(j):
        return jcopy(p_half.at[j, step_rows(1 - y), :], in_ry.at[j], J_RS_Y, j, ypeer)

    def block(j, s, xx):
        return y_all.at[j, s, pl.ds(pl.multiple_of(xx * half, 8), half), :]

    def spread(kind, j):
        own = block(j, my_step, x)
        ypart = block(j, 2 * c + 1 - y, x)
        xpart = block(j, my_step, 1 - x)
        diag = block(j, 2 * c + 1 - y, 1 - x)
        ref, who = {J_OWN_Y: (own, ypeer), J_OWN_X: (own, xpeer), J_OWN_C: (own, sib),
                    J_FWD_X: (ypart, xpeer), J_FWD_C: (ypart, sib),
                    J_XOWN_C: (xpart, sib), J_XFWD_C: (diag, sib)}[kind]
        return jcopy(ref, ref, kind, j, who)

    def stage(it, lag, body):
        j = it - lag

        @pl.when((j >= 0) & (j < chunks))
        def _():
            body(j)

    def do_product(j):
        item = chunks + j
        slot = lax.rem(item, RING)
        wait_item(slot)
        p_chunk[j] = jnp.dot(g_buf[...], ring[slot], preferred_element_type=F32)

        @pl.when(item + RING < 2 * chunks)
        def _():
            load_item(item + RING, slot)

        rs_core(j).start()

    def do_core_sum(j):
        rs_core(j).wait_recv()
        p_half[j] = p_chunk[j, step_rows(2 * c, 2), :] + in_rc[j]
        rs_y(j).start()

    def do_y_sum(j):
        rs_y(j).wait_recv()
        cols = pl.ds(pl.multiple_of(j * CHUNK, CHUNK), CHUNK)
        full = x_mid[:, cols] + (p_half[j, step_rows(y), :] + in_ry[j]) + bproj_ref[:, cols]
        y_all[j, my_step, pl.ds(pl.multiple_of(x * half, 8), half), :] = full.astype(BF16).astype(F32)
        for kind in (J_OWN_Y, J_OWN_X, J_OWN_C):
            spread(kind, j).start()

    def do_forward(j):
        spread(J_OWN_Y, j).wait_recv()
        spread(J_FWD_X, j).start()
        spread(J_FWD_C, j).start()
        spread(J_OWN_X, j).wait_recv()
        spread(J_XOWN_C, j).start()

    def do_diag(j):
        spread(J_FWD_X, j).wait_recv()
        spread(J_XFWD_C, j).start()

    def do_store(j):
        for kind in (J_OWN_C, J_FWD_C, J_XOWN_C, J_XFWD_C):
            spread(kind, j).wait_recv()
        y_ref[:, :, pl.ds(pl.multiple_of(j * CHUNK, CHUNK), CHUNK)] = y_all[j].astype(BF16)

    @pl.loop(0, chunks + 7)
    def _(it):
        stage(it, 0, do_product)
        stage(it, 1, do_core_sum)
        stage(it, 3, do_y_sum)
        stage(it, 5, do_forward)
        stage(it, 6, do_diag)
        stage(it, 7, do_store)

    for cp in (cp_stat, cp_peer, cp_own, cp_xe, cp_xo, cp_rs, cp_ry, cp_ay, cp_ac, cp_af):
        cp.wait_send()

    @pl.loop(0, chunks)
    def _(j):
        rs_core(j).wait_send()
        rs_y(j).wait_send()
        for kind in (J_OWN_Y, J_OWN_X, J_OWN_C, J_FWD_X, J_FWD_C, J_XOWN_C, J_XFWD_C):
            spread(kind, j).wait_send()


def tail(o_part, lse, x_steps, w_o, w_fc, w_proj, b_o, gain, shift, b_fc, b_proj, group, kvs):
    steps, batch, cols = o_part.shape
    half = batch // 2
    rows = steps * half
    d_model = w_o.shape[1]
    chunks = d_model // CHUNK
    ff_own = w_fc.shape[1] // 2
    assert ff_own == d_model and steps == 4 and kvs == 2
    head_cols = group * LANES
    vm = pl.BlockSpec(memory_space=pltpu.VMEM)
    hbm = pl.BlockSpec(memory_space=pl.ANY)
    cfg = (steps, batch, group, chunks, kvs)
    scratch = [
        pltpu.VMEM((steps, half, head_cols), F32),
        pltpu.VMEM((steps, half, head_cols), F32),
        pltpu.VMEM((steps, batch, LANES), F32),
        pltpu.VMEM((steps, half, head_cols), F32),
        pltpu.VMEM((steps, half, LANES), F32),
        pltpu.VMEM((steps, half, head_cols), F32),
        pltpu.VMEM((steps, half, head_cols), F32),
        pltpu.VMEM((steps, half, LANES), F32),
        pltpu.VMEM((rows, head_cols), BF16),
        pltpu.VMEM((head_cols, d_model), BF16),
        pltpu.VMEM((rows, d_model), F32),
        pltpu.VMEM((2 * half, d_model), F32),
        pltpu.VMEM((2 * half, d_model), F32),
        pltpu.VMEM((half, d_model), F32),
        pltpu.VMEM((half, d_model), F32),
        pltpu.VMEM((half, d_model), F32),
        pltpu.VMEM((rows, d_model), F32),
        pltpu.VMEM((rows, d_model), BF16),
        pltpu.VMEM((RING, d_model, CHUNK), BF16),
        pltpu.VMEM((rows, ff_own), BF16),
        pltpu.VMEM((chunks, rows, CHUNK), F32),
        pltpu.VMEM((chunks, 2 * half, CHUNK), F32),
        pltpu.VMEM((chunks, 2 * half, CHUNK), F32),
        pltpu.VMEM((chunks, half, CHUNK), F32),
        pltpu.VMEM((chunks, steps, batch, CHUNK), F32),
        pltpu.SemaphoreType.DMA((10,)),
        pltpu.SemaphoreType.DMA((10,)),
        pltpu.SemaphoreType.DMA((9, chunks)),
        pltpu.SemaphoreType.DMA((9, chunks)),
        pltpu.SemaphoreType.DMA,
        pltpu.SemaphoreType.DMA,
        pltpu.SemaphoreType.DMA((RING,)),
    ]
    return pl.pallas_call(
        functools.partial(tail_kernel, cfg),
        out_shape=jax.ShapeDtypeStruct((steps, batch, d_model), BF16),
        in_specs=[vm, vm, hbm, hbm, hbm, hbm] + [vm] * 5,
        out_specs=vm,
        scratch_shapes=scratch,
        compiler_params=pltpu.CompilerParams(collective_id=0, has_side_effects=True, vmem_limit_bytes=VMEM_CAP),
        cost_estimate=pl.CostEstimate(flops=2 * rows * d_model * (head_cols + 2 * ff_own), bytes_accessed=100_000_000, transcendentals=0),
        name="tail",
    )(o_part, lse, x_steps, w_o, w_fc, w_proj, b_o, gain, shift, b_fc, b_proj)


def solution(mesh):
    sq_size = mesh.shape["sq"]
    act_spec = P(None, "dp", None)
    cache_spec = P("dp", "sq", "tp", None)
    col_spec = P(None, "tp")
    row_spec = P("tp", None)
    vec_spec = P("tp")
    rep_spec = P(None)
    in_specs = (act_spec, P("dp"), cache_spec, cache_spec, col_spec, vec_spec, col_spec, vec_spec,
                col_spec, vec_spec, row_spec, rep_spec, rep_spec, rep_spec, rep_spec, rep_spec,
                col_spec, vec_spec, row_spec, rep_spec)
    out_specs = (act_spec, cache_spec, cache_spec)

    def per_device(x_steps, positions, key_buf, val_buf, w_q, b_q, w_k, b_k, w_v, b_v, w_o, b_o,
                   ln1_gain, ln1_bias, ln2_gain, ln2_bias, w_fc, b_fc, w_proj, b_proj):
        steps, batch, d_model = x_steps.shape
        slots_local, kvs, dim = key_buf.shape[1], key_buf.shape[2], key_buf.shape[3]
        slots = slots_local * sq_size
        group = w_q.shape[1] // (kvs * dim)
        first_slot = lax.axis_index("sq") * slots_local
        meta = jnp.concatenate([first_slot[None].astype(jnp.int32), positions])
        x_wide = x_steps.astype(F32)
        hidden = layer_norm(x_wide, ln1_gain, ln1_bias).astype(BF16)
        query = linear(hidden, w_q, b_q).astype(BF16).astype(F32)
        key_new = linear(hidden, w_k, b_k).astype(BF16).astype(F32)
        val_new = linear(hidden, w_v, b_v).astype(BF16)
        cur_pos = positions[None, :] + jnp.arange(steps, dtype=jnp.int32)[:, None]
        cos_t, sin_t = rope_tables(cur_pos, dim)
        q_rot = apply_rope(query.reshape(steps, batch, kvs, group, dim), cos_t[:, :, None, None, :], sin_t[:, :, None, None, :]).astype(BF16)
        k_rot = apply_rope(key_new.reshape(steps, batch, kvs, dim), cos_t[:, :, None, :], sin_t[:, :, None, :]).astype(BF16)
        q_rows = q_rot.transpose(1, 3, 2, 0, 4).reshape(batch, group * kvs * steps, dim)
        pad = lambda rows: jnp.pad(rows.transpose(1, 0, 2, 3).reshape(batch, steps * kvs, dim), ((0, 0), (0, 16 - steps * kvs), (0, 0)))
        k_out, v_out, o_part, lse = attend(meta, q_rows, pad(k_rot), pad(val_new.reshape(steps, batch, kvs, dim)),
                                           key_buf.reshape(batch, slots_local * kvs, dim), val_buf.reshape(batch, slots_local * kvs, dim),
                                           steps, kvs, group, slots)
        row = lambda vec: vec.astype(F32).reshape(1, -1)
        ys = tail(o_part, lse, x_wide, w_o, w_fc, w_proj, row(b_o), row(ln2_gain), row(ln2_bias),
                  b_fc.astype(F32).reshape(-1, CHUNK), row(b_proj), group, kvs)
        return ys, k_out.reshape(key_buf.shape), v_out.reshape(val_buf.shape)

    return jax.shard_map(per_device, mesh=mesh, in_specs=in_specs, out_specs=out_specs, check_vma=False)
```

time: 849 us -> 182 us (0.21)
  matrix products: 466 us -> 15.7 us
  waiting for transfers between devices: 181 us -> 0 us
  Pallas kernels: 0 us -> 140 us
  local copies, waits for them, and re-layouts: 120 us -> 11.9 us
  other arithmetic: 56.2 us -> 12.4 us
  between operations: 15.8 us -> 0.86 us
    dot_general x32 -> x3, matrix products: 466 us -> 15.7 us  [linear(): jnp.einsum('sbd,dn->sbn', rows_in, weight, preferred_element_type=F32)]
    psum x2 -> x0, waiting for transfers between devices: 181 us -> none  [the longest x1 92.7 us: layer_tail(): lax.psum(jnp.dot(attn_out, w_o, preferred_element_type=jnp.float32), 'tp')]
    pallas_call x0 -> x2, Pallas kernels: none -> 140 us  [the longest x1 91.7 us: tail(): pl.pallas_call(functools.partial(tail_kernel, cfg), out_shape=jax.ShapeDt...]
    scatter x8 -> x0, local copies, waits for them, and re-layouts: 54.9 us -> none  [the longest x4 27.8 us: per_device(): val_buf = val_buf.at[batch_ids, local_slot].set(v_heads, mode='drop')]
    unnamed x120 -> x21, local copies, waits for them, and re-layouts: 34.6 us -> 2.84 us
    reduce_sum x10 -> x0, other arithmetic: 17.1 us -> none  [the longest x2 14.8 us: partial_attention(): part_sum = jnp.sum(weights, axis=-1)]
    all_gather x4 -> x0, local copies, waits for them, and re-layouts: 9.62 us -> none  [per_device(): gathered = lax.all_gather(stats, 'sq')]
    broadcast_in_dim x8 -> x0, local copies, waits for them, and re-layouts: 9.06 us -> none  [the longest x4 6.27 us: partial_attention(): weights = jnp.where(slot_mask, jnp.exp(scores - part_max[..., None]), 0.0)]
  transfers between devices with their start and end apart: 6 -> 0, of which waited for: 2 -> 0; matrix products, arithmetic and copies ran while one was open for 26% -> 0% of each run, Pallas kernels for 0% -> 0%
where the time goes in v1:
time: 182 us; the launch traced here: 181 us
  Pallas kernels  140 us (77%)
  matrix products  15.7 us (9%)
  other arithmetic  12.4 us (7%)
  local copies, waits for them, and re-layouts  11.9 us (7%)
    pallas_call x1, Pallas kernels, tail(): pl.pallas_call(functools.partial(tail_kernel, cfg), out_shape=jax.ShapeDt...  91.7 us
    pallas_call x1, Pallas kernels, attend(): pl.pallas_call(functools.partial(attend_kernel, cfg), grid_spec=pltpu.Pre...  48 us
    dot_general x3, matrix products, linear(): jnp.einsum('sbd,dn->sbn', rows_in, weight, preferred_element_type=F32)  15.7 us

profile of v1, /device:TPU:0, one launch (start us, length us, event | category | flops | bytes accessed | tf_op | source)
XLA Modules:
  0.0 180.6 jit_solution(11091293430215699957)
XLA Ops:
  0.7 1.4 pad_add_fusion.meta
  2.1 0.7 convert_element_type.56
  2.8 0.7 convert_element_type.58
  3.4 0.7 add_convert_fusion.6
  4.1 1.8 convert_reduce_fusion
  5.9 2.1 %multiply_reduce_fusion = f32[4,48]{1,0:T(4,128)S(1)} fusion(bf16[4,48,4608]{2,1,0:T(8,128)(2,1)} %param.20, f32[4,48]{1,0:T(4,128)S(1)} %broadcast_multiply_fusion), kind=kLoop, calls=%fused_computation.6 | loop fusion | flops 3538752 | bytes 1771008 | tf_op jit(solution)/shard_map/reduce_sum | solution.py:25
  8.0 0.6 reshape.141.bo_ref
  8.6 0.6 reshape.143.gain_ref
  9.2 0.6 reshape.145.shift_ref
  9.9 0.6 reshape.149.bproj_ref
  10.5 0.6 reshape.147.bfc_ref
  11.2 2.5 %fusion.21 = bf16[4,48,256]{2,1,0:T(8,128)(2,1)S(1)} fusion(bf16[4608,256]{1,0:T(8,128)(2,1)} %param.28, f32[256]{0:T(256)S(1)} %convert_element_type.58, bf16[4,48,4608]{2,1,0:T(8,128)(2,1)S(1)} %copy-done, f32[4608]{0:T(1024)S(1)} %convert_element_type.51, f32[4608]{0:T(1024)S(1)} %convert_element_type.50, f32[4,48]{1,0:T(4,128)S(1)} %add_rsqrt_fusion, ...), kind=kOutput, calls=%fused_computation.17 | convolution fusion | flops 458391552 | bytes 4266496 | tf_op jit(solution)/shard_map/sbd,dn->sbn/dot_general | solution.py:44
  13.8 0.7 pad.8.vn_ref
  15.0 2.5 %fusion.27 = f32[4,48,256]{2,1,0:T(8,128)S(1)} fusion(bf16[4608,256]{1,0:T(8,128)(2,1)} %param.26, f32[256]{0:T(256)S(1)} %convert_element_type.56, bf16[4,48,4608]{2,1,0:T(8,128)(2,1)S(1)} %copy-done, f32[4608]{0:T(1024)S(1)} %convert_element_type.51, f32[4608]{0:T(1024)S(1)} %convert_element_type.50, f32[4,48]{1,0:T(4,128)S(1)} %add_rsqrt_fusion, ...), kind=kOutput, calls=%fused_computation.19 | convolution fusion | flops 458440704 | bytes 4364800 | tf_op jit(solution)/shard_map/sbd,dn->sbn/dot_general | solution.py:44
  18.4 0.7 pad.7.kn_ref
  19.1 10.7 %fusion.8 = f32[4,48,2304]{2,1,0:T(8,128)} fusion(bf16[4608,2304]{1,0:T(8,128)(2,1)} %param.24, f32[2304]{0:T(1024)S(1)} %convert_element_type.53, bf16[4,48,4608]{2,1,0:T(8,128)(2,1)S(1)} %copy-done, f32[4608]{0:T(1024)S(1)} %convert_element_type.51, f32[4608]{0:T(1024)S(1)} %convert_element_type.50, f32[4,48]{1,0:T(4,128)S(1)} %add_rsqrt_fusion, ...), kind=kOutput, calls=%fused_computation.4 | convolution fusion | flops 4083499008 | bytes 24820224 | tf_op jit(solution)/shard_map/sbd,dn->sbn/dot_general | solution.py:44
  29.8 2.3 %reshape.137 = f32[4,48,2,9,128]{4,3,2,1,0:T(8,128)S(1)} reshape(f32[4,48,2304]{2,1,0:T(8,128)} %fusion.8) | data formatting | bytes 3538944 | tf_op jit(solution)/shard_map/reshape | solution.py:502
  32.1 1.1 subtract_convert_fusion
  33.3 1.0 maximum_bitcast_fusion
  34.2 1.7 copy.28
  35.9 2.1 %convert_element_type.49.x_ref = f32[4,48,4608]{2,1,0:T(8,128)} convert(bf16[4,48,4608]{2,1,0:T(8,128)(2,1)S(1)} %copy-done.1) | non-fusion elementwise | flops 884736 | bytes 5308416 | tf_op jit(solution)/shard_map/convert_element_type | solution.py:495
  38.0 48.0 %attend.1 = (bf16[48,2048,128]{2,1,0:T(8,128)(2,1)}, bf16[48,2048,128]{2,1,0:T(8,128)(2,1)}, f32[4,48,2304]{2,1,0:T(8,128)}, f32[4,48,128]{2,1,0:T(8,128)}) custom-call(s32[49]{0:T(128)} %pad_add_fusion.meta, bf16[48,72,128]{2,1,0:T(8,128)(2,1)} %bitcast.41, bf16[48,16,128]{2,1,0:T(8,128)(2,1)} %pad.7.kn_ref, bf16[48,16,128]{2,1,0:T(8,128)(2,1)} %pad.8.vn_ref, ...), custom_call_target="tpu_custom_call" | custom-call | flops 3623878656 | bytes 100663296 | tf_op jit(solution)/shard_map/attend/pallas_call | solution.py:128
  86.0 91.7 %tail.1 = bf16[4,48,4608]{2,1,0:T(8,128)(2,1)} custom-call(f32[4,48,2304]{2,1,0:T(8,128)} %get-tuple-element.7.o_ref, f32[4,48,128]{2,1,0:T(8,128)} %get-tuple-element.8.lse_ref, f32[4,48,4608]{2,1,0:T(8,128)} %convert_element_type.49.x_ref, bf16[2304,4608]{1,0:T(8,128)(2,1)} %wo_hbm.1, bf16[4608,9216]{1,0:T(8,128)(2,1)} %wfc_hbm.1, ...), custom_call_target="tpu_custom_call" | custom-call | flops 9172942848 | bytes 100000000 | tf_op jit(solution)/shard_map/tail/pallas_call | solution.py:462
  177.8 2.8 %copy.41 = bf16[4,48,4608]{2,1,0:T(8,128)(2,1)} copy(bf16[4,48,4608]{2,1,0:T(8,128)(2,1)} %tail.1) | data formatting | bytes 3538944
  (35 shorter events, 1.5 us)
Async XLA Ops:
  0.6 10.5 %copy-start = (bf16[4,48,4608]{2,1,0:T(8,128)(2,1)S(1)}, bf16[4,48,4608]{2,1,0:T(8,128)(2,1)}, u32[]{:S(2)}) copy-start(bf16[4,48,4608]{2,1,0:T(8,128)(2,1)} %param.20) | copy-start | bytes 5308420
  0.6 9.2 %copy-start.6 = (bf16[4608]{0:T(1024)(128)(2,1)S(1)}, bf16[4608]{0:T(1024)(128)(2,1)}, u32[]{:S(2)}) copy-start(bf16[4608]{0:T(1024)(128)(2,1)} %param.39) | copy-start | bytes 27652
  0.7 9.9 %copy-start.2 = (bf16[9216]{0:T(1024)(128)(2,1)S(1)}, bf16[9216]{0:T(1024)(128)(2,1)}, u32[]{:S(2)}) copy-start(bf16[9216]{0:T(1024)(128)(2,1)} %param.37) | copy-start | bytes 55300
  0.7 8.6 %copy-start.5 = (bf16[4608]{0:T(1024)(128)(2,1)S(1)}, bf16[4608]{0:T(1024)(128)(2,1)}, u32[]{:S(2)}) copy-start(bf16[4608]{0:T(1024)(128)(2,1)} %param.35) | copy-start | bytes 27652
  0.7 8.0 %copy-start.4 = (bf16[4608]{0:T(1024)(128)(2,1)S(1)}, bf16[4608]{0:T(1024)(128)(2,1)}, u32[]{:S(2)}) copy-start(bf16[4608]{0:T(1024)(128)(2,1)} %param.34) | copy-start | bytes 27652
  0.7 9.8 %copy-start.8 = (bf16[4608]{0:T(1024)(128)(2,1)S(1)}, bf16[4608]{0:T(1024)(128)(2,1)}, u32[]{:S(2)}) copy-start(bf16[4608]{0:T(1024)(128)(2,1)} %param.33) | copy-start | bytes 27652
  0.7 9.8 %copy-start.7 = (bf16[4608]{0:T(1024)(128)(2,1)S(1)}, bf16[4608]{0:T(1024)(128)(2,1)}, u32[]{:S(2)}) copy-start(bf16[4608]{0:T(1024)(128)(2,1)} %param.32) | copy-start | bytes 27652
  0.7 7.3 %copy-start.3 = (bf16[4608]{0:T(1024)(128)(2,1)S(1)}, bf16[4608]{0:T(1024)(128)(2,1)}, u32[]{:S(2)}) copy-start(bf16[4608]{0:T(1024)(128)(2,1)} %param.31) | copy-start | bytes 27652
  0.7 7.3 %copy-start.9 = (bf16[2304]{0:T(1024)(128)(2,1)S(1)}, bf16[2304]{0:T(1024)(128)(2,1)}, u32[]{:S(2)}) copy-start(bf16[2304]{0:T(1024)(128)(2,1)} %param.25) | copy-start | bytes 13828
  33.2 2.6 %copy-start.1 = (bf16[4,48,4608]{2,1,0:T(8,128)(2,1)S(1)}, bf16[4,48,4608]{2,1,0:T(8,128)(2,1)}, u32[]{:S(2)}) copy-start(bf16[4,48,4608]{2,1,0:T(8,128)(2,1)} %param.20) | copy-start | bytes 5308420

commit v2 on v1

--- a/solution.py
+++ b/solution.py
@@ -19,13 +19,6 @@
 LANES = 128
 
 
-def layer_norm(vectors, gain, shift):
-    row_mean = jnp.mean(vectors, axis=-1, keepdims=True)
-    centered = vectors - row_mean
-    row_var = jnp.mean(centered * centered, axis=-1, keepdims=True)
-    return centered * lax.rsqrt(row_var + LN_EPS) * gain.astype(F32) + shift.astype(F32)
-
-
 def rope_tables(positions, head_dim):
     half_dim = head_dim // 2
     inv_freq = jnp.power(F32(ROPE_BASE), -2.0 * jnp.arange(half_dim, dtype=F32) / head_dim)
@@ -33,132 +26,280 @@
     return jnp.cos(angle), jnp.sin(angle)
 
 
-def apply_rope(vectors, cos_t, sin_t):
-    half_dim = vectors.shape[-1] // 2
-    first = vectors[..., :half_dim]
-    second = vectors[..., half_dim:]
-    return jnp.concatenate([first * cos_t - second * sin_t, second * cos_t + first * sin_t], axis=-1)
-
-
-def linear(rows_in, weight, bias):
-    return jnp.einsum("sbd,dn->sbn", rows_in, weight, preferred_element_type=F32) + bias.astype(F32)
-
-
-def attend_kernel(cfg, meta, q_ref, kn_ref, vn_ref, k_ref, v_ref, ko_ref, vo_ref, o_ref, lse_ref, o_rows, stat_rows):
-    steps, kvs, group, per, slots = cfg
-    rows = k_ref.shape[1]
+COLS = 256
+
+def front_kernel(cfg, x_ref, gain_ref, shift_ref, cos_ref, sin_ref, bq_ref, bk_ref, bv_ref, wq_hbm, wk_hbm, wv_hbm,
+                 q_out, kn_out, vn_out, hid, wq_buf, wk_buf, wv_buf, q_rows, kv_rows, bias_q, sem):
+    steps, kvs, group = cfg
+    batch, d_model = x_ref.shape[1], x_ref.shape[2]
+    n_q = wq_hbm.shape[1] // COLS
+    per_row = group * kvs * steps
+    copies = [pltpu.make_async_copy(wk_hbm, wk_buf, sem.at[n_q]), pltpu.make_async_copy(wv_hbm, wv_buf, sem.at[n_q + 1])]
+    for copy in copies:
+        copy.start()
+    for n in range(n_q):
+        pltpu.make_async_copy(wq_hbm.at[:, n * COLS:(n + 1) * COLS], wq_buf.at[n], sem.at[n]).start()
+
+    bias_q[...] = bq_ref[...].astype(F32)
+    gain = gain_ref[...].astype(F32)
+    shift = shift_ref[...].astype(F32)
+    for s in range(steps):
+        wide = x_ref[s].astype(F32)
+        mean = jnp.mean(wide, axis=-1, keepdims=True)
+        cent = wide - mean
+        rstd = lax.rsqrt(jnp.mean(cent * cent, axis=-1, keepdims=True) + LN_EPS)
+        for n in range(d_model // LANES):
+            cols = slice(n * LANES, (n + 1) * LANES)
+            hid[s * batch:(s + 1) * batch, cols] = (cent[:, cols] * rstd * gain[n:n + 1, :] + shift[n:n + 1, :]).astype(BF16)
+
+    cos = cos_ref[...].reshape(steps * batch, LANES // 2)
+    sin = sin_ref[...].reshape(steps * batch, LANES // 2)
+    cos_full = jnp.concatenate([cos, cos], axis=-1)
+    sin_full = jnp.concatenate([-sin, sin], axis=-1)
+
+    def rotate(vec):
+        return (vec * cos_full + pltpu.roll(vec, LANES // 2, 1) * sin_full).astype(BF16).astype(F32)
+
+    def rounded(weight, bias):
+        return (jnp.dot(hid[...], weight, preferred_element_type=F32) + bias).astype(BF16).astype(F32)
+
+    for rope, copy, buf, b_ref, out in ((True, copies[0], wk_buf, bk_ref, kn_out), (False, copies[1], wv_buf, bv_ref, vn_out)):
+        copy.wait()
+        kv_rows[...] = jnp.zeros_like(kv_rows)
+        bias = b_ref[...].astype(F32)
+        both = rounded(buf[...], jnp.concatenate([bias[h:h + 1] for h in range(kvs)], axis=-1))
+        for h in range(kvs):
+            vec = both[:, h * LANES:(h + 1) * LANES]
+            if rope:
+                vec = rotate(vec)
+            for s in range(steps):
+                kv_rows[pl.ds(s * kvs + h, batch, stride=16), :] = vec[s * batch:(s + 1) * batch]
+        out[...] = kv_rows[...].reshape(out.shape).astype(BF16)
+
+    heads = COLS // LANES
+
+    @pl.loop(0, n_q)
+    def _(n):
+        pltpu.make_async_copy(wq_hbm.at[:, 0:COLS], wq_buf.at[n], sem.at[n]).wait()
+        bias = jnp.concatenate([bias_q[pl.ds(n * heads + e, 1), :] for e in range(heads)], axis=-1)
+        both = rounded(wq_buf[n], bias)
+        for e in range(heads):
+            vec = rotate(both[:, e * LANES:(e + 1) * LANES])
+            head = n * heads + e
+            row = lax.rem(head, group) * (kvs * steps) + (head // group) * steps
+            for s in range(steps):
+                q_rows[pl.ds(row + s, batch, stride=per_row), :] = vec[s * batch:(s + 1) * batch]
+
+    @pl.loop(0, batch)
+    def _(b):
+        q_out[b] = q_rows[pl.ds(pl.multiple_of(b * per_row, 8), per_row), :].astype(BF16)
+
+
+def front(x_steps, gain, shift, cos_t, sin_t, b_q, b_k, b_v, w_q, w_k, w_v, kvs):
+    steps, batch, d_model = x_steps.shape
+    heads = w_q.shape[1] // LANES
+    group = heads // kvs
+    rows = group * kvs * steps
+    n_q = w_q.shape[1] // COLS
+    vm = pl.BlockSpec(memory_space=pltpu.VMEM)
+    hbm = pl.BlockSpec(memory_space=pl.ANY)
+    tiles = lambda vec: vec.reshape(-1, LANES)
+    return pl.pallas_call(
+        functools.partial(front_kernel, (steps, kvs, group)),
+        out_shape=[
+            jax.ShapeDtypeStruct((batch, rows, LANES), BF16),
+            jax.ShapeDtypeStruct((batch, 16, LANES), BF16),
+            jax.ShapeDtypeStruct((batch, 16, LANES), BF16),
+        ],
+        in_specs=[vm] * 8 + [hbm] * 3,
+        out_specs=[vm] * 3,
+        scratch_shapes=[
+            pltpu.VMEM((steps * batch, d_model), BF16),
+            pltpu.VMEM((n_q, d_model, COLS), BF16),
+            pltpu.VMEM(w_k.shape, BF16),
+            pltpu.VMEM(w_v.shape, BF16),
+            pltpu.VMEM((batch * rows, LANES), F32),
+            pltpu.VMEM((batch * 16, LANES), F32),
+            pltpu.VMEM((heads, LANES), F32),
+            pltpu.SemaphoreType.DMA((n_q + 2,)),
+        ],
+        compiler_params=pltpu.CompilerParams(vmem_limit_bytes=56 * 2**20),
+        cost_estimate=pl.CostEstimate(flops=2 * steps * batch * d_model * (w_q.shape[1] + 2 * w_k.shape[1]),
+                                      bytes_accessed=2 * d_model * (w_q.shape[1] + 2 * w_k.shape[1]), transcendentals=0),
+        name="front",
+    )(x_steps, tiles(gain), tiles(shift), cos_t, sin_t, tiles(b_q), tiles(b_k), tiles(b_v), w_q, w_k, w_v)
+
+
+PER = 2
+DEPTH = 8
+AHEAD = 4
+
+def attend_kernel(cfg, pos_ref, q_ref, kn_ref, vn_ref, k_hbm, v_hbm, ko_hbm, vo_hbm, o_ref, lse_ref,
+                  k_buf, v_buf, o_rows, stat_rows, k_in, v_in, k_up, v_up):
+    steps, kvs, group, slots, n_blocks = cfg
+    rows = k_hbm.shape[1]
     tile = steps * kvs
-    inner = pl.program_id(1)
-    base = (pl.program_id(0) * pl.num_programs(1) + inner) * per
-    first = meta[0]
+    per_row = group * tile
+    first = lax.axis_index("sq") * (rows // kvs)
     coef = LANES ** -0.5 * LOG2E
     contract_last = (((1,), (1,)), ((), ()))
+    blocks_per_tile = 8 // PER
+
+    def seqs(i):
+        return pl.ds(i * PER, PER)
+
+    def fetch(i):
+        slot = lax.rem(i, DEPTH)
+        return (pltpu.make_async_copy(k_hbm.at[seqs(i)], k_buf.at[slot], k_in.at[slot]),
+                pltpu.make_async_copy(v_hbm.at[seqs(i)], v_buf.at[slot], v_in.at[slot]))
+
+    def put(i):
+        slot = lax.rem(i, DEPTH)
+        return (pltpu.make_async_copy(k_buf.at[slot], ko_hbm.at[seqs(i)], k_up.at[slot]),
+                pltpu.make_async_copy(v_buf.at[slot], vo_hbm.at[seqs(i)], v_up.at[slot]))
+
+    for i in range(AHEAD):
+        for copy in fetch(jnp.int32(i)):
+            copy.start()
 
     sub = lax.broadcasted_iota(jnp.int32, (tile, rows), 0)
     lane = lax.broadcasted_iota(jnp.int32, (tile, rows), 1)
-    own_head = (lane % kvs) == (sub // steps)
-    slot = first + lane // kvs
-    sub2 = lax.broadcasted_iota(jnp.int32, (tile, kn_ref.shape[1]), 0)
-    lane2 = lax.broadcasted_iota(jnp.int32, (tile, kn_ref.shape[1]), 1)
-    new_head = (lane2 % kvs) == (sub2 // steps)
+    sub2 = lax.broadcasted_iota(jnp.int32, (tile, 16), 0)
+    lane2 = lax.broadcasted_iota(jnp.int32, (tile, 16), 1)
     new_step = lane2 // kvs
+    new_ok = ((lane2 % kvs) == (sub2 // steps)) & (new_step <= sub2 % steps)
     stat_sub = lax.broadcasted_iota(jnp.int32, (tile, LANES), 0)
     stat_lane = lax.broadcasted_iota(jnp.int32, (tile, LANES), 1) - (stat_sub // steps) * group
-    win_row = lax.broadcasted_iota(jnp.int32, (16, LANES), 0)
-
-    for one in range(per):
-        pos = meta[1 + base + one]
-        q = q_ref[one]
-        for src, dst, new in ((k_ref, ko_ref, kn_ref), (v_ref, vo_ref, vn_ref)):
-            dst[one] = src[one]
-            fresh = new[one].astype(F32)
-            for t in range(steps):
-                row = kvs * ((pos + t) % slots - first)
-                start = pl.multiple_of(jnp.clip(row // 16, 0, rows // 16 - 1) * 16, 16)
-                window = dst[one, pl.ds(start, 16), :].astype(F32)
-                offset = win_row + (start - row)
+    win_row = lax.broadcasted_iota(jnp.int32, (32, LANES), 0)
+
+    def renew(i):
+        slot_of = lax.rem(i, DEPTH)
+        for one in range(PER):
+            seq = i * PER + one
+            goal = kvs * ((pos_ref[seq] & (slots - 1)) - first)
+            goal = jnp.where(goal > kvs * (slots - steps), goal - kvs * slots, goal)
+            start = pl.multiple_of(jnp.clip((goal >> 4) << 4, 0, rows - 32), 16)
+            offset = win_row + (start - goal)
+            for buf, new in ((k_buf, kn_ref), (v_buf, vn_ref)):
+                fresh = new[seq].astype(F32)
+                window = buf[slot_of, one, pl.ds(start, 32), :].astype(F32)
+                for r in range(tile):
+                    window = jnp.where(offset == r, fresh[r:r + 1, :], window)
+                buf[slot_of, one, pl.ds(start, 32), :] = window.astype(BF16)
+
+    @pl.loop(0, n_blocks)
+    def _(i):
+        slot_now = lax.rem(i, DEPTH)
+
+        @pl.when(i >= 1)
+        def _():
+            renew(i - 1)
+
+        @pl.when(i >= AHEAD)
+        def _():
+            for copy in put(i - AHEAD):
+                copy.wait()
+
+        @pl.when(i + AHEAD < n_blocks)
+        def _():
+            for copy in fetch(i + AHEAD):
+                copy.start()
+
+        @pl.when(i >= 1)
+        def _():
+            for copy in put(i - 1):
+                copy.start()
+
+        k_copy, v_copy = fetch(i)
+        k_copy.wait()
+        v_copy.wait()
+        state = []
+        for one in range(PER):
+            seq = i * PER + one
+            pos = pos_ref[seq]
+            q = q_ref[seq]
+            raw = lax.dot_general(q, k_buf[slot_now, one], contract_last, preferred_element_type=F32)
+            raw2 = lax.dot_general(q, kn_ref[seq], contract_last, preferred_element_type=F32)
+            state.append((seq, pos, raw, raw2))
+        soft = []
+        for seq, pos, raw, raw2 in state:
+            slot = first + (lane >> 1)
+            ahead = (slot - pos) & (slots - 1)
+            ok = ((lane & 1) == (sub >> 2)) & (slot < pos) & (ahead > (sub & 3))
+            bias = jnp.where(ok, 0.0, NEG_BIG).astype(F32)
+            new_slot = ((pos + new_step) & (slots - 1)) - first
+            here = (new_slot >= 0) & (new_slot < rows // kvs)
+            bias2 = jnp.where(new_ok & here, 0.0, NEG_BIG).astype(F32)
+            score = raw.reshape(group, tile, rows) * coef + bias[None]
+            score2 = raw2.reshape(group, tile, 16) * coef + bias2[None]
+            top = jnp.maximum(jnp.max(score, axis=-1, keepdims=True), jnp.max(score2, axis=-1, keepdims=True))
+            top = jnp.maximum(top, NEG_HALF)
+            w = jnp.exp2(score - top)
+            w2 = jnp.exp2(score2 - top)
+            total = jnp.sum(w, axis=-1, keepdims=True) + jnp.sum(w2, axis=-1, keepdims=True)
+            soft.append((top, total, w.reshape(per_row, rows).astype(BF16), w2.reshape(per_row, 16).astype(BF16)))
+        for one in range(PER):
+            seq, pos = state[one][:2]
+            top, total, w, w2 = soft[one]
+            out = jnp.dot(w, v_buf[slot_now, one], preferred_element_type=F32)
+            out = out + jnp.dot(w2, vn_ref[seq], preferred_element_type=F32)
+            some = total > 0.0
+            safe = jnp.where(some, total, 1.0)
+            lse = jnp.where(some, top + jnp.log2(safe), NEG_BIG)
+            out = out.reshape(group, tile, LANES) * (1.0 / safe)
+            stats = jnp.zeros((tile, LANES), F32)
+            for n in range(group):
+                stats = jnp.where(stat_lane == n, lse[n], stats)
+            seat = lax.rem(i, blocks_per_tile) * PER + one
+            o_rows[pl.ds(pl.multiple_of(seat * per_row, 8), per_row), :] = out.reshape(per_row, LANES)
+            stat_rows[pl.ds(pl.multiple_of(seat * tile, 8), tile), :] = stats
+        @pl.when(lax.rem(i, blocks_per_tile) == blocks_per_tile - 1)
+        def _():
+            where = pl.ds(pl.multiple_of((i // blocks_per_tile) * 8, 8), 8)
+            for s in range(steps):
+                lse_ref[s, where, :] = sum(stat_rows[pl.ds(h * steps + s, 8, stride=tile), :] for h in range(kvs))
                 for h in range(kvs):
-                    window = jnp.where(offset == h, fresh[t * kvs + h:t * kvs + h + 1, :], window)
-                dst[one, pl.ds(start, 16), :] = window.astype(BF16)
-        ahead = (slot - pos) & (slots - 1)
-        bias = jnp.where(own_head & (slot < pos) & (ahead > sub % steps), 0.0, NEG_BIG).astype(F32)
-        new_slot = ((pos + new_step) & (slots - 1)) - first
-        here = (new_slot >= 0) & (new_slot < rows // kvs)
-        bias2 = jnp.where(new_head & (new_step <= sub2 % steps) & here, 0.0, NEG_BIG).astype(F32)
-        raw = lax.dot_general(q, k_ref[one], contract_last, preferred_element_type=F32)
-        raw2 = lax.dot_general(q, kn_ref[one], contract_last, preferred_element_type=F32)
-        score = raw.reshape(group, tile, rows) * coef + bias[None]
-        score2 = raw2.reshape(group, tile, -1) * coef + bias2[None]
-        top = jnp.maximum(jnp.max(score, axis=-1, keepdims=True), jnp.max(score2, axis=-1, keepdims=True))
-        top = jnp.maximum(top, NEG_HALF)
-        w = jnp.exp2(score - top)
-        w2 = jnp.exp2(score2 - top)
-        total = jnp.sum(w, axis=-1, keepdims=True) + jnp.sum(w2, axis=-1, keepdims=True)
-        out = jnp.dot(w.reshape(group * tile, rows).astype(BF16), v_ref[one], preferred_element_type=F32)
-        out = out + jnp.dot(w2.reshape(group * tile, -1).astype(BF16), vn_ref[one], preferred_element_type=F32)
-        some = total > 0.0
-        safe = jnp.where(some, total, 1.0)
-        lse = jnp.where(some, top + jnp.log2(safe), NEG_BIG)
-        out = out.reshape(group, tile, LANES) * (1.0 / safe)
-        stats = jnp.zeros((tile, LANES), F32)
-        for i in range(group):
-            stats = jnp.where(stat_lane == i, lse[i], stats)
-        seat = inner * per + one
-        o_rows[pl.ds(pl.multiple_of(seat * (group * tile), 8), group * tile), :] = out.reshape(group * tile, LANES)
-        stat_rows[pl.ds(pl.multiple_of(seat * tile, 8), tile), :] = stats
-
-    @pl.when(inner == pl.num_programs(1) - 1)
-    def _():
-        for s in range(steps):
-            lse_ref[s] = sum(stat_rows[pl.ds(h * steps + s, 8, stride=tile), :] for h in range(kvs))
-            for h in range(kvs):
-                for i in range(group):
-                    col = (h * group + i) * LANES
-                    o_ref[s, :, col:col + LANES] = o_rows[pl.ds(i * tile + h * steps + s, 8, stride=group * tile), :]
-
-
-def attend(meta, q, k_new, v_new, k_rows, v_rows, steps, kvs, group, slots):
+                    for n in range(group):
+                        col = (h * group + n) * LANES
+                        o_ref[s, where, col:col + LANES] = o_rows[pl.ds(n * tile + h * steps + s, 8, stride=per_row), :]
+
+    renew(jnp.int32(n_blocks - 1))
+    for copy in put(n_blocks - 1):
+        copy.start()
+    for j in range(AHEAD):
+        for copy in put(n_blocks - AHEAD + j):
+            copy.wait()
+
+
+def attend(positions, q, k_new, v_new, k_rows, v_rows, steps, kvs, group, slots):
     batch, rows, dim = k_rows.shape
-    per, eight = 2, 8
-    inner = eight // per
-    cfg = (steps, kvs, group, per, slots)
-    seq = lambda g, j, meta: (g * inner + j, 0, 0)
-    wide = lambda g, j, meta: (0, g, 0)
-    cache_spec = pl.BlockSpec((per, rows, dim), seq)
+    vm = pl.BlockSpec(memory_space=pltpu.VMEM)
+    hbm = pl.BlockSpec(memory_space=pl.ANY)
     return pl.pallas_call(
-        functools.partial(attend_kernel, cfg),
-        grid_spec=pltpu.PrefetchScalarGridSpec(
-            num_scalar_prefetch=1,
-            grid=(batch // eight, inner),
-            in_specs=[
-                pl.BlockSpec((per, q.shape[1], dim), seq),
-                pl.BlockSpec((per, k_new.shape[1], dim), seq),
-                pl.BlockSpec((per, v_new.shape[1], dim), seq),
-                cache_spec,
-                cache_spec,
-            ],
-            out_specs=[
-                cache_spec,
-                cache_spec,
-                pl.BlockSpec((steps, eight, kvs * group * dim), wide),
-                pl.BlockSpec((steps, eight, LANES), wide),
-            ],
-            scratch_shapes=[
-                pltpu.VMEM((eight * q.shape[1], dim), F32),
-                pltpu.VMEM((eight * steps * kvs, dim), F32),
-            ],
-        ),
+        functools.partial(attend_kernel, (steps, kvs, group, slots, batch // PER)),
+        in_specs=[pl.BlockSpec(memory_space=pltpu.SMEM), vm, vm, vm, hbm, hbm],
+        out_specs=[hbm, hbm, vm, vm],
         out_shape=[
             jax.ShapeDtypeStruct(k_rows.shape, BF16),
             jax.ShapeDtypeStruct(v_rows.shape, BF16),
             jax.ShapeDtypeStruct((steps, batch, kvs * group * dim), F32),
             jax.ShapeDtypeStruct((steps, batch, LANES), F32),
         ],
-        compiler_params=pltpu.CompilerParams(dimension_semantics=("arbitrary", "arbitrary")),
+        scratch_shapes=[
+            pltpu.VMEM((DEPTH, PER, rows, dim), BF16),
+            pltpu.VMEM((DEPTH, PER, rows, dim), BF16),
+            pltpu.VMEM((8 * q.shape[1], dim), F32),
+            pltpu.VMEM((8 * steps * kvs, dim), F32),
+            pltpu.SemaphoreType.DMA((DEPTH,)),
+            pltpu.SemaphoreType.DMA((DEPTH,)),
+            pltpu.SemaphoreType.DMA((DEPTH,)),
+            pltpu.SemaphoreType.DMA((DEPTH,)),
+        ],
+        compiler_params=pltpu.CompilerParams(vmem_limit_bytes=56 * 2**20),
         cost_estimate=pl.CostEstimate(flops=4 * batch * rows * q.shape[1] * dim, bytes_accessed=8 * batch * rows * dim,
                                       transcendentals=batch * rows * q.shape[1]),
         name="attend",
-    )(meta, q, k_new, v_new, k_rows, v_rows)
+    )(positions, q, k_new, v_new, k_rows, v_rows)
 
 
 CHUNK = 512
@@ -490,24 +631,13 @@
         slots_local, kvs, dim = key_buf.shape[1], key_buf.shape[2], key_buf.shape[3]
         slots = slots_local * sq_size
         group = w_q.shape[1] // (kvs * dim)
-        first_slot = lax.axis_index("sq") * slots_local
-        meta = jnp.concatenate([first_slot[None].astype(jnp.int32), positions])
-        x_wide = x_steps.astype(F32)
-        hidden = layer_norm(x_wide, ln1_gain, ln1_bias).astype(BF16)
-        query = linear(hidden, w_q, b_q).astype(BF16).astype(F32)
-        key_new = linear(hidden, w_k, b_k).astype(BF16).astype(F32)
-        val_new = linear(hidden, w_v, b_v).astype(BF16)
         cur_pos = positions[None, :] + jnp.arange(steps, dtype=jnp.int32)[:, None]
         cos_t, sin_t = rope_tables(cur_pos, dim)
-        q_rot = apply_rope(query.reshape(steps, batch, kvs, group, dim), cos_t[:, :, None, None, :], sin_t[:, :, None, None, :]).astype(BF16)
-        k_rot = apply_rope(key_new.reshape(steps, batch, kvs, dim), cos_t[:, :, None, :], sin_t[:, :, None, :]).astype(BF16)
-        q_rows = q_rot.transpose(1, 3, 2, 0, 4).reshape(batch, group * kvs * steps, dim)
-        pad = lambda rows: jnp.pad(rows.transpose(1, 0, 2, 3).reshape(batch, steps * kvs, dim), ((0, 0), (0, 16 - steps * kvs), (0, 0)))
-        k_out, v_out, o_part, lse = attend(meta, q_rows, pad(k_rot), pad(val_new.reshape(steps, batch, kvs, dim)),
-                                           key_buf.reshape(batch, slots_local * kvs, dim), val_buf.reshape(batch, slots_local * kvs, dim),
-                                           steps, kvs, group, slots)
+        q_rows, k_new, v_new = front(x_steps, ln1_gain, ln1_bias, cos_t, sin_t, b_q, b_k, b_v, w_q, w_k, w_v, kvs)
+        k_out, v_out, o_part, lse = attend(positions, q_rows, k_new, v_new, key_buf.reshape(batch, slots_local * kvs, dim),
+                                           val_buf.reshape(batch, slots_local * kvs, dim), steps, kvs, group, slots)
         row = lambda vec: vec.astype(F32).reshape(1, -1)
-        ys = tail(o_part, lse, x_wide, w_o, w_fc, w_proj, row(b_o), row(ln2_gain), row(ln2_bias),
+        ys = tail(o_part, lse, x_steps.astype(F32), w_o, w_fc, w_proj, row(b_o), row(ln2_gain), row(ln2_bias),
                   b_fc.astype(F32).reshape(-1, CHUNK), row(b_proj), group, kvs)
         return ys, k_out.reshape(key_buf.shape), v_out.reshape(val_buf.shape)
 

time: 182 us -> 157 us (0.86)
  matrix products: 15.7 us -> 0 us
  other arithmetic: 12.4 us -> 4.05 us
  local copies, waits for them, and re-layouts: 11.9 us -> 9.44 us
  Pallas kernels: 140 us -> 142 us
    dot_general x3 -> x0, matrix products: 15.7 us -> none  [linear(): jnp.einsum('sbd,dn->sbn', rows_in, weight, preferred_element_type=F32)]
    reduce_sum x2 -> x0, other arithmetic: 3.89 us -> none  [the longest x1 2.09 us: layer_norm(): row_var = jnp.mean(centered * centered, axis=-1, keepdims=True)]
    reshape x4, local copies, waits for them, and re-layouts: 2.46 us -> 5.28 us  [per_device(): row = lambda vec: vec.astype(F32).reshape(1, -1)]
    reshape x4 -> x0, local copies, waits for them, and re-layouts: 2.49 us -> none  [the longest x1 2.29 us: per_device(): query.reshape(steps, batch, kvs, group, dim)]
    pallas_call x1 -> x2, Pallas kernels: 48 us -> 50.2 us  [the longest x1 36.7 us: attend(): pl.pallas_call(functools.partial(attend_kernel, (steps, kvs, group, slots...]
where the time goes in v2:
time: 157 us; the launch traced here: 156 us
  Pallas kernels  142 us (90%)
  local copies, waits for them, and re-layouts  9.44 us (6%)
  other arithmetic  4.05 us (3%)
    pallas_call x1, Pallas kernels, tail(): pl.pallas_call(functools.partial(tail_kernel, cfg), out_shape=jax.ShapeDt...  91.8 us
    pallas_call x1, Pallas kernels, attend(): pl.pallas_call(functools.partial(attend_kernel, (steps, kvs, group, slots...  36.7 us
    pallas_call x1, Pallas kernels, front(): pl.pallas_call(functools.partial(front_kernel, (steps, kvs, group)), out_...  13.5 us
    reshape x4, local copies, waits for them, and re-layouts, per_device(): row = lambda vec: vec.astype(F32).reshape(1, -1)  5.28 us

profile of v2, /device:TPU:0, one launch (start us, length us, event | category | flops | bytes accessed | tf_op | source)
XLA Modules:
  0.0 156.1 jit_solution(4690001675935007559)
XLA Ops:
  0.6 0.0 copy-start
  0.7 0.8 add_convert_fusion
  1.4 1.3 reshape.102.bo_ref
  2.8 1.3 reshape.104.gain_ref
  4.1 1.3 reshape.106.shift_ref
  5.4 1.3 reshape.110.bproj_ref
  6.7 1.4 reshape.108.bfc_ref
  8.1 1.1 multiply_sine_fusion
  9.2 13.5 %front.1 = (bf16[48,72,128]{2,1,0:T(8,128)(2,1)}, bf16[48,16,128]{2,1,0:T(8,128)(2,1)}, bf16[48,16,128]{2,1,0:T(8,128)(2,1)}) custom-call(bf16[4,48,4608]{2,1,0:T(8,128)(2,1)} %x_ref.1, bf16[36,128]{1,0:T(8,128)(2,1)} %bitcast.11, bf16[36,128]{1,0:T(8,128)(2,1)} %bitcast.12, f32[4,48,64]{2,1,0:T(8,128)} %get-tuple-element.18.cos_ref, ...), custom_call_target="tpu_custom_call" | custom-call | flops 4982833152 | bytes 25952256 | tf_op jit(solution)/shard_map/front/pallas_call | solution.py:107
  22.7 0.0 copy-done
  22.7 2.1 %convert_element_type.16.x_ref = f32[4,48,4608]{2,1,0:T(8,128)} convert(bf16[4,48,4608]{2,1,0:T(8,128)(2,1)S(1)} %copy-done) | non-fusion elementwise | flops 884736 | bytes 5308416 | tf_op jit(solution)/shard_map/convert_element_type | solution.py:640
  24.9 36.7 %attend.1 = (bf16[48,2048,128]{2,1,0:T(8,128)(2,1)}, bf16[48,2048,128]{2,1,0:T(8,128)(2,1)}, f32[4,48,2304]{2,1,0:T(8,128)}, f32[4,48,128]{2,1,0:T(8,128)}) custom-call(s32[48]{0:T(128)} %pos_ref.1, bf16[48,72,128]{2,1,0:T(8,128)(2,1)} %get-tuple-element.10.q_ref, bf16[48,16,128]{2,1,0:T(8,128)(2,1)} %get-tuple-element.11.kn_ref, ...), custom_call_target="tpu_custom_call" | custom-call | flops 3623878656 | bytes 100663296 | tf_op jit(solution)/shard_map/attend/pallas_call | solution.py:278
  61.5 91.8 %tail.1 = bf16[4,48,4608]{2,1,0:T(8,128)(2,1)} custom-call(f32[4,48,2304]{2,1,0:T(8,128)} %get-tuple-element.13.o_ref, f32[4,48,128]{2,1,0:T(8,128)} %get-tuple-element.14.lse_ref, f32[4,48,4608]{2,1,0:T(8,128)} %convert_element_type.16.x_ref, bf16[2304,4608]{1,0:T(8,128)(2,1)} %wo_hbm.1, bf16[4608,9216]{1,0:T(8,128)(2,1)} %wfc_hbm.1, ...), custom_call_target="tpu_custom_call" | custom-call | flops 9172942848 | bytes 100000000 | tf_op jit(solution)/shard_map/tail/pallas_call | solution.py:603
  153.3 2.8 %copy.24 = bf16[4,48,4608]{2,1,0:T(8,128)(2,1)} copy(bf16[4,48,4608]{2,1,0:T(8,128)(2,1)} %tail.1) | data formatting | bytes 3538944
  (1 shorter events, 0.0 us)
Async XLA Ops:
  0.6 22.1 %copy-start = (bf16[4,48,4608]{2,1,0:T(8,128)(2,1)S(1)}, bf16[4,48,4608]{2,1,0:T(8,128)(2,1)}, u32[]{:S(2)}) copy-start(bf16[4,48,4608]{2,1,0:T(8,128)(2,1)} %x_ref.1) | copy-start | bytes 5308420

commit v3 on v2

--- a/solution.py
+++ b/solution.py
@@ -134,9 +134,12 @@
 DEPTH = 8
 AHEAD = 4
 
-def attend_kernel(cfg, pos_ref, q_ref, kn_ref, vn_ref, k_hbm, v_hbm, ko_hbm, vo_hbm, o_ref, lse_ref,
-                  k_buf, v_buf, o_rows, stat_rows, k_in, v_in, k_up, v_up):
-    steps, kvs, group, slots, n_blocks = cfg
+def attend_kernel(cfg, pos_ref, q_ref, kn_ref, vn_ref, k_hbm, v_hbm, *refs):
+    steps, kvs, group, slots, n_blocks, own_half = cfg
+    ko_hbm, vo_hbm, o_ref, k_buf, v_buf, o_rows, stat_rows, k_in, v_in, k_up, v_up = refs[2 if own_half else 0:]
+    x = lax.axis_index("sq") // 2
+    base = (x if own_half else 1 - x) * (n_blocks * PER)
+    lse_cols = slice(kvs * group * LANES, (kvs * group + 1) * LANES)
     rows = k_hbm.shape[1]
     tile = steps * kvs
     per_row = group * tile
@@ -146,7 +149,7 @@
     blocks_per_tile = 8 // PER
 
     def seqs(i):
-        return pl.ds(i * PER, PER)
+        return pl.ds(base + i * PER, PER)
 
     def fetch(i):
         slot = lax.rem(i, DEPTH)
@@ -175,7 +178,7 @@
     def renew(i):
         slot_of = lax.rem(i, DEPTH)
         for one in range(PER):
-            seq = i * PER + one
+            seq = base + i * PER + one
             goal = kvs * ((pos_ref[seq] & (slots - 1)) - first)
             goal = jnp.where(goal > kvs * (slots - steps), goal - kvs * slots, goal)
             start = pl.multiple_of(jnp.clip((goal >> 4) << 4, 0, rows - 32), 16)
@@ -215,7 +218,7 @@
         v_copy.wait()
         state = []
         for one in range(PER):
-            seq = i * PER + one
+            seq = base + i * PER + one
             pos = pos_ref[seq]
             q = q_ref[seq]
             raw = lax.dot_general(q, k_buf[slot_now, one], contract_last, preferred_element_type=F32)
@@ -257,7 +260,7 @@
         def _():
             where = pl.ds(pl.multiple_of((i // blocks_per_tile) * 8, 8), 8)
             for s in range(steps):
-                lse_ref[s, where, :] = sum(stat_rows[pl.ds(h * steps + s, 8, stride=tile), :] for h in range(kvs))
+                o_ref[s, where, lse_cols] = sum(stat_rows[pl.ds(h * steps + s, 8, stride=tile), :] for h in range(kvs))
                 for h in range(kvs):
                     for n in range(group):
                         col = (h * group + n) * LANES
@@ -271,20 +274,21 @@
             copy.wait()
 
 
-def attend(positions, q, k_new, v_new, k_rows, v_rows, steps, kvs, group, slots):
+def attend(positions, q, k_new, v_new, k_rows, v_rows, steps, kvs, group, slots, handed=()):
     batch, rows, dim = k_rows.shape
+    half = batch // 2
     vm = pl.BlockSpec(memory_space=pltpu.VMEM)
     hbm = pl.BlockSpec(memory_space=pl.ANY)
     return pl.pallas_call(
-        functools.partial(attend_kernel, (steps, kvs, group, slots, batch // PER)),
-        in_specs=[pl.BlockSpec(memory_space=pltpu.SMEM), vm, vm, vm, hbm, hbm],
-        out_specs=[hbm, hbm, vm, vm],
+        functools.partial(attend_kernel, (steps, kvs, group, slots, half // PER, bool(handed))),
+        in_specs=[pl.BlockSpec(memory_space=pltpu.SMEM), vm, vm, vm, hbm, hbm] + [hbm] * len(handed),
+        out_specs=[hbm, hbm, vm],
         out_shape=[
             jax.ShapeDtypeStruct(k_rows.shape, BF16),
             jax.ShapeDtypeStruct(v_rows.shape, BF16),
-            jax.ShapeDtypeStruct((steps, batch, kvs * group * dim), F32),
-            jax.ShapeDtypeStruct((steps, batch, LANES), F32),
+            jax.ShapeDtypeStruct((steps, half, (kvs * group + 1) * dim), F32),
         ],
+        input_output_aliases={6: 0, 7: 1} if handed else {},
         scratch_shapes=[
             pltpu.VMEM((DEPTH, PER, rows, dim), BF16),
             pltpu.VMEM((DEPTH, PER, rows, dim), BF16),
@@ -295,31 +299,30 @@
             pltpu.SemaphoreType.DMA((DEPTH,)),
             pltpu.SemaphoreType.DMA((DEPTH,)),
         ],
-        compiler_params=pltpu.CompilerParams(vmem_limit_bytes=56 * 2**20),
-        cost_estimate=pl.CostEstimate(flops=4 * batch * rows * q.shape[1] * dim, bytes_accessed=8 * batch * rows * dim,
-                                      transcendentals=batch * rows * q.shape[1]),
-        name="attend",
-    )(positions, q, k_new, v_new, k_rows, v_rows)
+        compiler_params=pltpu.CompilerParams(vmem_limit_bytes=48 * 2**20),
+        cost_estimate=pl.CostEstimate(flops=20_000_000_000, bytes_accessed=4 * batch * rows * dim,
+                                      transcendentals=half * rows * q.shape[1]),
+        name="attend_own" if handed else "attend_peer",
+    )(positions, q, k_new, v_new, k_rows, v_rows, *handed)
 
 
 CHUNK = 512
 RING = 6
-(C_PEER_O, C_STAT, C_OWN_O, C_X_O, C_X_E, C_RS_CORE, C_RS_Y, C_AG_Y, C_AG_OWN, C_AG_FWD) = range(10)
-(J_RS_CORE, J_RS_Y, J_OWN_Y, J_OWN_X, J_OWN_C, J_FWD_X, J_FWD_C, J_XOWN_C, J_XFWD_C) = range(9)
-
-
-def tail_kernel(cfg, o_ref, lse_ref, x_ref, wo_hbm, wfc_hbm, wproj_hbm, bo_ref, gain_ref, shift_ref, bfc_ref, bproj_ref,
+(C_OWN_O, C_X_O, C_OWN_E, C_X_E, C_HID_A, C_HID_B) = range(6)
+(W_CORE, W_Y, J_CORE, J_Y, J_OWN_X, J_OWN_C, J_FWD_C) = range(7)
+
+
+def tail_kernel(cfg, own_ref, xin_ref, x_hbm, wo_hbm, wfc_hbm, wproj_hbm, bo_ref, gain_ref, shift_ref, bfc_ref, bproj_ref,
                 y_ref,
-                in_o_peer, in_o_own, in_lse, to_x, to_x_e, mine, in_x, in_x_e, a_buf,
-                wo_buf, part, in_part, half_sum, in_y, x_buf, x_mid, hid, hid_b,
-                ring, g_buf, p_chunk, in_rc, p_half, in_ry, y_all,
+                sib_own, sib_x, sib_own_e, sib_x_e, a_buf, wo_buf, w_part, w_core, w_half, w_y, x_buf, x_mid, hid, hid_b,
+                ring, g_buf, p_part, p_core, p_half, p_y, y_all, bo_rows, bfc_rows, bproj_rows,
                 send_a, recv_a, send_j, recv_j, wo_sem, x_sem, ring_sem):
     steps, batch, group, chunks, kvs = cfg
     half = batch // 2
-    quarter = half
-    d_model = wo_hbm.shape[1]
+    pair = steps // 2 * half
     head_cols = group * LANES
     ff_own = wfc_hbm.shape[1] // 2
+    per_chunk = CHUNK // LANES
     y = lax.axis_index("tp")
     sq = lax.axis_index("sq")
     x, c = sq // 2, sq % 2
@@ -327,7 +330,9 @@
     xpeer = {"sq": (1 - x) * 2 + c}
     ypeer = {"tp": 1 - y}
     MESH = pl.DeviceIdType.MESH
-    my_step = 2 * c + y
+
+    def chunk_cols(j):
+        return pl.ds(pl.multiple_of(j * CHUNK, CHUNK), CHUNK)
 
     def load_item(item, slot):
         @pl.when(item < chunks)
@@ -337,16 +342,16 @@
 
         @pl.when(item >= chunks)
         def _():
-            col = pl.multiple_of((item - chunks) * CHUNK, CHUNK)
             row = pl.multiple_of(c * ff_own, CHUNK)
-            pltpu.make_async_copy(wproj_hbm.at[pl.ds(row, ff_own), pl.ds(col, CHUNK)], ring.at[slot], ring_sem.at[slot]).start()
+            pltpu.make_async_copy(wproj_hbm.at[pl.ds(row, ff_own), chunk_cols(item - chunks)], ring.at[slot], ring_sem.at[slot]).start()
 
     def wait_item(slot):
         pltpu.make_async_copy(wfc_hbm.at[:, pl.ds(0, CHUNK)], ring.at[slot], ring_sem.at[slot]).wait()
 
-    wo_copy = pltpu.make_async_copy(wo_hbm.at[pl.ds(pl.multiple_of(c * head_cols, LANES), head_cols), :], wo_buf, wo_sem)
+    wo_rows = pl.ds(pl.multiple_of(c * head_cols, LANES), head_cols)
+    wo_copy = pltpu.make_async_copy(wo_hbm.at[wo_rows, :], wo_buf, wo_sem)
     wo_copy.start()
-    x_copy = pltpu.make_async_copy(x_ref.at[my_step, pl.ds(pl.multiple_of(x * half, 8), half), :], x_buf, x_sem)
+    x_copy = pltpu.make_async_copy(x_hbm.at[pl.ds(2 * c, 2), pl.ds(pl.multiple_of(x * half, 8), half), :], x_buf, x_sem)
     x_copy.start()
     for k in range(RING):
         load_item(jnp.int32(k), k)
@@ -360,179 +365,161 @@
         return pltpu.make_async_remote_copy(src_ref=src, dst_ref=dst, send_sem=send_a.at[kind], recv_sem=recv_a.at[kind],
                                             device_id=who, device_id_type=MESH)
 
-    peer_rows = pl.ds(pl.multiple_of((1 - x) * half, 8), half)
-    own_rows = pl.ds(pl.multiple_of(x * half, 8), half)
     sib_cols = pl.ds(pl.multiple_of((1 - c) * head_cols, LANES), head_cols)
-    cp_stat = remote(lse_ref, in_lse, C_STAT, sib)
-    cp_peer = remote(o_ref.at[:, peer_rows, sib_cols], in_o_peer, C_PEER_O, sib)
-    cp_own = remote(o_ref.at[:, own_rows, sib_cols], in_o_own, C_OWN_O, sib)
-    cp_stat.start()
-    cp_peer.start()
-    cp_own.start()
+    stat_cols = slice(kvs * head_cols, kvs * head_cols + LANES)
+    swaps = [remote(own_ref.at[:, :, stat_cols], sib_own_e, C_OWN_E, sib), remote(xin_ref.at[:, :, stat_cols], sib_x_e, C_X_E, sib),
+             remote(own_ref.at[:, :, sib_cols], sib_own, C_OWN_O, sib), remote(xin_ref.at[:, :, sib_cols], sib_x, C_X_O, sib)]
+    for copy in swaps:
+        copy.start()
+    bo_rows[...] = bo_ref[...].astype(F32)
+    bfc_rows[...] = bfc_ref[...].astype(F32)
+    bproj_rows[...] = bproj_ref[...].astype(F32)
+
+    def flat(block):
+        return block.reshape(steps * half, LANES)
 
     def my_lanes(stat):
+        stat = flat(stat)
         return jnp.where(c == 0, stat, pltpu.roll(stat, LANES - group, 1))
 
-    def weights_of(e1, e2):
-        top = jnp.maximum(e1, e2)
-        w1 = jnp.exp2(e1 - top)
-        w2 = jnp.exp2(e2 - top)
-        tot = w1 + w2
-        inv = 1.0 / tot
-        return w1 * inv, w2 * inv, top + jnp.log2(tot)
-
-    def merge_core(rows, incoming, out, keep_e):
-        for s in range(steps):
-            w1, w2, e = weights_of(my_lanes(lse_ref[s, rows, :]), my_lanes(in_lse[s, rows, :]))
-            keep_e[s] = e
-            for i in range(group):
-                col = pl.ds(pl.multiple_of(c * head_cols + i * LANES, LANES), LANES)
-                out[s, :, i * LANES:(i + 1) * LANES] = (w1[:, i:i + 1] * o_ref[s, rows, col]
-                                                        + w2[:, i:i + 1] * incoming[s, :, i * LANES:(i + 1) * LANES])
-
-    mine_e = hid.at[pl.ds(0, steps * half), pl.ds(0, LANES)]
-    cp_stat.wait_recv()
-    cp_peer.wait_recv()
-    merge_core(peer_rows, in_o_peer, to_x, to_x_e)
-    cp_xe = remote(to_x_e, in_x_e, C_X_E, xpeer)
-    cp_xo = remote(to_x, in_x, C_X_O, xpeer)
-    cp_xe.start()
-    cp_xo.start()
-    cp_own.wait_recv()
-    for s in range(steps):
-        w1, w2, e = weights_of(my_lanes(lse_ref[s, own_rows, :]), my_lanes(in_lse[s, own_rows, :]))
-        mine_e[s * half:(s + 1) * half, :] = e
-        for i in range(group):
-            col = pl.ds(pl.multiple_of(c * head_cols + i * LANES, LANES), LANES)
-            mine[s, :, i * LANES:(i + 1) * LANES] = (w1[:, i:i + 1] * o_ref[s, own_rows, col]
-                                                     + w2[:, i:i + 1] * in_o_own[s, :, i * LANES:(i + 1) * LANES])
+    swaps[0].wait_recv()
+    swaps[1].wait_recv()
+    logs = [my_lanes(own_ref[:, :, stat_cols]), my_lanes(sib_own_e[...]), my_lanes(xin_ref[:, :, stat_cols]), my_lanes(sib_x_e[...])]
+    top = functools.reduce(jnp.maximum, logs)
+    shares = [jnp.exp2(e - top) for e in logs]
+    inv = 1.0 / sum(shares)
+    shares = [w * inv for w in shares]
+    swaps[2].wait_recv()
+    swaps[3].wait_recv()
+    for i in range(group):
+        mine = pl.ds(pl.multiple_of(c * head_cols + i * LANES, LANES), LANES)
+        theirs = slice(i * LANES, (i + 1) * LANES)
+        parts = [own_ref[:, :, mine], sib_own[:, :, theirs], xin_ref[:, :, mine], sib_x[:, :, theirs]]
+        a_buf[:, theirs] = sum(w[:, i:i + 1] * flat(part) for w, part in zip(shares, parts)).astype(BF16)
+
+    def jcopy(src, dst, kind, j, who):
+        return pltpu.make_async_remote_copy(src_ref=src, dst_ref=dst, send_sem=send_j.at[kind, j], recv_sem=recv_j.at[kind, j],
+                                            device_id=who, device_id_type=MESH)
+
+    def pair_rows(core):
+        return pl.ds(pl.multiple_of(core * pair, 8), pair)
+
+    def to_core(part, inbox, kind, j):
+        return jcopy(part.at[j, pair_rows(1 - c), :], inbox.at[j], kind, j, sib)
+
+    def to_y(total, inbox, kind, j):
+        return jcopy(total.at[j], inbox.at[j], kind, j, ypeer)
+
+    def core_sum(part, inbox, total, inbox_y, kind, kind_y, j):
+        to_core(part, inbox, kind, j).wait_recv()
+        total[j] = part[j, pair_rows(c), :] + inbox[j]
+        to_y(total, inbox_y, kind_y, j).start()
+
+    def bias_of(rows, j):
+        return jnp.concatenate([rows[pl.ds(j * per_chunk + e, 1), :] for e in range(per_chunk)], axis=-1)
+
+    def y_sum(total, inbox):
+        low = jnp.where(y == 0, total, inbox)
+        high = jnp.where(y == 0, inbox, total)
+        return low + high
+
+    def stage(it, lag, body):
+        j = it - lag
+
+        @pl.when((j >= 0) & (j < chunks))
+        def _():
+            body(j)
+
+    def o_product(j):
+        w_part[j] = jnp.dot(a_buf[...], wo_buf[:, chunk_cols(j)], preferred_element_type=F32)
+        to_core(w_part, w_core, W_CORE, j).start()
+
+    def o_core_sum(j):
+        core_sum(w_part, w_core, w_half, w_y, W_CORE, W_Y, j)
+
+    wo_copy.wait()
     x_copy.wait()
-    cp_xe.wait_recv()
-    cp_xo.wait_recv()
-    w1, w2, _ = weights_of(mine_e[...], in_x_e[...].reshape(steps * half, LANES))
-    for i in range(group):
-        cols = slice(i * LANES, (i + 1) * LANES)
-        a_buf[:, cols] = (w1[:, i:i + 1] * mine[:, :, cols].reshape(steps * half, LANES)
-                          + w2[:, i:i + 1] * in_x[:, :, cols].reshape(steps * half, LANES)).astype(BF16)
-
-    wo_copy.wait()
+
+    @pl.loop(0, chunks + 3)
+    def _(it):
+        stage(it, 0, o_product)
+        stage(it, 3, o_core_sum)
 
     @pl.loop(0, chunks)
     def _(j):
-        cols = pl.ds(pl.multiple_of(j * CHUNK, CHUNK), CHUNK)
-        part[:, cols] = jnp.dot(a_buf[...], wo_buf[:, cols], preferred_element_type=F32)
-
-    def step_rows(s, n=1):
-        return pl.ds(pl.multiple_of(s * half, 8), n * half)
-
-    cp_rs = remote(part.at[step_rows(2 * (1 - c), 2), :], in_part, C_RS_CORE, sib)
-    cp_rs.start()
-    cp_rs.wait_recv()
-    half_sum[...] = part[step_rows(2 * c, 2), :] + in_part[...]
-    cp_ry = remote(half_sum.at[step_rows(1 - y), :], in_y, C_RS_Y, ypeer)
-    cp_ry.start()
-    cp_ry.wait_recv()
-    x_new = (x_buf[...] + (half_sum[step_rows(y), :] + in_y[...]) + bo_ref[...]).astype(BF16).astype(F32)
-    x_mid[...] = x_new
-    mean = jnp.mean(x_new, axis=-1, keepdims=True)
-    cent = x_new - mean
-    var = jnp.mean(cent * cent, axis=-1, keepdims=True)
-    normed = cent * lax.rsqrt(var + LN_EPS) * gain_ref[...] + shift_ref[...]
-    hid[step_rows(my_step), :] = normed.astype(BF16).astype(F32)
-
-    own_h = hid.at[step_rows(my_step), :]
-    peer_h = hid.at[step_rows(2 * c + 1 - y), :]
-    cp_ay = remote(own_h, own_h, C_AG_Y, ypeer)
-    cp_ac = remote(own_h, own_h, C_AG_OWN, sib)
-    cp_ay.start()
-    cp_ac.start()
-    cp_ay.wait_recv()
-    cp_af = remote(peer_h, peer_h, C_AG_FWD, sib)
-    cp_af.start()
-    cp_ac.wait_recv()
-    cp_af.wait_recv()
+        cols = chunk_cols(j)
+        to_y(w_half, w_y, W_Y, j).wait_recv()
+        x_in = x_buf[:, :, cols].astype(F32).reshape(pair, CHUNK)
+        x_mid[:, cols] = (x_in + y_sum(w_half[j], w_y[j]) + bias_of(bo_rows, j)).astype(BF16).astype(F32)
+
+    gain = gain_ref[...].astype(F32)
+    shift = shift_ref[...].astype(F32)
+    d_model = x_mid.shape[1]
+    hid_copies = []
+    for part in range(2):
+        src = slice(part * half, (part + 1) * half)
+        dst = pl.ds(pl.multiple_of(c * pair + part * half, 8), half)
+        rows = x_mid[src, :]
+        mean = jnp.mean(rows, axis=-1, keepdims=True)
+        cent = rows - mean
+        rstd = lax.rsqrt(jnp.mean(cent * cent, axis=-1, keepdims=True) + LN_EPS)
+        for n in range(d_model // LANES):
+            cols = slice(n * LANES, (n + 1) * LANES)
+            hid[dst, cols] = (cent[:, cols] * rstd * gain[n:n + 1, :] + shift[n:n + 1, :]).astype(BF16).astype(F32)
+        copy = remote(hid.at[dst, :], hid.at[dst, :], (C_HID_A, C_HID_B)[part], sib)
+        copy.start()
+        hid_copies.append(copy)
+    for copy in hid_copies:
+        copy.wait_recv()
     hid_b[...] = hid[...].astype(BF16)
 
     @pl.loop(0, chunks)
     def _(j):
         slot = lax.rem(j, RING)
         wait_item(slot)
-        pre = jnp.dot(hid_b[...], ring[slot], preferred_element_type=F32) + bfc_ref[pl.ds(c * chunks + j, 1), :]
+        pre = jnp.dot(hid_b[...], ring[slot], preferred_element_type=F32) + bias_of(bfc_rows, c * chunks + j)
         cube = pre * pre * pre
         act = 0.5 * pre * (1.0 + jnp.tanh(math.sqrt(2.0 / math.pi) * (pre + 0.044715 * cube)))
-        g_buf[:, pl.ds(pl.multiple_of(j * CHUNK, CHUNK), CHUNK)] = act.astype(BF16)
+        g_buf[:, chunk_cols(j)] = act.astype(BF16)
         load_item(j + RING, slot)
 
-    def jcopy(src, dst, kind, j, who):
-        return pltpu.make_async_remote_copy(src_ref=src, dst_ref=dst, send_sem=send_j.at[kind, j], recv_sem=recv_j.at[kind, j],
-                                            device_id=who, device_id_type=MESH)
-
-    def rs_core(j):
-        return jcopy(p_chunk.at[j, step_rows(2 * (1 - c), 2), :], in_rc.at[j], J_RS_CORE, j, sib)
-
-    def rs_y(j):
-        return jcopy(p_half.at[j, step_rows(1 - y), :], in_ry.at[j], J_RS_Y, j, ypeer)
-
-    def block(j, s, xx):
-        return y_all.at[j, s, pl.ds(pl.multiple_of(xx * half, 8), half), :]
+    def block(j, core, xx):
+        return y_all.at[j, pl.ds(2 * core, 2), pl.ds(pl.multiple_of(xx * half, 8), half), :]
 
     def spread(kind, j):
-        own = block(j, my_step, x)
-        ypart = block(j, 2 * c + 1 - y, x)
-        xpart = block(j, my_step, 1 - x)
-        diag = block(j, 2 * c + 1 - y, 1 - x)
-        ref, who = {J_OWN_Y: (own, ypeer), J_OWN_X: (own, xpeer), J_OWN_C: (own, sib),
-                    J_FWD_X: (ypart, xpeer), J_FWD_C: (ypart, sib),
-                    J_XOWN_C: (xpart, sib), J_XFWD_C: (diag, sib)}[kind]
+        ref, who = {J_OWN_X: (block(j, c, x), xpeer), J_OWN_C: (block(j, c, x), sib), J_FWD_C: (block(j, c, 1 - x), sib)}[kind]
         return jcopy(ref, ref, kind, j, who)
-
-    def stage(it, lag, body):
-        j = it - lag
-
-        @pl.when((j >= 0) & (j < chunks))
-        def _():
-            body(j)
 
     def do_product(j):
         item = chunks + j
         slot = lax.rem(item, RING)
         wait_item(slot)
-        p_chunk[j] = jnp.dot(g_buf[...], ring[slot], preferred_element_type=F32)
+        p_part[j] = jnp.dot(g_buf[...], ring[slot], preferred_element_type=F32)
 
         @pl.when(item + RING < 2 * chunks)
         def _():
             load_item(item + RING, slot)
 
-        rs_core(j).start()
+        to_core(p_part, p_core, J_CORE, j).start()
 
     def do_core_sum(j):
-        rs_core(j).wait_recv()
-        p_half[j] = p_chunk[j, step_rows(2 * c, 2), :] + in_rc[j]
-        rs_y(j).start()
+        core_sum(p_part, p_core, p_half, p_y, J_CORE, J_Y, j)
 
     def do_y_sum(j):
-        rs_y(j).wait_recv()
-        cols = pl.ds(pl.multiple_of(j * CHUNK, CHUNK), CHUNK)
-        full = x_mid[:, cols] + (p_half[j, step_rows(y), :] + in_ry[j]) + bproj_ref[:, cols]
-        y_all[j, my_step, pl.ds(pl.multiple_of(x * half, 8), half), :] = full.astype(BF16).astype(F32)
-        for kind in (J_OWN_Y, J_OWN_X, J_OWN_C):
-            spread(kind, j).start()
+        to_y(p_half, p_y, J_Y, j).wait_recv()
+        full = x_mid[:, chunk_cols(j)] + y_sum(p_half[j], p_y[j]) + bias_of(bproj_rows, j)
+        y_all[j, pl.ds(2 * c, 2), pl.ds(pl.multiple_of(x * half, 8), half), :] = full.astype(BF16).astype(F32).reshape(2, half, CHUNK)
+        spread(J_OWN_X, j).start()
+        spread(J_OWN_C, j).start()
 
     def do_forward(j):
-        spread(J_OWN_Y, j).wait_recv()
-        spread(J_FWD_X, j).start()
+        spread(J_OWN_X, j).wait_recv()
         spread(J_FWD_C, j).start()
-        spread(J_OWN_X, j).wait_recv()
-        spread(J_XOWN_C, j).start()
-
-    def do_diag(j):
-        spread(J_FWD_X, j).wait_recv()
-        spread(J_XFWD_C, j).start()
 
     def do_store(j):
-        for kind in (J_OWN_C, J_FWD_C, J_XOWN_C, J_XFWD_C):
-            spread(kind, j).wait_recv()
-        y_ref[:, :, pl.ds(pl.multiple_of(j * CHUNK, CHUNK), CHUNK)] = y_all[j].astype(BF16)
+        spread(J_OWN_C, j).wait_recv()
+        spread(J_FWD_C, j).wait_recv()
+        y_ref[:, :, chunk_cols(j)] = y_all[j].astype(BF16)
 
     @pl.loop(0, chunks + 7)
     def _(it):
@@ -540,24 +527,26 @@
         stage(it, 1, do_core_sum)
         stage(it, 3, do_y_sum)
         stage(it, 5, do_forward)
-        stage(it, 6, do_diag)
         stage(it, 7, do_store)
 
-    for cp in (cp_stat, cp_peer, cp_own, cp_xe, cp_xo, cp_rs, cp_ry, cp_ay, cp_ac, cp_af):
-        cp.wait_send()
+    for copy in swaps + hid_copies:
+        copy.wait_send()
 
     @pl.loop(0, chunks)
     def _(j):
-        rs_core(j).wait_send()
-        rs_y(j).wait_send()
-        for kind in (J_OWN_Y, J_OWN_X, J_OWN_C, J_FWD_X, J_FWD_C, J_XOWN_C, J_XFWD_C):
+        to_core(w_part, w_core, W_CORE, j).wait_send()
+        to_y(w_half, w_y, W_Y, j).wait_send()
+        to_core(p_part, p_core, J_CORE, j).wait_send()
+        to_y(p_half, p_y, J_Y, j).wait_send()
+        for kind in (J_OWN_X, J_OWN_C, J_FWD_C):
             spread(kind, j).wait_send()
 
 
-def tail(o_part, lse, x_steps, w_o, w_fc, w_proj, b_o, gain, shift, b_fc, b_proj, group, kvs):
-    steps, batch, cols = o_part.shape
-    half = batch // 2
+def tail(own, x_in, x_steps, w_o, w_fc, w_proj, b_o, gain, shift, b_fc, b_proj, group, kvs):
+    steps, half, _ = own.shape
+    batch = 2 * half
     rows = steps * half
+    pair = rows // 2
     d_model = w_o.shape[1]
     chunks = d_model // CHUNK
     ff_own = w_fc.shape[1] // 2
@@ -566,36 +555,36 @@
     vm = pl.BlockSpec(memory_space=pltpu.VMEM)
     hbm = pl.BlockSpec(memory_space=pl.ANY)
     cfg = (steps, batch, group, chunks, kvs)
+    tiles = lambda vec: vec.reshape(-1, LANES)
     scratch = [
         pltpu.VMEM((steps, half, head_cols), F32),
         pltpu.VMEM((steps, half, head_cols), F32),
-        pltpu.VMEM((steps, batch, LANES), F32),
-        pltpu.VMEM((steps, half, head_cols), F32),
         pltpu.VMEM((steps, half, LANES), F32),
-        pltpu.VMEM((steps, half, head_cols), F32),
-        pltpu.VMEM((steps, half, head_cols), F32),
         pltpu.VMEM((steps, half, LANES), F32),
         pltpu.VMEM((rows, head_cols), BF16),
         pltpu.VMEM((head_cols, d_model), BF16),
-        pltpu.VMEM((rows, d_model), F32),
-        pltpu.VMEM((2 * half, d_model), F32),
-        pltpu.VMEM((2 * half, d_model), F32),
-        pltpu.VMEM((half, d_model), F32),
-        pltpu.VMEM((half, d_model), F32),
-        pltpu.VMEM((half, d_model), F32),
+        pltpu.VMEM((chunks, rows, CHUNK), F32),
+        pltpu.VMEM((chunks, pair, CHUNK), F32),
+        pltpu.VMEM((chunks, pair, CHUNK), F32),
+        pltpu.VMEM((chunks, pair, CHUNK), F32),
+        pltpu.VMEM((2, half, d_model), BF16),
+        pltpu.VMEM((pair, d_model), F32),
         pltpu.VMEM((rows, d_model), F32),
         pltpu.VMEM((rows, d_model), BF16),
         pltpu.VMEM((RING, d_model, CHUNK), BF16),
         pltpu.VMEM((rows, ff_own), BF16),
         pltpu.VMEM((chunks, rows, CHUNK), F32),
-        pltpu.VMEM((chunks, 2 * half, CHUNK), F32),
-        pltpu.VMEM((chunks, 2 * half, CHUNK), F32),
-        pltpu.VMEM((chunks, half, CHUNK), F32),
+        pltpu.VMEM((chunks, pair, CHUNK), F32),
+        pltpu.VMEM((chunks, pair, CHUNK), F32),
+        pltpu.VMEM((chunks, pair, CHUNK), F32),
         pltpu.VMEM((chunks, steps, batch, CHUNK), F32),
-        pltpu.SemaphoreType.DMA((10,)),
-        pltpu.SemaphoreType.DMA((10,)),
-        pltpu.SemaphoreType.DMA((9, chunks)),
-        pltpu.SemaphoreType.DMA((9, chunks)),
+        pltpu.VMEM((d_model // LANES, LANES), F32),
+        pltpu.VMEM((2 * ff_own // LANES, LANES), F32),
+        pltpu.VMEM((d_model // LANES, LANES), F32),
+        pltpu.SemaphoreType.DMA((6,)),
+        pltpu.SemaphoreType.DMA((6,)),
+        pltpu.SemaphoreType.DMA((7, chunks)),
+        pltpu.SemaphoreType.DMA((7, chunks)),
         pltpu.SemaphoreType.DMA,
         pltpu.SemaphoreType.DMA,
         pltpu.SemaphoreType.DMA((RING,)),
@@ -609,7 +598,7 @@
         compiler_params=pltpu.CompilerParams(collective_id=0, has_side_effects=True, vmem_limit_bytes=VMEM_CAP),
         cost_estimate=pl.CostEstimate(flops=2 * rows * d_model * (head_cols + 2 * ff_own), bytes_accessed=100_000_000, transcendentals=0),
         name="tail",
-    )(o_part, lse, x_steps, w_o, w_fc, w_proj, b_o, gain, shift, b_fc, b_proj)
+    )(own, x_in, x_steps, w_o, w_fc, w_proj, tiles(b_o), tiles(gain), tiles(shift), tiles(b_fc), tiles(b_proj))
 
 
 def solution(mesh):
@@ -634,11 +623,13 @@
         cur_pos = positions[None, :] + jnp.arange(steps, dtype=jnp.int32)[:, None]
         cos_t, sin_t = rope_tables(cur_pos, dim)
         q_rows, k_new, v_new = front(x_steps, ln1_gain, ln1_bias, cos_t, sin_t, b_q, b_k, b_v, w_q, w_k, w_v, kvs)
-        k_out, v_out, o_part, lse = attend(positions, q_rows, k_new, v_new, key_buf.reshape(batch, slots_local * kvs, dim),
-                                           val_buf.reshape(batch, slots_local * kvs, dim), steps, kvs, group, slots)
-        row = lambda vec: vec.astype(F32).reshape(1, -1)
-        ys = tail(o_part, lse, x_steps.astype(F32), w_o, w_fc, w_proj, row(b_o), row(ln2_gain), row(ln2_bias),
-                  b_fc.astype(F32).reshape(-1, CHUNK), row(b_proj), group, kvs)
+        k_rows = key_buf.reshape(batch, slots_local * kvs, dim)
+        v_rows = val_buf.reshape(batch, slots_local * kvs, dim)
+        caches = (positions, q_rows, k_new, v_new, k_rows, v_rows, steps, kvs, group, slots)
+        k_out, v_out, for_peer = attend(*caches)
+        from_peer = lax.ppermute(for_peer, "sq", [(d, d ^ 2) for d in range(sq_size)])
+        k_out, v_out, own = attend(*caches, handed=(k_out, v_out))
+        ys = tail(own, from_peer, x_steps, w_o, w_fc, w_proj, b_o, ln2_gain, ln2_bias, b_fc, b_proj, group, kvs)
         return ys, k_out.reshape(key_buf.shape), v_out.reshape(val_buf.shape)
 
     return jax.shard_map(per_device, mesh=mesh, in_specs=in_specs, out_specs=out_specs, check_vma=False)

time: 157 us -> 143 us (0.911)
  Pallas kernels: 142 us -> 128 us
  starting transfers between devices: 0 us -> 3.37 us
  other arithmetic: 4.05 us -> 1.82 us
  local copies, waits for them, and re-layouts: 9.44 us -> 7.7 us
    pallas_call x1, Pallas kernels: 91.8 us -> 77.6 us  [tail(): pl.pallas_call(functools.partial(tail_kernel, cfg), out_shape=jax.ShapeDt...]
    reshape x5 -> x0, local copies, waits for them, and re-layouts: 6.64 us -> none  [the longest x4 5.28 us: per_device(): row = lambda vec: vec.astype(F32).reshape(1, -1)]
    unnamed x3 -> x13, local copies, waits for them, and re-layouts: 2.8 us -> 7.7 us
    ppermute x0 -> x1, starting transfers between devices: none -> 3.37 us  [per_device(): lax.ppermute(for_peer, 'sq', [(d, d ^ 2) for d in range(sq_size)])]
    convert_element_type x1 -> x0, other arithmetic: 2.15 us -> none  [per_device(): x_steps.astype(F32)]
    pallas_call x1 -> x2, Pallas kernels: 36.7 us -> 36.9 us  [attend(): pl.pallas_call(functools.partial(attend_kernel, (steps, kvs, group, slots...]
  transfers between devices with their start and end apart: 0 -> 1, of which waited for: 0 -> 1; matrix products, arithmetic and copies ran while one was open for 0% -> 0% of each run, Pallas kernels for 0% -> 13%
where the time goes in v3:
time: 143 us
  Pallas kernels  128 us (90%)
  local copies, waits for them, and re-layouts  7.7 us (5%)
  starting transfers between devices  3.37 us (2%)
  other arithmetic  1.82 us (1%)
    pallas_call x1, Pallas kernels, tail(): pl.pallas_call(functools.partial(tail_kernel, cfg), out_shape=jax.ShapeDt...  77.6 us
    pallas_call x2, Pallas kernels, attend(): pl.pallas_call(functools.partial(attend_kernel, (steps, kvs, group, slots...  36.9 us
    pallas_call x1, Pallas kernels, front(): pl.pallas_call(functools.partial(front_kernel, (steps, kvs, group)), out_...  13.5 us
    unnamed x13, local copies, waits for them, and re-layouts  7.7 us
    ppermute x1, starting transfers between devices, per_device(): lax.ppermute(for_peer, 'sq', [(d, d ^ 2) for d in range(sq_size)])  3.37 us
  transfers between devices with their start and end apart: 1, of which 1 were waited for; matrix products, arithmetic and copies ran while one was open for 0% of the time, Pallas kernels for 13%

profile of v3, /device:TPU:0, one launch (start us, length us, event | category | flops | bytes accessed | tf_op | source)
XLA Modules:
  0.0 142.8 jit_solution(10902261645119237335)
XLA Ops:
  0.6 0.0 copy-start.4
  0.7 0.7 add_convert_fusion
  1.4 1.1 multiply_sine_fusion
  2.5 13.5 %front.1 = (bf16[48,72,128]{2,1,0:T(8,128)(2,1)}, bf16[48,16,128]{2,1,0:T(8,128)(2,1)}, bf16[48,16,128]{2,1,0:T(8,128)(2,1)}) custom-call(bf16[4,48,4608]{2,1,0:T(8,128)(2,1)} %x_hbm.1, bf16[36,128]{1,0:T(8,128)(2,1)} %bitcast.21, bf16[36,128]{1,0:T(8,128)(2,1)} %bitcast.22, f32[4,48,64]{2,1,0:T(8,128)} %get-tuple-element.22.cos_ref, ...), custom_call_target="tpu_custom_call" | custom-call | flops 4982833152 | bytes 25952256 | tf_op jit(solution)/shard_map/front/pallas_call | solution.py:107
  16.0 0.0 copy-done.4
  16.0 0.0 copy-start.1
  16.0 1.2 copy-done.1
  17.1 0.0 copy-start.2
  17.1 0.9 copy-done.2
  18.1 0.0 copy-start.3
  18.1 0.9 copy-done.3
  19.0 18.4 %attend_peer.1 = (bf16[48,2048,128]{2,1,0:T(8,128)(2,1)}, bf16[48,2048,128]{2,1,0:T(8,128)(2,1)}, f32[4,24,2432]{2,1,0:T(8,128)S(1)}) custom-call(s32[48]{0:T(128)S(1)} %copy-done.4, bf16[48,72,128]{2,1,0:T(8,128)(2,1)S(1)} %copy-done.1, bf16[48,16,128]{2,1,0:T(8,128)(2,1)S(1)} %copy-done.2, bf16[48,16,128]{2,1,0:T(8,128)(2,1)S(1)} %copy-done.3, ...), custom_call_target="tpu_custom_call" | custom-call | flops 20000000000 | bytes 50331648 | tf_op jit(solution)/shard_map/attend_peer/pallas_call | solution.py:282
  37.4 3.4 %collective-permute-start = (f32[4,24,2432]{2,1,0:T(8,128)S(1)}, f32[4,24,2432]{2,1,0:T(8,128)S(1)}, u32[]{:S(2)}, u32[]{:S(2)}) collective-permute-start(f32[4,24,2432]{2,1,0:T(8,128)S(1)} %get-tuple-element.18), channel_id=1, source_target_pairs={{0,2},{1,3},{2,0},{3,1},{4,6},{5,7},{6,4},{7,5}} | collective-permute-start | bytes 2801672 | tf_op jit(solution)/shard_map/ppermute | solution.py:630
  40.8 18.4 %attend_own.1 = (bf16[48,2048,128]{2,1,0:T(8,128)(2,1)}, bf16[48,2048,128]{2,1,0:T(8,128)(2,1)}, f32[4,24,2432]{2,1,0:T(8,128)S(1)}) custom-call(s32[48]{0:T(128)S(1)} %copy-done.4, bf16[48,72,128]{2,1,0:T(8,128)(2,1)S(1)} %copy-done.1, bf16[48,16,128]{2,1,0:T(8,128)(2,1)S(1)} %copy-done.2, ...), custom_call_target="tpu_custom_call", output_to_operand_aliasing={{0}: (6, {}), {1}: (7, {})} | custom-call | flops 20000000000 | bytes 50331648 | tf_op jit(solution)/shard_map/attend_own/pallas_call | solution.py:282
  59.2 0.0 copy-start
  59.3 0.9 copy-done
  60.2 1.3 collective-permute-done.xin_ref
  61.5 0.0 copy-start.5
  61.5 1.0 copy-done.5
  62.5 77.6 %tail.1 = bf16[4,48,4608]{2,1,0:T(8,128)(2,1)} custom-call(f32[4,24,2432]{2,1,0:T(8,128)} %copy-done, f32[4,24,2432]{2,1,0:T(8,128)} %copy-done.5, bf16[4,48,4608]{2,1,0:T(8,128)(2,1)} %x_hbm.1, bf16[2304,4608]{1,0:T(8,128)(2,1)} %wo_hbm.1, bf16[4608,9216]{1,0:T(8,128)(2,1)} %wfc_hbm.1, bf16[9216,4608]{1,0:T(8,128)(2,1)} %wproj_hbm.1, ...), custom_call_target="tpu_custom_call" | custom-call | flops 9172942848 | bytes 100000000 | tf_op jit(solution)/shard_map/tail/pallas_call | solution.py:592
  140.0 2.8 %copy.28 = bf16[4,48,4608]{2,1,0:T(8,128)(2,1)} copy(bf16[4,48,4608]{2,1,0:T(8,128)(2,1)} %tail.1) | data formatting | bytes 3538944
  (1 shorter events, 0.0 us)
Async XLA Ops:
  0.6 15.3 %copy-start.4 = (s32[48]{0:T(128)S(1)}, s32[48]{0:T(128)}, u32[]{:S(2)}) copy-start(s32[48]{0:T(128)} %pos_ref.3) | copy-start | bytes 580
  16.0 1.2 copy-start.1
  17.1 0.9 copy-start.2
  18.1 0.9 copy-start.3
  37.4 24.1 %collective-permute-start = (f32[4,24,2432]{2,1,0:T(8,128)S(1)}, f32[4,24,2432]{2,1,0:T(8,128)S(1)}, u32[]{:S(2)}, u32[]{:S(2)}) collective-permute-start(f32[4,24,2432]{2,1,0:T(8,128)S(1)} %get-tuple-element.18), channel_id=1, source_target_pairs={{0,2},{1,3},{2,0},{3,1},{4,6},{5,7},{6,4},{7,5}} | collective-permute-start | bytes 2801672 | tf_op jit(solution)/shard_map/ppermute | solution.py:630
  59.2 0.9 copy-start
  61.5 1.0 copy-start.5

commit v4 on v3

--- a/solution.py
+++ b/solution.py
@@ -134,9 +134,10 @@
 DEPTH = 8
 AHEAD = 4
 
-def attend_kernel(cfg, pos_ref, q_ref, kn_ref, vn_ref, k_hbm, v_hbm, *refs):
+def attend_kernel(cfg, pos_ref, q_hbm, kn_hbm, vn_hbm, k_hbm, v_hbm, *refs):
     steps, kvs, group, slots, n_blocks, own_half = cfg
-    ko_hbm, vo_hbm, o_ref, k_buf, v_buf, o_rows, stat_rows, k_in, v_in, k_up, v_up = refs[2 if own_half else 0:]
+    (ko_hbm, vo_hbm, o_hbm, k_buf, v_buf, q_ref, kn_ref, vn_ref, o_tile, o_rows, stat_rows,
+     k_in, v_in, k_up, v_up, small_in, o_up) = refs[2 if own_half else 0:]
     x = lax.axis_index("sq") // 2
     base = (x if own_half else 1 - x) * (n_blocks * PER)
     lse_cols = slice(kvs * group * LANES, (kvs * group + 1) * LANES)
@@ -161,9 +162,20 @@
         return (pltpu.make_async_copy(k_buf.at[slot], ko_hbm.at[seqs(i)], k_up.at[slot]),
                 pltpu.make_async_copy(v_buf.at[slot], vo_hbm.at[seqs(i)], v_up.at[slot]))
 
+    half_seqs = pl.ds(base, n_blocks * PER)
+    small = [pltpu.make_async_copy(src.at[half_seqs], dst, small_in.at[n])
+             for n, (src, dst) in enumerate(((q_hbm, q_ref), (kn_hbm, kn_ref), (vn_hbm, vn_ref)))]
+    for copy in small:
+        copy.start()
     for i in range(AHEAD):
         for copy in fetch(jnp.int32(i)):
             copy.start()
+
+    def put_tile(t):
+        return pltpu.make_async_copy(o_tile.at[t], o_hbm.at[:, pl.ds(pl.multiple_of(t * 8, 8), 8), :], o_up.at[t])
+
+    for copy in small:
+        copy.wait()
 
     sub = lax.broadcasted_iota(jnp.int32, (tile, rows), 0)
     lane = lax.broadcasted_iota(jnp.int32, (tile, rows), 1)
@@ -178,8 +190,8 @@
     def renew(i):
         slot_of = lax.rem(i, DEPTH)
         for one in range(PER):
-            seq = base + i * PER + one
-            goal = kvs * ((pos_ref[seq] & (slots - 1)) - first)
+            seq = i * PER + one
+            goal = kvs * ((pos_ref[base + seq] & (slots - 1)) - first)
             goal = jnp.where(goal > kvs * (slots - steps), goal - kvs * slots, goal)
             start = pl.multiple_of(jnp.clip((goal >> 4) << 4, 0, rows - 32), 16)
             offset = win_row + (start - goal)
@@ -213,13 +225,17 @@
             for copy in put(i - 1):
                 copy.start()
 
+        @pl.when((i >= 1) & (lax.rem(i, blocks_per_tile) == 0))
+        def _():
+            put_tile(i // blocks_per_tile - 1).start()
+
         k_copy, v_copy = fetch(i)
         k_copy.wait()
         v_copy.wait()
         state = []
         for one in range(PER):
-            seq = base + i * PER + one
-            pos = pos_ref[seq]
+            seq = i * PER + one
+            pos = pos_ref[base + seq]
             q = q_ref[seq]
             raw = lax.dot_general(q, k_buf[slot_now, one], contract_last, preferred_element_type=F32)
             raw2 = lax.dot_general(q, kn_ref[seq], contract_last, preferred_element_type=F32)
@@ -258,31 +274,34 @@
             stat_rows[pl.ds(pl.multiple_of(seat * tile, 8), tile), :] = stats
         @pl.when(lax.rem(i, blocks_per_tile) == blocks_per_tile - 1)
         def _():
-            where = pl.ds(pl.multiple_of((i // blocks_per_tile) * 8, 8), 8)
+            t = i // blocks_per_tile
             for s in range(steps):
-                o_ref[s, where, lse_cols] = sum(stat_rows[pl.ds(h * steps + s, 8, stride=tile), :] for h in range(kvs))
+                o_tile[t, s, :, lse_cols] = sum(stat_rows[pl.ds(h * steps + s, 8, stride=tile), :] for h in range(kvs))
                 for h in range(kvs):
                     for n in range(group):
                         col = (h * group + n) * LANES
-                        o_ref[s, where, col:col + LANES] = o_rows[pl.ds(n * tile + h * steps + s, 8, stride=per_row), :]
+                        o_tile[t, s, :, col:col + LANES] = o_rows[pl.ds(n * tile + h * steps + s, 8, stride=per_row), :]
 
     renew(jnp.int32(n_blocks - 1))
     for copy in put(n_blocks - 1):
         copy.start()
+    tiles = n_blocks // blocks_per_tile
+    put_tile(tiles - 1).start()
     for j in range(AHEAD):
         for copy in put(n_blocks - AHEAD + j):
             copy.wait()
+    for t in range(tiles):
+        put_tile(t).wait()
 
 
 def attend(positions, q, k_new, v_new, k_rows, v_rows, steps, kvs, group, slots, handed=()):
     batch, rows, dim = k_rows.shape
     half = batch // 2
-    vm = pl.BlockSpec(memory_space=pltpu.VMEM)
     hbm = pl.BlockSpec(memory_space=pl.ANY)
     return pl.pallas_call(
         functools.partial(attend_kernel, (steps, kvs, group, slots, half // PER, bool(handed))),
-        in_specs=[pl.BlockSpec(memory_space=pltpu.SMEM), vm, vm, vm, hbm, hbm] + [hbm] * len(handed),
-        out_specs=[hbm, hbm, vm],
+        in_specs=[pl.BlockSpec(memory_space=pltpu.SMEM)] + [hbm] * (5 + len(handed)),
+        out_specs=[hbm, hbm, hbm],
         out_shape=[
             jax.ShapeDtypeStruct(k_rows.shape, BF16),
             jax.ShapeDtypeStruct(v_rows.shape, BF16),
@@ -292,14 +311,20 @@
         scratch_shapes=[
             pltpu.VMEM((DEPTH, PER, rows, dim), BF16),
             pltpu.VMEM((DEPTH, PER, rows, dim), BF16),
+            pltpu.VMEM((half, q.shape[1], dim), BF16),
+            pltpu.VMEM((half, k_new.shape[1], dim), BF16),
+            pltpu.VMEM((half, v_new.shape[1], dim), BF16),
+            pltpu.VMEM((half // 8, steps, 8, (kvs * group + 1) * dim), F32),
             pltpu.VMEM((8 * q.shape[1], dim), F32),
             pltpu.VMEM((8 * steps * kvs, dim), F32),
             pltpu.SemaphoreType.DMA((DEPTH,)),
             pltpu.SemaphoreType.DMA((DEPTH,)),
             pltpu.SemaphoreType.DMA((DEPTH,)),
             pltpu.SemaphoreType.DMA((DEPTH,)),
+            pltpu.SemaphoreType.DMA((3,)),
+            pltpu.SemaphoreType.DMA((half // 8,)),
         ],
-        compiler_params=pltpu.CompilerParams(vmem_limit_bytes=48 * 2**20),
+        compiler_params=pltpu.CompilerParams(vmem_limit_bytes=VMEM_CAP),
         cost_estimate=pl.CostEstimate(flops=20_000_000_000, bytes_accessed=4 * batch * rows * dim,
                                       transcendentals=half * rows * q.shape[1]),
         name="attend_own" if handed else "attend_peer",
@@ -307,16 +332,17 @@
 
 
 CHUNK = 512
-RING = 6
+RING = 9
+WO_SLOTS = 3
 (C_OWN_O, C_X_O, C_OWN_E, C_X_E, C_HID_A, C_HID_B) = range(6)
 (W_CORE, W_Y, J_CORE, J_Y, J_OWN_X, J_OWN_C, J_FWD_C) = range(7)
 
 
-def tail_kernel(cfg, own_ref, xin_ref, x_hbm, wo_hbm, wfc_hbm, wproj_hbm, bo_ref, gain_ref, shift_ref, bfc_ref, bproj_ref,
+def tail_kernel(cfg, own_hbm, xin_hbm, x_hbm, wo_hbm, wfc_hbm, wproj_hbm, bo_ref, gain_ref, shift_ref, bfc_ref, bproj_ref,
                 y_ref,
-                sib_own, sib_x, sib_own_e, sib_x_e, a_buf, wo_buf, w_part, w_core, w_half, w_y, x_buf, x_mid, hid, hid_b,
+                my_own, my_x, my_own_e, my_x_e, sib_own, sib_x, sib_own_e, sib_x_e, a_buf, w_part, w_core, w_half, w_y, x_buf, x_mid, hid, hid_b,
                 ring, g_buf, p_part, p_core, p_half, p_y, y_all, bo_rows, bfc_rows, bproj_rows,
-                send_a, recv_a, send_j, recv_j, wo_sem, x_sem, ring_sem):
+                send_a, recv_a, send_j, recv_j, local_sem, wo_sem, x_sem, ring_sem):
     steps, batch, group, chunks, kvs = cfg
     half = batch // 2
     pair = steps // 2 * half
@@ -349,13 +375,28 @@
         pltpu.make_async_copy(wfc_hbm.at[:, pl.ds(0, CHUNK)], ring.at[slot], ring_sem.at[slot]).wait()
 
     wo_rows = pl.ds(pl.multiple_of(c * head_cols, LANES), head_cols)
-    wo_copy = pltpu.make_async_copy(wo_hbm.at[wo_rows, :], wo_buf, wo_sem)
-    wo_copy.start()
+    per_slot = ring.shape[1] // head_cols
+
+    def wo_place(j):
+        return ring.at[j // per_slot, pl.ds(pl.multiple_of(lax.rem(j, per_slot) * head_cols, LANES), head_cols), :]
+
+    def wo_copy(j):
+        return pltpu.make_async_copy(wo_hbm.at[wo_rows, chunk_cols(j)], wo_place(j), wo_sem.at[j])
+
+    def slot_of(item):
+        return lax.rem(item + WO_SLOTS, RING)
+
+    my_cols = pl.ds(pl.multiple_of(c * head_cols, LANES), head_cols)
+    stat_cols = slice(kvs * head_cols, kvs * head_cols + LANES)
+    locals_ = [pltpu.make_async_copy(src, dst, local_sem.at[n]) for n, (src, dst) in enumerate((
+        (own_hbm.at[:, :, stat_cols], my_own_e), (xin_hbm.at[:, :, stat_cols], my_x_e),
+        (own_hbm.at[:, :, my_cols], my_own), (xin_hbm.at[:, :, my_cols], my_x)))]
+    for copy in locals_:
+        copy.start()
+    for j in range(chunks):
+        wo_copy(jnp.int32(j)).start()
     x_copy = pltpu.make_async_copy(x_hbm.at[pl.ds(2 * c, 2), pl.ds(pl.multiple_of(x * half, 8), half), :], x_buf, x_sem)
     x_copy.start()
-    for k in range(RING):
-        load_item(jnp.int32(k), k)
-
     barrier = pltpu.get_barrier_semaphore()
     for who in (sib, xpeer, ypeer):
         pl.semaphore_signal(barrier, inc=1, device_id=who, device_id_type=MESH)
@@ -366,9 +407,8 @@
                                             device_id=who, device_id_type=MESH)
 
     sib_cols = pl.ds(pl.multiple_of((1 - c) * head_cols, LANES), head_cols)
-    stat_cols = slice(kvs * head_cols, kvs * head_cols + LANES)
-    swaps = [remote(own_ref.at[:, :, stat_cols], sib_own_e, C_OWN_E, sib), remote(xin_ref.at[:, :, stat_cols], sib_x_e, C_X_E, sib),
-             remote(own_ref.at[:, :, sib_cols], sib_own, C_OWN_O, sib), remote(xin_ref.at[:, :, sib_cols], sib_x, C_X_O, sib)]
+    swaps = [remote(own_hbm.at[:, :, stat_cols], sib_own_e, C_OWN_E, sib), remote(xin_hbm.at[:, :, stat_cols], sib_x_e, C_X_E, sib),
+             remote(own_hbm.at[:, :, sib_cols], sib_own, C_OWN_O, sib), remote(xin_hbm.at[:, :, sib_cols], sib_x, C_X_O, sib)]
     for copy in swaps:
         copy.start()
     bo_rows[...] = bo_ref[...].astype(F32)
@@ -382,9 +422,11 @@
         stat = flat(stat)
         return jnp.where(c == 0, stat, pltpu.roll(stat, LANES - group, 1))
 
+    for copy in locals_:
+        copy.wait()
     swaps[0].wait_recv()
     swaps[1].wait_recv()
-    logs = [my_lanes(own_ref[:, :, stat_cols]), my_lanes(sib_own_e[...]), my_lanes(xin_ref[:, :, stat_cols]), my_lanes(sib_x_e[...])]
+    logs = [my_lanes(my_own_e[...]), my_lanes(sib_own_e[...]), my_lanes(my_x_e[...]), my_lanes(sib_x_e[...])]
     top = functools.reduce(jnp.maximum, logs)
     shares = [jnp.exp2(e - top) for e in logs]
     inv = 1.0 / sum(shares)
@@ -392,10 +434,9 @@
     swaps[2].wait_recv()
     swaps[3].wait_recv()
     for i in range(group):
-        mine = pl.ds(pl.multiple_of(c * head_cols + i * LANES, LANES), LANES)
-        theirs = slice(i * LANES, (i + 1) * LANES)
-        parts = [own_ref[:, :, mine], sib_own[:, :, theirs], xin_ref[:, :, mine], sib_x[:, :, theirs]]
-        a_buf[:, theirs] = sum(w[:, i:i + 1] * flat(part) for w, part in zip(shares, parts)).astype(BF16)
+        cols = slice(i * LANES, (i + 1) * LANES)
+        parts = [part[:, :, cols] for part in (my_own, sib_own, my_x, sib_x)]
+        a_buf[:, cols] = sum(w[:, i:i + 1] * flat(part) for w, part in zip(shares, parts)).astype(BF16)
 
     def jcopy(src, dst, kind, j, who):
         return pltpu.make_async_remote_copy(src_ref=src, dst_ref=dst, send_sem=send_j.at[kind, j], recv_sem=recv_j.at[kind, j],
@@ -431,19 +472,24 @@
             body(j)
 
     def o_product(j):
-        w_part[j] = jnp.dot(a_buf[...], wo_buf[:, chunk_cols(j)], preferred_element_type=F32)
+        wo_copy(j).wait()
+        w_part[j] = jnp.dot(a_buf[...], wo_place(j)[...], preferred_element_type=F32)
         to_core(w_part, w_core, W_CORE, j).start()
 
     def o_core_sum(j):
         core_sum(w_part, w_core, w_half, w_y, W_CORE, W_Y, j)
 
-    wo_copy.wait()
-    x_copy.wait()
+    for k in range(RING - WO_SLOTS):
+        load_item(jnp.int32(k), slot_of(k))
 
     @pl.loop(0, chunks + 3)
     def _(it):
         stage(it, 0, o_product)
         stage(it, 3, o_core_sum)
+
+    for k in range(RING - WO_SLOTS, RING):
+        load_item(jnp.int32(k), slot_of(k))
+    x_copy.wait()
 
     @pl.loop(0, chunks)
     def _(j):
@@ -475,7 +521,7 @@
 
     @pl.loop(0, chunks)
     def _(j):
-        slot = lax.rem(j, RING)
+        slot = slot_of(j)
         wait_item(slot)
         pre = jnp.dot(hid_b[...], ring[slot], preferred_element_type=F32) + bias_of(bfc_rows, c * chunks + j)
         cube = pre * pre * pre
@@ -492,7 +538,7 @@
 
     def do_product(j):
         item = chunks + j
-        slot = lax.rem(item, RING)
+        slot = slot_of(item)
         wait_item(slot)
         p_part[j] = jnp.dot(g_buf[...], ring[slot], preferred_element_type=F32)
 
@@ -561,8 +607,11 @@
         pltpu.VMEM((steps, half, head_cols), F32),
         pltpu.VMEM((steps, half, LANES), F32),
         pltpu.VMEM((steps, half, LANES), F32),
+        pltpu.VMEM((steps, half, head_cols), F32),
+        pltpu.VMEM((steps, half, head_cols), F32),
+        pltpu.VMEM((steps, half, LANES), F32),
+        pltpu.VMEM((steps, half, LANES), F32),
         pltpu.VMEM((rows, head_cols), BF16),
-        pltpu.VMEM((head_cols, d_model), BF16),
         pltpu.VMEM((chunks, rows, CHUNK), F32),
         pltpu.VMEM((chunks, pair, CHUNK), F32),
         pltpu.VMEM((chunks, pair, CHUNK), F32),
@@ -585,14 +634,15 @@
         pltpu.SemaphoreType.DMA((6,)),
         pltpu.SemaphoreType.DMA((7, chunks)),
         pltpu.SemaphoreType.DMA((7, chunks)),
-        pltpu.SemaphoreType.DMA,
+        pltpu.SemaphoreType.DMA((4,)),
+        pltpu.SemaphoreType.DMA((chunks,)),
         pltpu.SemaphoreType.DMA,
         pltpu.SemaphoreType.DMA((RING,)),
     ]
     return pl.pallas_call(
         functools.partial(tail_kernel, cfg),
         out_shape=jax.ShapeDtypeStruct((steps, batch, d_model), BF16),
-        in_specs=[vm, vm, hbm, hbm, hbm, hbm] + [vm] * 5,
+        in_specs=[hbm] * 6 + [vm] * 5,
         out_specs=vm,
         scratch_shapes=scratch,
         compiler_params=pltpu.CompilerParams(collective_id=0, has_side_effects=True, vmem_limit_bytes=VMEM_CAP),

time: 143 us -> 134 us (0.937)
  local copies, waits for them, and re-layouts: 7.7 us -> 2.8 us
  Pallas kernels: 128 us -> 124 us
    pallas_call x1, Pallas kernels: 77.6 us -> 70.5 us  [tail(): pl.pallas_call(functools.partial(tail_kernel, cfg), out_shape=jax.ShapeDt...]
    unnamed x13 -> x1, local copies, waits for them, and re-layouts: 7.7 us -> 2.8 us
    pallas_call x2, Pallas kernels: 36.9 us -> 39.9 us  [attend(): pl.pallas_call(functools.partial(attend_kernel, (steps, kvs, group, slots...]
  transfers between devices with their start and end apart: 1 -> 1, of which waited for: 1 -> 1; matrix products, arithmetic and copies ran while one was open for 0% -> 0% of each run, Pallas kernels for 13% -> 15%
where the time goes in v4:
time: 134 us; the launch traced here: 133 us
  Pallas kernels  124 us (93%)
  starting transfers between devices  3.36 us (3%)
  local copies, waits for them, and re-layouts  2.8 us (2%)
  other arithmetic  1.77 us (1%)
    pallas_call x1, Pallas kernels, tail(): pl.pallas_call(functools.partial(tail_kernel, cfg), out_shape=jax.ShapeDt...  70.5 us
    pallas_call x2, Pallas kernels, attend(): pl.pallas_call(functools.partial(attend_kernel, (steps, kvs, group, slots...  39.9 us
    pallas_call x1, Pallas kernels, front(): pl.pallas_call(functools.partial(front_kernel, (steps, kvs, group)), out_...  13.5 us
    ppermute x1, starting transfers between devices, per_device(): lax.ppermute(for_peer, 'sq', [(d, d ^ 2) for d in range(sq_size)])  3.36 us
    unnamed x1, local copies, waits for them, and re-layouts  2.8 us
  transfers between devices with their start and end apart: 1, of which 1 were waited for; matrix products, arithmetic and copies ran while one was open for 0% of the time, Pallas kernels for 15%

profile of v4, /device:TPU:0, one launch (start us, length us, event | category | flops | bytes accessed | tf_op | source)
XLA Modules:
  0.0 133.3 jit_solution(12690085067416115990)
XLA Ops:
  0.6 0.7 add_convert_fusion
  1.3 1.1 multiply_sine_fusion
  2.4 13.5 %front.1 = (bf16[48,72,128]{2,1,0:T(8,128)(2,1)}, bf16[48,16,128]{2,1,0:T(8,128)(2,1)}, bf16[48,16,128]{2,1,0:T(8,128)(2,1)}) custom-call(bf16[4,48,4608]{2,1,0:T(8,128)(2,1)} %x_hbm.1, bf16[36,128]{1,0:T(8,128)(2,1)} %bitcast.21, bf16[36,128]{1,0:T(8,128)(2,1)} %bitcast.22, f32[4,48,64]{2,1,0:T(8,128)} %get-tuple-element.22.cos_ref, ...), custom_call_target="tpu_custom_call" | custom-call | flops 4982833152 | bytes 25952256 | tf_op jit(solution)/shard_map/front/pallas_call | solution.py:107
  15.9 19.9 %attend_peer.1 = (bf16[48,2048,128]{2,1,0:T(8,128)(2,1)}, bf16[48,2048,128]{2,1,0:T(8,128)(2,1)}, f32[4,24,2432]{2,1,0:T(8,128)}) custom-call(s32[48]{0:T(128)} %pos_ref.3, bf16[48,72,128]{2,1,0:T(8,128)(2,1)} %get-tuple-element.12.q_hbm, bf16[48,16,128]{2,1,0:T(8,128)(2,1)} %get-tuple-element.13.kn_hbm, bf16[48,16,128]{2,1,0:T(8,128)(2,1)} %get-tuple-element.14.vn_hbm, ...), custom_call_target="tpu_custom_call" | custom-call | flops 20000000000 | bytes 50331648 | tf_op jit(solution)/shard_map/attend_peer/pallas_call | solution.py:301
  35.9 3.4 %collective-permute-start = (f32[4,24,2432]{2,1,0:T(8,128)}, f32[4,24,2432]{2,1,0:T(8,128)}, u32[]{:S(2)}, u32[]{:S(2)}) collective-permute-start(f32[4,24,2432]{2,1,0:T(8,128)} %get-tuple-element.18), channel_id=1, source_target_pairs={{0,2},{1,3},{2,0},{3,1},{4,6},{5,7},{6,4},{7,5}} | collective-permute-start | bytes 2801672 | tf_op jit(solution)/shard_map/ppermute | solution.py:680
  39.2 19.9 %attend_own.1 = (bf16[48,2048,128]{2,1,0:T(8,128)(2,1)}, bf16[48,2048,128]{2,1,0:T(8,128)(2,1)}, f32[4,24,2432]{2,1,0:T(8,128)}) custom-call(s32[48]{0:T(128)} %pos_ref.3, bf16[48,72,128]{2,1,0:T(8,128)(2,1)} %get-tuple-element.12.q_hbm, bf16[48,16,128]{2,1,0:T(8,128)(2,1)} %get-tuple-element.13.kn_hbm, ...), custom_call_target="tpu_custom_call", output_to_operand_aliasing={{0}: (6, {}), {1}: (7, {})} | custom-call | flops 20000000000 | bytes 50331648 | tf_op jit(solution)/shard_map/attend_own/pallas_call | solution.py:301
  59.2 0.8 collective-permute-done.xin_hbm
  59.9 70.5 %tail.1 = bf16[4,48,4608]{2,1,0:T(8,128)(2,1)} custom-call(f32[4,24,2432]{2,1,0:T(8,128)} %get-tuple-element.17.own_hbm, f32[4,24,2432]{2,1,0:T(8,128)} %collective-permute-done.xin_hbm, bf16[4,48,4608]{2,1,0:T(8,128)(2,1)} %x_hbm.1, bf16[2304,4608]{1,0:T(8,128)(2,1)} %wo_hbm.1, bf16[4608,9216]{1,0:T(8,128)(2,1)} %wfc_hbm.1, bf16[9216,4608]{1,0:T(8,128)(2,1)} %wproj_hbm.1, ...), custom_call_target="tpu_custom_call" | custom-call | flops 9172942848 | bytes 100000000 | tf_op jit(solution)/shard_map/tail/pallas_call | solution.py:642
  130.5 2.8 %copy.28 = bf16[4,48,4608]{2,1,0:T(8,128)(2,1)} copy(bf16[4,48,4608]{2,1,0:T(8,128)(2,1)} %tail.1) | data formatting | bytes 3538944
  (1 shorter events, 0.0 us)
Async XLA Ops:
  35.9 24.1 %collective-permute-start = (f32[4,24,2432]{2,1,0:T(8,128)}, f32[4,24,2432]{2,1,0:T(8,128)}, u32[]{:S(2)}, u32[]{:S(2)}) collective-permute-start(f32[4,24,2432]{2,1,0:T(8,128)} %get-tuple-element.18), channel_id=1, source_target_pairs={{0,2},{1,3},{2,0},{3,1},{4,6},{5,7},{6,4},{7,5}} | collective-permute-start | bytes 2801672 | tf_op jit(solution)/shard_map/ppermute | solution.py:680

commit v5 on v4

--- a/solution.py
+++ b/solution.py
@@ -19,32 +19,52 @@
 LANES = 128
 
 
-def rope_tables(positions, head_dim):
-    half_dim = head_dim // 2
-    inv_freq = jnp.power(F32(ROPE_BASE), -2.0 * jnp.arange(half_dim, dtype=F32) / head_dim)
-    angle = positions.astype(F32)[..., None] * inv_freq
-    return jnp.cos(angle), jnp.sin(angle)
-
-
 COLS = 256
 
-def front_kernel(cfg, x_ref, gain_ref, shift_ref, cos_ref, sin_ref, bq_ref, bk_ref, bv_ref, wq_hbm, wk_hbm, wv_hbm,
-                 q_out, kn_out, vn_out, hid, wq_buf, wk_buf, wv_buf, q_rows, kv_rows, bias_q, sem):
+def front_kernel(cfg, pos_ref, x_hbm, freq_ref, gain_ref, shift_ref, bq_ref, bk_ref, bv_ref, wq_hbm, wk_hbm, wv_hbm,
+                 q_out, kn_out, vn_out, x_buf, hid, w_buf, mine, theirs, pos_rows, q_rows, kn_rows, vn_rows, bias_q,
+                 sem, x_sem, send, recv):
     steps, kvs, group = cfg
-    batch, d_model = x_ref.shape[1], x_ref.shape[2]
-    n_q = wq_hbm.shape[1] // COLS
+    batch, d_model = x_buf.shape[1], x_buf.shape[2]
+    head_cols = group * LANES
     per_row = group * kvs * steps
-    copies = [pltpu.make_async_copy(wk_hbm, wk_buf, sem.at[n_q]), pltpu.make_async_copy(wv_hbm, wv_buf, sem.at[n_q + 1])]
-    for copy in copies:
+    sq = lax.axis_index("sq")
+    c = sq % 2
+    sib = {"sq": (sq // 2) * 2 + 1 - c}
+
+    x_copies = [pltpu.make_async_copy(x_hbm.at[s], x_buf.at[s], x_sem.at[s]) for s in range(steps)]
+    for copy in x_copies:
         copy.start()
-    for n in range(n_q):
-        pltpu.make_async_copy(wq_hbm.at[:, n * COLS:(n + 1) * COLS], wq_buf.at[n], sem.at[n]).start()
+    head_at = pl.multiple_of(c * LANES, LANES)
+    pieces = []
+    for at in range(0, head_cols, COLS):
+        width = min(COLS, head_cols - at)
+        pieces.append((wq_hbm.at[:, pl.ds(pl.multiple_of(c * head_cols + at, LANES), width)], at, width))
+    pieces.append((wk_hbm.at[:, pl.ds(head_at, LANES)], head_cols, LANES))
+    pieces.append((wv_hbm.at[:, pl.ds(head_at, LANES)], head_cols + LANES, LANES))
+    w_copies = [pltpu.make_async_copy(src, w_buf.at[:, at:at + width], sem.at[n]) for n, (src, at, width) in enumerate(pieces)]
+    for copy in w_copies:
+        copy.start()
+
+    barrier = pltpu.get_barrier_semaphore()
+    pl.semaphore_signal(barrier, inc=1, device_id=sib, device_id_type=pl.DeviceIdType.MESH)
+    pl.semaphore_wait(barrier, 1)
+
+    for b in range(batch):
+        pos_rows[b:b + 1, :] = jnp.full((1, LANES), pos_ref[b], jnp.int32).astype(F32)
+    half = LANES // 2
+    where = pos_rows[:, :half]
+    angle = jnp.concatenate([where + float(s) for s in range(steps)], axis=0) * freq_ref[...]
+    cos, sin = jnp.cos(angle), jnp.sin(angle)
+    cos_full = jnp.concatenate([cos, cos], axis=-1)
+    sin_full = jnp.concatenate([-sin, sin], axis=-1)
 
     bias_q[...] = bq_ref[...].astype(F32)
     gain = gain_ref[...].astype(F32)
     shift = shift_ref[...].astype(F32)
     for s in range(steps):
-        wide = x_ref[s].astype(F32)
+        x_copies[s].wait()
+        wide = x_buf[s].astype(F32)
         mean = jnp.mean(wide, axis=-1, keepdims=True)
         cent = wide - mean
         rstd = lax.rsqrt(jnp.mean(cent * cent, axis=-1, keepdims=True) + LN_EPS)
@@ -52,55 +72,64 @@
             cols = slice(n * LANES, (n + 1) * LANES)
             hid[s * batch:(s + 1) * batch, cols] = (cent[:, cols] * rstd * gain[n:n + 1, :] + shift[n:n + 1, :]).astype(BF16)
 
-    cos = cos_ref[...].reshape(steps * batch, LANES // 2)
-    sin = sin_ref[...].reshape(steps * batch, LANES // 2)
-    cos_full = jnp.concatenate([cos, cos], axis=-1)
-    sin_full = jnp.concatenate([-sin, sin], axis=-1)
-
     def rotate(vec):
-        return (vec * cos_full + pltpu.roll(vec, LANES // 2, 1) * sin_full).astype(BF16).astype(F32)
-
-    def rounded(weight, bias):
-        return (jnp.dot(hid[...], weight, preferred_element_type=F32) + bias).astype(BF16).astype(F32)
-
-    for rope, copy, buf, b_ref, out in ((True, copies[0], wk_buf, bk_ref, kn_out), (False, copies[1], wv_buf, bv_ref, vn_out)):
-        copy.wait()
-        kv_rows[...] = jnp.zeros_like(kv_rows)
-        bias = b_ref[...].astype(F32)
-        both = rounded(buf[...], jnp.concatenate([bias[h:h + 1] for h in range(kvs)], axis=-1))
-        for h in range(kvs):
-            vec = both[:, h * LANES:(h + 1) * LANES]
-            if rope:
-                vec = rotate(vec)
-            for s in range(steps):
-                kv_rows[pl.ds(s * kvs + h, batch, stride=16), :] = vec[s * batch:(s + 1) * batch]
-        out[...] = kv_rows[...].reshape(out.shape).astype(BF16)
-
-    heads = COLS // LANES
-
-    @pl.loop(0, n_q)
-    def _(n):
-        pltpu.make_async_copy(wq_hbm.at[:, 0:COLS], wq_buf.at[n], sem.at[n]).wait()
-        bias = jnp.concatenate([bias_q[pl.ds(n * heads + e, 1), :] for e in range(heads)], axis=-1)
-        both = rounded(wq_buf[n], bias)
-        for e in range(heads):
-            vec = rotate(both[:, e * LANES:(e + 1) * LANES])
-            head = n * heads + e
-            row = lax.rem(head, group) * (kvs * steps) + (head // group) * steps
-            for s in range(steps):
-                q_rows[pl.ds(row + s, batch, stride=per_row), :] = vec[s * batch:(s + 1) * batch]
+        return (vec * cos_full + pltpu.roll(vec, half, 1) * sin_full).astype(BF16).astype(F32)
+
+    def swap(n):
+        return pltpu.make_async_remote_copy(src_ref=mine.at[n], dst_ref=theirs.at[n], send_sem=send.at[n], recv_sem=recv.at[n],
+                                            device_id=sib, device_id_type=pl.DeviceIdType.MESH)
+
+    def place(n, core, block):
+        for s in range(steps):
+            rows = block[s * batch:(s + 1) * batch, :]
+            if n < group:
+                q_rows[pl.ds(n * kvs * steps + core * steps + s, batch, stride=per_row), :] = rows
+            elif n == group:
+                kn_rows[pl.ds(s * kvs + core, batch, stride=16), :] = rows
+            else:
+                vn_rows[pl.ds(s * kvs + core, batch, stride=16), :] = rows
+
+    kn_rows[...] = jnp.zeros_like(kn_rows)
+    vn_rows[...] = jnp.zeros_like(vn_rows)
+    kv_bias = [jnp.where(c == 0, ref[0:1, :].astype(F32), ref[1:2, :].astype(F32)) for ref in (bk_ref, bv_ref)]
+    total = group + 2
+    per = COLS // LANES
+    done = 0
+    for first in range(0, total, per):
+        count = min(per, total - first)
+        upto = (first + count) * LANES
+        while done < len(pieces) and pieces[done][1] < upto:
+            w_copies[done].wait()
+            done += 1
+        block = jnp.dot(hid[...], w_buf[:, first * LANES:upto], preferred_element_type=F32)
+        for n in range(first, first + count):
+            bias = bias_q[pl.ds(c * group + n, 1), :] if n < group else kv_bias[n - group]
+            vec = (block[:, (n - first) * LANES:(n - first + 1) * LANES] + bias).astype(BF16).astype(F32)
+            mine[n] = rotate(vec) if n <= group else vec
+            swap(n).start()
+            place(n, c, mine.at[n])
+    for n in range(total):
+        swap(n).wait_recv()
+        place(n, 1 - c, theirs.at[n])
+
+    kn_out[...] = kn_rows[...].reshape(kn_out.shape).astype(BF16)
+    vn_out[...] = vn_rows[...].reshape(vn_out.shape).astype(BF16)
 
     @pl.loop(0, batch)
     def _(b):
         q_out[b] = q_rows[pl.ds(pl.multiple_of(b * per_row, 8), per_row), :].astype(BF16)
 
-
-def front(x_steps, gain, shift, cos_t, sin_t, b_q, b_k, b_v, w_q, w_k, w_v, kvs):
+    for n in range(total):
+        swap(n).wait_send()
+
+
+def front(positions, x_steps, gain, shift, b_q, b_k, b_v, w_q, w_k, w_v, kvs):
     steps, batch, d_model = x_steps.shape
     heads = w_q.shape[1] // LANES
     group = heads // kvs
     rows = group * kvs * steps
-    n_q = w_q.shape[1] // COLS
+    assert kvs == 2
+    inv_freq = jnp.power(F32(ROPE_BASE), -2.0 * jnp.arange(LANES // 2, dtype=F32) / LANES).reshape(1, -1)
     vm = pl.BlockSpec(memory_space=pltpu.VMEM)
     hbm = pl.BlockSpec(memory_space=pl.ANY)
     tiles = lambda vec: vec.reshape(-1, LANES)
@@ -111,23 +140,29 @@
             jax.ShapeDtypeStruct((batch, 16, LANES), BF16),
             jax.ShapeDtypeStruct((batch, 16, LANES), BF16),
         ],
-        in_specs=[vm] * 8 + [hbm] * 3,
+        in_specs=[pl.BlockSpec(memory_space=pltpu.SMEM), hbm] + [vm] * 6 + [hbm] * 3,
         out_specs=[vm] * 3,
         scratch_shapes=[
+            pltpu.VMEM((steps, batch, d_model), BF16),
             pltpu.VMEM((steps * batch, d_model), BF16),
-            pltpu.VMEM((n_q, d_model, COLS), BF16),
-            pltpu.VMEM(w_k.shape, BF16),
-            pltpu.VMEM(w_v.shape, BF16),
+            pltpu.VMEM((d_model, (group + 2) * LANES), BF16),
+            pltpu.VMEM((group + 2, steps * batch, LANES), F32),
+            pltpu.VMEM((group + 2, steps * batch, LANES), F32),
+            pltpu.VMEM((batch, LANES), F32),
             pltpu.VMEM((batch * rows, LANES), F32),
             pltpu.VMEM((batch * 16, LANES), F32),
+            pltpu.VMEM((batch * 16, LANES), F32),
             pltpu.VMEM((heads, LANES), F32),
-            pltpu.SemaphoreType.DMA((n_q + 2,)),
+            pltpu.SemaphoreType.DMA((group + 2,)),
+            pltpu.SemaphoreType.DMA((steps,)),
+            pltpu.SemaphoreType.DMA((group + 2,)),
+            pltpu.SemaphoreType.DMA((group + 2,)),
         ],
-        compiler_params=pltpu.CompilerParams(vmem_limit_bytes=56 * 2**20),
-        cost_estimate=pl.CostEstimate(flops=2 * steps * batch * d_model * (w_q.shape[1] + 2 * w_k.shape[1]),
-                                      bytes_accessed=2 * d_model * (w_q.shape[1] + 2 * w_k.shape[1]), transcendentals=0),
+        compiler_params=pltpu.CompilerParams(collective_id=1, has_side_effects=True, vmem_limit_bytes=VMEM_CAP),
+        cost_estimate=pl.CostEstimate(flops=steps * batch * d_model * (w_q.shape[1] + 2 * w_k.shape[1]),
+                                      bytes_accessed=d_model * (w_q.shape[1] + 2 * w_k.shape[1]), transcendentals=0),
         name="front",
-    )(x_steps, tiles(gain), tiles(shift), cos_t, sin_t, tiles(b_q), tiles(b_k), tiles(b_v), w_q, w_k, w_v)
+    )(positions, x_steps, inv_freq, tiles(gain), tiles(shift), tiles(b_q), tiles(b_k), tiles(b_v), w_q, w_k, w_v)
 
 
 PER = 2
@@ -167,15 +202,12 @@
              for n, (src, dst) in enumerate(((q_hbm, q_ref), (kn_hbm, kn_ref), (vn_hbm, vn_ref)))]
     for copy in small:
         copy.start()
-    for i in range(AHEAD):
+    for i in range(2):
         for copy in fetch(jnp.int32(i)):
             copy.start()
 
     def put_tile(t):
         return pltpu.make_async_copy(o_tile.at[t], o_hbm.at[:, pl.ds(pl.multiple_of(t * 8, 8), 8), :], o_up.at[t])
-
-    for copy in small:
-        copy.wait()
 
     sub = lax.broadcasted_iota(jnp.int32, (tile, rows), 0)
     lane = lax.broadcasted_iota(jnp.int32, (tile, rows), 1)
@@ -215,6 +247,12 @@
             for copy in put(i - AHEAD):
                 copy.wait()
 
+        @pl.when(i == 0)
+        def _():
+            for later in range(2, AHEAD):
+                for copy in fetch(jnp.int32(later)):
+                    copy.start()
+
         @pl.when(i + AHEAD < n_blocks)
         def _():
             for copy in fetch(i + AHEAD):
@@ -230,6 +268,11 @@
             put_tile(i // blocks_per_tile - 1).start()
 
         k_copy, v_copy = fetch(i)
+        @pl.when(i == 0)
+        def _():
+            for copy in small:
+                copy.wait()
+
         k_copy.wait()
         v_copy.wait()
         state = []
@@ -332,6 +375,7 @@
 
 
 CHUNK = 512
+PIECE = 256
 RING = 9
 WO_SLOTS = 3
 (C_OWN_O, C_X_O, C_OWN_E, C_X_E, C_HID_A, C_HID_B) = range(6)
@@ -348,7 +392,8 @@
     pair = steps // 2 * half
     head_cols = group * LANES
     ff_own = wfc_hbm.shape[1] // 2
-    per_chunk = CHUNK // LANES
+    pieces = chunks * CHUNK // PIECE
+    per = CHUNK // PIECE
     y = lax.axis_index("tp")
     sq = lax.axis_index("sq")
     x, c = sq // 2, sq % 2
@@ -456,8 +501,18 @@
         total[j] = part[j, pair_rows(c), :] + inbox[j]
         to_y(total, inbox_y, kind_y, j).start()
 
-    def bias_of(rows, j):
-        return jnp.concatenate([rows[pl.ds(j * per_chunk + e, 1), :] for e in range(per_chunk)], axis=-1)
+    def bias_of(rows, j, width):
+        n = width // LANES
+        return jnp.concatenate([rows[pl.ds(j * n + e, 1), :] for e in range(n)], axis=-1)
+
+    def piece_cols(u):
+        return pl.ds(pl.multiple_of(u * PIECE, PIECE), PIECE)
+
+    def send_product(product, part, inbox, kind, j):
+        for e in range(per):
+            part[j * per + e] = product[:, e * PIECE:(e + 1) * PIECE]
+        for e in range(per):
+            to_core(part, inbox, kind, j * per + e).start()
 
     def y_sum(total, inbox):
         low = jnp.where(y == 0, total, inbox)
@@ -465,16 +520,21 @@
         return low + high
 
     def stage(it, lag, body):
-        j = it - lag
-
-        @pl.when((j >= 0) & (j < chunks))
-        def _():
-            body(j)
+        u = it - lag
+
+        @pl.when((u >= 0) & (u < pieces))
+        def _():
+            body(u)
+
+    def product_stage(it, body):
+        @pl.when((it < pieces) & (lax.rem(it, per) == 0))
+        def _():
+            body(it // per)
 
     def o_product(j):
         wo_copy(j).wait()
-        w_part[j] = jnp.dot(a_buf[...], wo_place(j)[...], preferred_element_type=F32)
-        to_core(w_part, w_core, W_CORE, j).start()
+        product = jnp.dot(a_buf[...], wo_place(j)[...], preferred_element_type=F32)
+        send_product(product, w_part, w_core, W_CORE, j)
 
     def o_core_sum(j):
         core_sum(w_part, w_core, w_half, w_y, W_CORE, W_Y, j)
@@ -482,21 +542,21 @@
     for k in range(RING - WO_SLOTS):
         load_item(jnp.int32(k), slot_of(k))
 
-    @pl.loop(0, chunks + 3)
+    @pl.loop(0, pieces + 6)
     def _(it):
-        stage(it, 0, o_product)
-        stage(it, 3, o_core_sum)
+        product_stage(it, o_product)
+        stage(it, 6, o_core_sum)
 
     for k in range(RING - WO_SLOTS, RING):
         load_item(jnp.int32(k), slot_of(k))
     x_copy.wait()
 
-    @pl.loop(0, chunks)
-    def _(j):
-        cols = chunk_cols(j)
-        to_y(w_half, w_y, W_Y, j).wait_recv()
-        x_in = x_buf[:, :, cols].astype(F32).reshape(pair, CHUNK)
-        x_mid[:, cols] = (x_in + y_sum(w_half[j], w_y[j]) + bias_of(bo_rows, j)).astype(BF16).astype(F32)
+    @pl.loop(0, pieces)
+    def _(u):
+        cols = piece_cols(u)
+        to_y(w_half, w_y, W_Y, u).wait_recv()
+        x_in = x_buf[:, :, cols].astype(F32).reshape(pair, PIECE)
+        x_mid[:, cols] = (x_in + y_sum(w_half[u], w_y[u]) + bias_of(bo_rows, u, PIECE)).astype(BF16).astype(F32)
 
     gain = gain_ref[...].astype(F32)
     shift = shift_ref[...].astype(F32)
@@ -523,7 +583,7 @@
     def _(j):
         slot = slot_of(j)
         wait_item(slot)
-        pre = jnp.dot(hid_b[...], ring[slot], preferred_element_type=F32) + bias_of(bfc_rows, c * chunks + j)
+        pre = jnp.dot(hid_b[...], ring[slot], preferred_element_type=F32) + bias_of(bfc_rows, c * chunks + j, CHUNK)
         cube = pre * pre * pre
         act = 0.5 * pre * (1.0 + jnp.tanh(math.sqrt(2.0 / math.pi) * (pre + 0.044715 * cube)))
         g_buf[:, chunk_cols(j)] = act.astype(BF16)
@@ -540,21 +600,20 @@
         item = chunks + j
         slot = slot_of(item)
         wait_item(slot)
-        p_part[j] = jnp.dot(g_buf[...], ring[slot], preferred_element_type=F32)
+        product = jnp.dot(g_buf[...], ring[slot], preferred_element_type=F32)
+        send_product(product, p_part, p_core, J_CORE, j)
 
         @pl.when(item + RING < 2 * chunks)
         def _():
             load_item(item + RING, slot)
-
-        to_core(p_part, p_core, J_CORE, j).start()
 
     def do_core_sum(j):
         core_sum(p_part, p_core, p_half, p_y, J_CORE, J_Y, j)
 
     def do_y_sum(j):
         to_y(p_half, p_y, J_Y, j).wait_recv()
-        full = x_mid[:, chunk_cols(j)] + y_sum(p_half[j], p_y[j]) + bias_of(bproj_rows, j)
-        y_all[j, pl.ds(2 * c, 2), pl.ds(pl.multiple_of(x * half, 8), half), :] = full.astype(BF16).astype(F32).reshape(2, half, CHUNK)
+        full = x_mid[:, piece_cols(j)] + y_sum(p_half[j], p_y[j]) + bias_of(bproj_rows, j, PIECE)
+        y_all[j, pl.ds(2 * c, 2), pl.ds(pl.multiple_of(x * half, 8), half), :] = full.astype(BF16).astype(F32).reshape(2, half, PIECE)
         spread(J_OWN_X, j).start()
         spread(J_OWN_C, j).start()
 
@@ -565,20 +624,20 @@
     def do_store(j):
         spread(J_OWN_C, j).wait_recv()
         spread(J_FWD_C, j).wait_recv()
-        y_ref[:, :, chunk_cols(j)] = y_all[j].astype(BF16)
-
-    @pl.loop(0, chunks + 7)
+        y_ref[:, :, piece_cols(j)] = y_all[j].astype(BF16)
+
+    @pl.loop(0, pieces + 13)
     def _(it):
-        stage(it, 0, do_product)
-        stage(it, 1, do_core_sum)
-        stage(it, 3, do_y_sum)
-        stage(it, 5, do_forward)
-        stage(it, 7, do_store)
+        product_stage(it, do_product)
+        stage(it, 2, do_core_sum)
+        stage(it, 7, do_y_sum)
+        stage(it, 11, do_forward)
+        stage(it, 13, do_store)
 
     for copy in swaps + hid_copies:
         copy.wait_send()
 
-    @pl.loop(0, chunks)
+    @pl.loop(0, pieces)
     def _(j):
         to_core(w_part, w_core, W_CORE, j).wait_send()
         to_y(w_half, w_y, W_Y, j).wait_send()
@@ -595,6 +654,7 @@
     pair = rows // 2
     d_model = w_o.shape[1]
     chunks = d_model // CHUNK
+    pieces = d_model // PIECE
     ff_own = w_fc.shape[1] // 2
     assert ff_own == d_model and steps == 4 and kvs == 2
     head_cols = group * LANES
@@ -612,28 +672,28 @@
         pltpu.VMEM((steps, half, LANES), F32),
         pltpu.VMEM((steps, half, LANES), F32),
         pltpu.VMEM((rows, head_cols), BF16),
-        pltpu.VMEM((chunks, rows, CHUNK), F32),
-        pltpu.VMEM((chunks, pair, CHUNK), F32),
-        pltpu.VMEM((chunks, pair, CHUNK), F32),
-        pltpu.VMEM((chunks, pair, CHUNK), F32),
+        pltpu.VMEM((pieces, rows, PIECE), F32),
+        pltpu.VMEM((pieces, pair, PIECE), F32),
+        pltpu.VMEM((pieces, pair, PIECE), F32),
+        pltpu.VMEM((pieces, pair, PIECE), F32),
         pltpu.VMEM((2, half, d_model), BF16),
         pltpu.VMEM((pair, d_model), F32),
         pltpu.VMEM((rows, d_model), F32),
         pltpu.VMEM((rows, d_model), BF16),
         pltpu.VMEM((RING, d_model, CHUNK), BF16),
         pltpu.VMEM((rows, ff_own), BF16),
-        pltpu.VMEM((chunks, rows, CHUNK), F32),
-        pltpu.VMEM((chunks, pair, CHUNK), F32),
-        pltpu.VMEM((chunks, pair, CHUNK), F32),
-        pltpu.VMEM((chunks, pair, CHUNK), F32),
-        pltpu.VMEM((chunks, steps, batch, CHUNK), F32),
+        pltpu.VMEM((pieces, rows, PIECE), F32),
+        pltpu.VMEM((pieces, pair, PIECE), F32),
+        pltpu.VMEM((pieces, pair, PIECE), F32),
+        pltpu.VMEM((pieces, pair, PIECE), F32),
+        pltpu.VMEM((pieces, steps, batch, PIECE), F32),
         pltpu.VMEM((d_model // LANES, LANES), F32),
         pltpu.VMEM((2 * ff_own // LANES, LANES), F32),
         pltpu.VMEM((d_model // LANES, LANES), F32),
         pltpu.SemaphoreType.DMA((6,)),
         pltpu.SemaphoreType.DMA((6,)),
-        pltpu.SemaphoreType.DMA((7, chunks)),
-        pltpu.SemaphoreType.DMA((7, chunks)),
+        pltpu.SemaphoreType.DMA((7, pieces)),
+        pltpu.SemaphoreType.DMA((7, pieces)),
         pltpu.SemaphoreType.DMA((4,)),
         pltpu.SemaphoreType.DMA((chunks,)),
         pltpu.SemaphoreType.DMA,
@@ -670,9 +730,7 @@
         slots_local, kvs, dim = key_buf.shape[1], key_buf.shape[2], key_buf.shape[3]
         slots = slots_local * sq_size
         group = w_q.shape[1] // (kvs * dim)
-        cur_pos = positions[None, :] + jnp.arange(steps, dtype=jnp.int32)[:, None]
-        cos_t, sin_t = rope_tables(cur_pos, dim)
-        q_rows, k_new, v_new = front(x_steps, ln1_gain, ln1_bias, cos_t, sin_t, b_q, b_k, b_v, w_q, w_k, w_v, kvs)
+        q_rows, k_new, v_new = front(positions, x_steps, ln1_gain, ln1_bias, b_q, b_k, b_v, w_q, w_k, w_v, kvs)
         k_rows = key_buf.reshape(batch, slots_local * kvs, dim)
         v_rows = val_buf.reshape(batch, slots_local * kvs, dim)
         caches = (positions, q_rows, k_new, v_new, k_rows, v_rows, steps, kvs, group, slots)

time: 134 us -> 135 us (level)
  Pallas kernels: 124 us -> 126 us
  waiting for transfers between devices: 0.76 us -> 2.29 us
    pallas_call x1, Pallas kernels: 13.5 us -> 17.1 us  [front(): pl.pallas_call(functools.partial(front_kernel, (steps, kvs, group)), out_...]
    pallas_call x2, Pallas kernels: 39.9 us -> 38.3 us  [attend(): pl.pallas_call(functools.partial(attend_kernel, (steps, kvs, group, slots...]
    ppermute x1, waiting for transfers between devices: 0.76 us -> 2.29 us  [per_device(): lax.ppermute(for_peer, 'sq', [(d, d ^ 2) for d in range(sq_size)])]
  transfers between devices with their start and end apart: 1 -> 1, of which waited for: 1 -> 1; matrix products, arithmetic and copies ran while one was open for 0% -> 0% of each run, Pallas kernels for 15% -> 14%
where the time goes in v5:
time: 135 us; the launch traced here: 134 us
  Pallas kernels  126 us (93%)
  local copies, waits for them, and re-layouts  2.8 us (2%)
  starting transfers between devices  2.33 us (2%)
  waiting for transfers between devices  2.29 us (2%)
    pallas_call x1, Pallas kernels, tail(): pl.pallas_call(functools.partial(tail_kernel, cfg), out_shape=jax.ShapeDt...  70.5 us
    pallas_call x2, Pallas kernels, attend(): pl.pallas_call(functools.partial(attend_kernel, (steps, kvs, group, slots...  38.3 us
    pallas_call x1, Pallas kernels, front(): pl.pallas_call(functools.partial(front_kernel, (steps, kvs, group)), out_...  17.1 us
    unnamed x1, local copies, waits for them, and re-layouts  2.8 us
  transfers between devices with their start and end apart: 1, of which 1 were waited for; matrix products, arithmetic and copies ran while one was open for 0% of the time, Pallas kernels for 14%

profile of v5, /device:TPU:0, one launch (start us, length us, event | category | flops | bytes accessed | tf_op | source)
XLA Modules:
  0.0 134.4 jit_solution(16488119488893502208)
XLA Ops:
  0.6 0.5 multiply_power_fusion.freq_ref
  1.2 17.1 %front.1 = (bf16[48,72,128]{2,1,0:T(8,128)(2,1)}, bf16[48,16,128]{2,1,0:T(8,128)(2,1)}, bf16[48,16,128]{2,1,0:T(8,128)(2,1)}) custom-call(s32[48]{0:T(128)} %pos_ref.5, bf16[4,48,4608]{2,1,0:T(8,128)(2,1)} %x_hbm.3, f32[1,64]{1,0:T(1,128)} %multiply_power_fusion.freq_ref, bf16[36,128]{1,0:T(8,128)(2,1)} %bitcast.21, bf16[36,128]{1,0:T(8,128)(2,1)} %bitcast.22, ...), custom_call_target="tpu_custom_call" | custom-call | flops 2491416576 | bytes 12976128 | tf_op jit(solution)/shard_map/front/pallas_call | solution.py:136
  18.2 19.2 %attend_peer.1 = (bf16[48,2048,128]{2,1,0:T(8,128)(2,1)}, bf16[48,2048,128]{2,1,0:T(8,128)(2,1)}, f32[4,24,2432]{2,1,0:T(8,128)}) custom-call(s32[48]{0:T(128)} %pos_ref.5, bf16[48,72,128]{2,1,0:T(8,128)(2,1)} %get-tuple-element.12.q_hbm, bf16[48,16,128]{2,1,0:T(8,128)(2,1)} %get-tuple-element.13.kn_hbm, bf16[48,16,128]{2,1,0:T(8,128)(2,1)} %get-tuple-element.14.vn_hbm, ...), custom_call_target="tpu_custom_call" | custom-call | flops 20000000000 | bytes 50331648 | tf_op jit(solution)/shard_map/attend_peer/pallas_call | solution.py:344
  37.4 2.3 %collective-permute-start = (f32[4,24,2432]{2,1,0:T(8,128)}, f32[4,24,2432]{2,1,0:T(8,128)}, u32[]{:S(2)}, u32[]{:S(2)}) collective-permute-start(f32[4,24,2432]{2,1,0:T(8,128)} %get-tuple-element.18), channel_id=1, source_target_pairs={{0,2},{1,3},{2,0},{3,1},{4,6},{5,7},{6,4},{7,5}} | collective-permute-start | bytes 2801672 | tf_op jit(solution)/shard_map/ppermute | solution.py:738
  39.7 19.1 %attend_own.1 = (bf16[48,2048,128]{2,1,0:T(8,128)(2,1)}, bf16[48,2048,128]{2,1,0:T(8,128)(2,1)}, f32[4,24,2432]{2,1,0:T(8,128)}) custom-call(s32[48]{0:T(128)} %pos_ref.5, bf16[48,72,128]{2,1,0:T(8,128)(2,1)} %get-tuple-element.12.q_hbm, bf16[48,16,128]{2,1,0:T(8,128)(2,1)} %get-tuple-element.13.kn_hbm, ...), custom_call_target="tpu_custom_call", output_to_operand_aliasing={{0}: (6, {}), {1}: (7, {})} | custom-call | flops 20000000000 | bytes 50331648 | tf_op jit(solution)/shard_map/attend_own/pallas_call | solution.py:344
  58.9 2.3 %collective-permute-done.xin_hbm = f32[4,24,2432]{2,1,0:T(8,128)} collective-permute-done((f32[4,24,2432]{2,1,0:T(8,128)}, f32[4,24,2432]{2,1,0:T(8,128)}, u32[]{:S(2)}, u32[]{:S(2)}) %collective-permute-start) | collective-permute-done | bytes 933920 | tf_op jit(solution)/shard_map/ppermute | solution.py:738
  61.2 70.5 %tail.1 = bf16[4,48,4608]{2,1,0:T(8,128)(2,1)} custom-call(f32[4,24,2432]{2,1,0:T(8,128)} %get-tuple-element.17.own_hbm, f32[4,24,2432]{2,1,0:T(8,128)} %collective-permute-done.xin_hbm, bf16[4,48,4608]{2,1,0:T(8,128)(2,1)} %x_hbm.3, bf16[2304,4608]{1,0:T(8,128)(2,1)} %wo_hbm.1, bf16[4608,9216]{1,0:T(8,128)(2,1)} %wfc_hbm.1, bf16[9216,4608]{1,0:T(8,128)(2,1)} %wproj_hbm.1, ...), custom_call_target="tpu_custom_call" | custom-call | flops 9172942848 | bytes 100000000 | tf_op jit(solution)/shard_map/tail/pallas_call | solution.py:702
  131.6 2.8 %copy.28 = bf16[4,48,4608]{2,1,0:T(8,128)(2,1)} copy(bf16[4,48,4608]{2,1,0:T(8,128)(2,1)} %tail.1) | data formatting | bytes 3538944
Async XLA Ops:
  37.4 23.8 %collective-permute-start = (f32[4,24,2432]{2,1,0:T(8,128)}, f32[4,24,2432]{2,1,0:T(8,128)}, u32[]{:S(2)}, u32[]{:S(2)}) collective-permute-start(f32[4,24,2432]{2,1,0:T(8,128)} %get-tuple-element.18), channel_id=1, source_target_pairs={{0,2},{1,3},{2,0},{3,1},{4,6},{5,7},{6,4},{7,5}} | collective-permute-start | bytes 2801672 | tf_op jit(solution)/shard_map/ppermute | solution.py:738

commit v6 on v5

--- a/solution.py
+++ b/solution.py
@@ -14,15 +14,16 @@
 NEG_HALF = -1e29
 LOG2E = 1.4426950408889634
 VMEM_CAP = 67_043_328
+TAIL_VMEM = 64_900_000
 F32 = jnp.float32
 BF16 = jnp.bfloat16
 LANES = 128
 
 
-COLS = 256
+COLS = 384
 
 def front_kernel(cfg, pos_ref, x_hbm, freq_ref, gain_ref, shift_ref, bq_ref, bk_ref, bv_ref, wq_hbm, wk_hbm, wv_hbm,
-                 q_out, kn_out, vn_out, x_buf, hid, w_buf, mine, theirs, pos_rows, q_rows, kn_rows, vn_rows, bias_q,
+                 q_out, kn_out, vn_out, x_buf, hid, wq_buf, wkv_buf, mine, theirs, pos_rows, q_rows, kn_rows, vn_rows, bias_q,
                  sem, x_sem, send, recv):
     steps, kvs, group = cfg
     batch, d_model = x_buf.shape[1], x_buf.shape[2]
@@ -36,13 +37,11 @@
     for copy in x_copies:
         copy.start()
     head_at = pl.multiple_of(c * LANES, LANES)
-    pieces = []
-    for at in range(0, head_cols, COLS):
-        width = min(COLS, head_cols - at)
-        pieces.append((wq_hbm.at[:, pl.ds(pl.multiple_of(c * head_cols + at, LANES), width)], at, width))
-    pieces.append((wk_hbm.at[:, pl.ds(head_at, LANES)], head_cols, LANES))
-    pieces.append((wv_hbm.at[:, pl.ds(head_at, LANES)], head_cols + LANES, LANES))
-    w_copies = [pltpu.make_async_copy(src, w_buf.at[:, at:at + width], sem.at[n]) for n, (src, at, width) in enumerate(pieces)]
+    n_q = head_cols // COLS
+    w_copies = [pltpu.make_async_copy(wq_hbm.at[:, pl.ds(pl.multiple_of(c * head_cols + n * COLS, LANES), COLS)], wq_buf.at[n], sem.at[n])
+                for n in range(n_q)]
+    w_copies += [pltpu.make_async_copy(src.at[:, pl.ds(head_at, LANES)], wkv_buf.at[n], sem.at[n_q + n])
+                 for n, src in enumerate((wk_hbm, wv_hbm))]
     for copy in w_copies:
         copy.start()
 
@@ -94,17 +93,14 @@
     kv_bias = [jnp.where(c == 0, ref[0:1, :].astype(F32), ref[1:2, :].astype(F32)) for ref in (bk_ref, bv_ref)]
     total = group + 2
     per = COLS // LANES
-    done = 0
-    for first in range(0, total, per):
-        count = min(per, total - first)
-        upto = (first + count) * LANES
-        while done < len(pieces) and pieces[done][1] < upto:
-            w_copies[done].wait()
-            done += 1
-        block = jnp.dot(hid[...], w_buf[:, first * LANES:upto], preferred_element_type=F32)
-        for n in range(first, first + count):
+    groups = [(range(n * per, (n + 1) * per), wq_buf.at[n], w_copies[n]) for n in range(n_q)]
+    groups += [((group + n,), wkv_buf.at[n], w_copies[n_q + n]) for n in range(2)]
+    for heads, weight, copy in groups:
+        copy.wait()
+        block = jnp.dot(hid[...], weight[...], preferred_element_type=F32)
+        for at, n in enumerate(heads):
             bias = bias_q[pl.ds(c * group + n, 1), :] if n < group else kv_bias[n - group]
-            vec = (block[:, (n - first) * LANES:(n - first + 1) * LANES] + bias).astype(BF16).astype(F32)
+            vec = (block[:, at * LANES:(at + 1) * LANES] + bias).astype(BF16).astype(F32)
             mine[n] = rotate(vec) if n <= group else vec
             swap(n).start()
             place(n, c, mine.at[n])
@@ -145,7 +141,8 @@
         scratch_shapes=[
             pltpu.VMEM((steps, batch, d_model), BF16),
             pltpu.VMEM((steps * batch, d_model), BF16),
-            pltpu.VMEM((d_model, (group + 2) * LANES), BF16),
+            pltpu.VMEM((group * LANES // COLS, d_model, COLS), BF16),
+            pltpu.VMEM((2, d_model, LANES), BF16),
             pltpu.VMEM((group + 2, steps * batch, LANES), F32),
             pltpu.VMEM((group + 2, steps * batch, LANES), F32),
             pltpu.VMEM((batch, LANES), F32),
@@ -579,15 +576,20 @@
         copy.wait_recv()
     hid_b[...] = hid[...].astype(BF16)
 
-    @pl.loop(0, chunks)
-    def _(j):
-        slot = slot_of(j)
-        wait_item(slot)
-        pre = jnp.dot(hid_b[...], ring[slot], preferred_element_type=F32) + bias_of(bfc_rows, c * chunks + j, CHUNK)
-        cube = pre * pre * pre
-        act = 0.5 * pre * (1.0 + jnp.tanh(math.sqrt(2.0 / math.pi) * (pre + 0.044715 * cube)))
-        g_buf[:, chunk_cols(j)] = act.astype(BF16)
-        load_item(j + RING, slot)
+    together = 3
+
+    @pl.loop(0, chunks // together)
+    def _(first):
+        group_of = [first * together + e for e in range(together)]
+        for j in group_of:
+            wait_item(slot_of(j))
+        for j in group_of:
+            pre = jnp.dot(hid_b[...], ring[slot_of(j)], preferred_element_type=F32) + bias_of(bfc_rows, c * chunks + j, CHUNK)
+            cube = pre * pre * pre
+            act = 0.5 * pre * (1.0 + jnp.tanh(math.sqrt(2.0 / math.pi) * (pre + 0.044715 * cube)))
+            g_buf[:, chunk_cols(j)] = act.astype(BF16)
+        for j in group_of:
+            load_item(j + RING, slot_of(j))
 
     def block(j, core, xx):
         return y_all.at[j, pl.ds(2 * core, 2), pl.ds(pl.multiple_of(xx * half, 8), half), :]
@@ -701,11 +703,11 @@
     ]
     return pl.pallas_call(
         functools.partial(tail_kernel, cfg),
-        out_shape=jax.ShapeDtypeStruct((steps, batch, d_model), BF16),
+        out_shape=pltpu.VMEM((steps, batch, d_model), BF16),
         in_specs=[hbm] * 6 + [vm] * 5,
         out_specs=vm,
         scratch_shapes=scratch,
-        compiler_params=pltpu.CompilerParams(collective_id=0, has_side_effects=True, vmem_limit_bytes=VMEM_CAP),
+        compiler_params=pltpu.CompilerParams(collective_id=0, has_side_effects=True, vmem_limit_bytes=TAIL_VMEM),
         cost_estimate=pl.CostEstimate(flops=2 * rows * d_model * (head_cols + 2 * ff_own), bytes_accessed=100_000_000, transcendentals=0),
         name="tail",
     )(own, x_in, x_steps, w_o, w_fc, w_proj, tiles(b_o), tiles(gain), tiles(shift), tiles(b_fc), tiles(b_proj))

time: 135 us -> 129 us (0.956)
  Pallas kernels: 126 us -> 122 us
  local copies, waits for them, and re-layouts: 2.8 us -> 1.21 us
    pallas_call x1, Pallas kernels: 70.5 us -> 68 us  [tail(): pl.pallas_call(functools.partial(tail_kernel, cfg), out_shape=pltpu.VMEM(...]
    unnamed x1, local copies, waits for them, and re-layouts: 2.8 us -> 1.21 us
    pallas_call x1, Pallas kernels: 17.1 us -> 15.5 us  [front(): pl.pallas_call(functools.partial(front_kernel, (steps, kvs, group)), out_...]
  transfers between devices with their start and end apart: 1 -> 1, of which waited for: 1 -> 1; matrix products, arithmetic and copies ran while one was open for 0% -> 0% of each run, Pallas kernels for 14% -> 15%
where the time goes in v6:
time: 129 us
  Pallas kernels  122 us (95%)
  starting transfers between devices  2.34 us (2%)
  waiting for transfers between devices  2.29 us (2%)
    pallas_call x1, Pallas kernels, tail(): pl.pallas_call(functools.partial(tail_kernel, cfg), out_shape=pltpu.VMEM(...  68 us
    pallas_call x2, Pallas kernels, attend(): pl.pallas_call(functools.partial(attend_kernel, (steps, kvs, group, slots...  38.3 us
    pallas_call x1, Pallas kernels, front(): pl.pallas_call(functools.partial(front_kernel, (steps, kvs, group)), out_...  15.5 us
  transfers between devices with their start and end apart: 1, of which 1 were waited for; matrix products, arithmetic and copies ran while one was open for 0% of the time, Pallas kernels for 15%

profile of v6, /device:TPU:0, one launch (start us, length us, event | category | flops | bytes accessed | tf_op | source)
XLA Modules:
  0.0 128.9 jit_solution(12722441956144308600)
XLA Ops:
  0.6 0.5 multiply_power_fusion.freq_ref
  1.2 15.5 %front.1 = (bf16[48,72,128]{2,1,0:T(8,128)(2,1)}, bf16[48,16,128]{2,1,0:T(8,128)(2,1)}, bf16[48,16,128]{2,1,0:T(8,128)(2,1)}) custom-call(s32[48]{0:T(128)} %pos_ref.5, bf16[4,48,4608]{2,1,0:T(8,128)(2,1)} %x_hbm.3, f32[1,64]{1,0:T(1,128)} %multiply_power_fusion.freq_ref, bf16[36,128]{1,0:T(8,128)(2,1)} %bitcast.21, bf16[36,128]{1,0:T(8,128)(2,1)} %bitcast.22, ...), custom_call_target="tpu_custom_call" | custom-call | flops 2491416576 | bytes 12976128 | tf_op jit(solution)/shard_map/front/pallas_call | solution.py:132
  16.7 19.1 %attend_peer.1 = (bf16[48,2048,128]{2,1,0:T(8,128)(2,1)}, bf16[48,2048,128]{2,1,0:T(8,128)(2,1)}, f32[4,24,2432]{2,1,0:T(8,128)}) custom-call(s32[48]{0:T(128)} %pos_ref.5, bf16[48,72,128]{2,1,0:T(8,128)(2,1)} %get-tuple-element.12.q_hbm, bf16[48,16,128]{2,1,0:T(8,128)(2,1)} %get-tuple-element.13.kn_hbm, bf16[48,16,128]{2,1,0:T(8,128)(2,1)} %get-tuple-element.14.vn_hbm, ...), custom_call_target="tpu_custom_call" | custom-call | flops 20000000000 | bytes 50331648 | tf_op jit(solution)/shard_map/attend_peer/pallas_call | solution.py:341
  35.8 2.3 %collective-permute-start = (f32[4,24,2432]{2,1,0:T(8,128)}, f32[4,24,2432]{2,1,0:T(8,128)}, u32[]{:S(2)}, u32[]{:S(2)}) collective-permute-start(f32[4,24,2432]{2,1,0:T(8,128)} %get-tuple-element.18), channel_id=1, source_target_pairs={{0,2},{1,3},{2,0},{3,1},{4,6},{5,7},{6,4},{7,5}} | collective-permute-start | bytes 2801672 | tf_op jit(solution)/shard_map/ppermute | solution.py:740
  38.2 19.1 %attend_own.1 = (bf16[48,2048,128]{2,1,0:T(8,128)(2,1)}, bf16[48,2048,128]{2,1,0:T(8,128)(2,1)}, f32[4,24,2432]{2,1,0:T(8,128)}) custom-call(s32[48]{0:T(128)} %pos_ref.5, bf16[48,72,128]{2,1,0:T(8,128)(2,1)} %get-tuple-element.12.q_hbm, bf16[48,16,128]{2,1,0:T(8,128)(2,1)} %get-tuple-element.13.kn_hbm, ...), custom_call_target="tpu_custom_call", output_to_operand_aliasing={{0}: (6, {}), {1}: (7, {})} | custom-call | flops 20000000000 | bytes 50331648 | tf_op jit(solution)/shard_map/attend_own/pallas_call | solution.py:341
  57.3 2.3 %collective-permute-done.xin_hbm = f32[4,24,2432]{2,1,0:T(8,128)} collective-permute-done((f32[4,24,2432]{2,1,0:T(8,128)}, f32[4,24,2432]{2,1,0:T(8,128)}, u32[]{:S(2)}, u32[]{:S(2)}) %collective-permute-start) | collective-permute-done | bytes 933920 | tf_op jit(solution)/shard_map/ppermute | solution.py:740
  59.6 68.0 %tail.1 = bf16[4,48,4608]{2,1,0:T(8,128)(2,1)S(1)} custom-call(f32[4,24,2432]{2,1,0:T(8,128)} %get-tuple-element.17.own_hbm, f32[4,24,2432]{2,1,0:T(8,128)} %collective-permute-done.xin_hbm, bf16[4,48,4608]{2,1,0:T(8,128)(2,1)} %x_hbm.3, bf16[2304,4608]{1,0:T(8,128)(2,1)} %wo_hbm.1, bf16[4608,9216]{1,0:T(8,128)(2,1)} %wfc_hbm.1, ...), custom_call_target="tpu_custom_call" | custom-call | flops 9172942848 | bytes 100000000 | tf_op jit(solution)/shard_map/tail/pallas_call | solution.py:704
  127.7 1.2 copy.28
Async XLA Ops:
  35.8 23.8 %collective-permute-start = (f32[4,24,2432]{2,1,0:T(8,128)}, f32[4,24,2432]{2,1,0:T(8,128)}, u32[]{:S(2)}, u32[]{:S(2)}) collective-permute-start(f32[4,24,2432]{2,1,0:T(8,128)} %get-tuple-element.18), channel_id=1, source_target_pairs={{0,2},{1,3},{2,0},{3,1},{4,6},{5,7},{6,4},{7,5}} | collective-permute-start | bytes 2801672 | tf_op jit(solution)/shard_map/ppermute | solution.py:740

commit v7 on v6

--- a/solution.py
+++ b/solution.py
@@ -42,7 +42,7 @@
                 for n in range(n_q)]
     w_copies += [pltpu.make_async_copy(src.at[:, pl.ds(head_at, LANES)], wkv_buf.at[n], sem.at[n_q + n])
                  for n, src in enumerate((wk_hbm, wv_hbm))]
-    for copy in w_copies:
+    for copy in w_copies[:2]:
         copy.start()
 
     barrier = pltpu.get_barrier_semaphore()
@@ -67,6 +67,8 @@
         mean = jnp.mean(wide, axis=-1, keepdims=True)
         cent = wide - mean
         rstd = lax.rsqrt(jnp.mean(cent * cent, axis=-1, keepdims=True) + LN_EPS)
+        for copy in {1: w_copies[2:3], 3: w_copies[3:]}.get(s, ()):
+            copy.start()
         for n in range(d_model // LANES):
             cols = slice(n * LANES, (n + 1) * LANES)
             hid[s * batch:(s + 1) * batch, cols] = (cent[:, cols] * rstd * gain[n:n + 1, :] + shift[n:n + 1, :]).astype(BF16)
@@ -399,6 +401,10 @@
     ypeer = {"tp": 1 - y}
     MESH = pl.DeviceIdType.MESH
 
+    barrier = pltpu.get_barrier_semaphore()
+    for who in (sib, xpeer, ypeer):
+        pl.semaphore_signal(barrier, inc=1, device_id=who, device_id_type=MESH)
+
     def chunk_cols(j):
         return pl.ds(pl.multiple_of(j * CHUNK, CHUNK), CHUNK)
 
@@ -435,13 +441,8 @@
         (own_hbm.at[:, :, my_cols], my_own), (xin_hbm.at[:, :, my_cols], my_x)))]
     for copy in locals_:
         copy.start()
-    for j in range(chunks):
-        wo_copy(jnp.int32(j)).start()
     x_copy = pltpu.make_async_copy(x_hbm.at[pl.ds(2 * c, 2), pl.ds(pl.multiple_of(x * half, 8), half), :], x_buf, x_sem)
     x_copy.start()
-    barrier = pltpu.get_barrier_semaphore()
-    for who in (sib, xpeer, ypeer):
-        pl.semaphore_signal(barrier, inc=1, device_id=who, device_id_type=MESH)
     pl.semaphore_wait(barrier, 3)
 
     def remote(src, dst, kind, who):
@@ -453,6 +454,8 @@
              remote(own_hbm.at[:, :, sib_cols], sib_own, C_OWN_O, sib), remote(xin_hbm.at[:, :, sib_cols], sib_x, C_X_O, sib)]
     for copy in swaps:
         copy.start()
+    for j in range(chunks):
+        wo_copy(jnp.int32(j)).start()
     bo_rows[...] = bo_ref[...].astype(F32)
     bfc_rows[...] = bfc_ref[...].astype(F32)
     bproj_rows[...] = bproj_ref[...].astype(F32)

time: 129 us -> 126 us (0.977)
  Pallas kernels: 122 us -> 119 us
    pallas_call x1, Pallas kernels: 15.5 us -> 12.9 us  [front(): pl.pallas_call(functools.partial(front_kernel, (steps, kvs, group)), out_...]
where the time goes in v7:
time: 126 us
  Pallas kernels  119 us (94%)
  waiting for transfers between devices  2.4 us (2%)
  starting transfers between devices  2.33 us (2%)
    pallas_call x1, Pallas kernels, tail(): pl.pallas_call(functools.partial(tail_kernel, cfg), out_shape=pltpu.VMEM(...  67.9 us
    pallas_call x2, Pallas kernels, attend(): pl.pallas_call(functools.partial(attend_kernel, (steps, kvs, group, slots...  38.3 us
    pallas_call x1, Pallas kernels, front(): pl.pallas_call(functools.partial(front_kernel, (steps, kvs, group)), out_...  12.9 us
  transfers between devices with their start and end apart: 1, of which 1 were waited for; matrix products, arithmetic and copies ran while one was open for 0% of the time, Pallas kernels for 15%

profile of v7, /device:TPU:0, one launch (start us, length us, event | category | flops | bytes accessed | tf_op | source)
XLA Modules:
  0.0 126.2 jit_solution(15970746189118651895)
XLA Ops:
  0.6 0.5 multiply_power_fusion.freq_ref
  1.2 12.9 %front.1 = (bf16[48,72,128]{2,1,0:T(8,128)(2,1)}, bf16[48,16,128]{2,1,0:T(8,128)(2,1)}, bf16[48,16,128]{2,1,0:T(8,128)(2,1)}) custom-call(s32[48]{0:T(128)} %pos_ref.5, bf16[4,48,4608]{2,1,0:T(8,128)(2,1)} %x_hbm.3, f32[1,64]{1,0:T(1,128)} %multiply_power_fusion.freq_ref, bf16[36,128]{1,0:T(8,128)(2,1)} %bitcast.21, bf16[36,128]{1,0:T(8,128)(2,1)} %bitcast.22, ...), custom_call_target="tpu_custom_call" | custom-call | flops 2491416576 | bytes 12976128 | tf_op jit(solution)/shard_map/front/pallas_call | solution.py:134
  14.1 19.2 %attend_peer.1 = (bf16[48,2048,128]{2,1,0:T(8,128)(2,1)}, bf16[48,2048,128]{2,1,0:T(8,128)(2,1)}, f32[4,24,2432]{2,1,0:T(8,128)}) custom-call(s32[48]{0:T(128)} %pos_ref.5, bf16[48,72,128]{2,1,0:T(8,128)(2,1)} %get-tuple-element.12.q_hbm, bf16[48,16,128]{2,1,0:T(8,128)(2,1)} %get-tuple-element.13.kn_hbm, bf16[48,16,128]{2,1,0:T(8,128)(2,1)} %get-tuple-element.14.vn_hbm, ...), custom_call_target="tpu_custom_call" | custom-call | flops 20000000000 | bytes 50331648 | tf_op jit(solution)/shard_map/attend_peer/pallas_call | solution.py:343
  33.3 2.3 %collective-permute-start = (f32[4,24,2432]{2,1,0:T(8,128)}, f32[4,24,2432]{2,1,0:T(8,128)}, u32[]{:S(2)}, u32[]{:S(2)}) collective-permute-start(f32[4,24,2432]{2,1,0:T(8,128)} %get-tuple-element.18), channel_id=1, source_target_pairs={{0,2},{1,3},{2,0},{3,1},{4,6},{5,7},{6,4},{7,5}} | collective-permute-start | bytes 2801672 | tf_op jit(solution)/shard_map/ppermute | solution.py:743
  35.6 19.1 %attend_own.1 = (bf16[48,2048,128]{2,1,0:T(8,128)(2,1)}, bf16[48,2048,128]{2,1,0:T(8,128)(2,1)}, f32[4,24,2432]{2,1,0:T(8,128)}) custom-call(s32[48]{0:T(128)} %pos_ref.5, bf16[48,72,128]{2,1,0:T(8,128)(2,1)} %get-tuple-element.12.q_hbm, bf16[48,16,128]{2,1,0:T(8,128)(2,1)} %get-tuple-element.13.kn_hbm, ...), custom_call_target="tpu_custom_call", output_to_operand_aliasing={{0}: (6, {}), {1}: (7, {})} | custom-call | flops 20000000000 | bytes 50331648 | tf_op jit(solution)/shard_map/attend_own/pallas_call | solution.py:343
  54.7 2.4 %collective-permute-done.xin_hbm = f32[4,24,2432]{2,1,0:T(8,128)} collective-permute-done((f32[4,24,2432]{2,1,0:T(8,128)}, f32[4,24,2432]{2,1,0:T(8,128)}, u32[]{:S(2)}, u32[]{:S(2)}) %collective-permute-start) | collective-permute-done | bytes 933920 | tf_op jit(solution)/shard_map/ppermute | solution.py:743
  57.1 67.9 %tail.1 = bf16[4,48,4608]{2,1,0:T(8,128)(2,1)S(1)} custom-call(f32[4,24,2432]{2,1,0:T(8,128)} %get-tuple-element.17.own_hbm, f32[4,24,2432]{2,1,0:T(8,128)} %collective-permute-done.xin_hbm, bf16[4,48,4608]{2,1,0:T(8,128)(2,1)} %x_hbm.3, bf16[2304,4608]{1,0:T(8,128)(2,1)} %wo_hbm.1, bf16[4608,9216]{1,0:T(8,128)(2,1)} %wfc_hbm.1, ...), custom_call_target="tpu_custom_call" | custom-call | flops 9172942848 | bytes 100000000 | tf_op jit(solution)/shard_map/tail/pallas_call | solution.py:707
  125.0 1.2 copy.28
Async XLA Ops:
  33.3 23.9 %collective-permute-start = (f32[4,24,2432]{2,1,0:T(8,128)}, f32[4,24,2432]{2,1,0:T(8,128)}, u32[]{:S(2)}, u32[]{:S(2)}) collective-permute-start(f32[4,24,2432]{2,1,0:T(8,128)} %get-tuple-element.18), channel_id=1, source_target_pairs={{0,2},{1,3},{2,0},{3,1},{4,6},{5,7},{6,4},{7,5}} | collective-permute-start | bytes 2801672 | tf_op jit(solution)/shard_map/ppermute | solution.py:743

commit v8 on v7

--- a/solution.py
+++ b/solution.py
@@ -377,8 +377,8 @@
 PIECE = 256
 RING = 9
 WO_SLOTS = 3
-(C_OWN_O, C_X_O, C_OWN_E, C_X_E, C_HID_A, C_HID_B) = range(6)
-(W_CORE, W_Y, J_CORE, J_Y, J_OWN_X, J_OWN_C, J_FWD_C) = range(7)
+(C_OWN_O, C_X_O, C_OWN_E, C_X_E) = range(4)
+(W_CORE, W_Y, J_CORE, J_Y, J_OWN_X, J_OWN_C, J_FWD_C, W_MID) = range(8)
 
 
 def tail_kernel(cfg, own_hbm, xin_hbm, x_hbm, wo_hbm, wfc_hbm, wproj_hbm, bo_ref, gain_ref, shift_ref, bfc_ref, bproj_ref,
@@ -551,33 +551,37 @@
         load_item(jnp.int32(k), slot_of(k))
     x_copy.wait()
 
+    def share_mid(u):
+        piece = hid.at[pair_rows(c), piece_cols(u)]
+        return jcopy(piece, piece, W_MID, u, sib)
+
     @pl.loop(0, pieces)
     def _(u):
         cols = piece_cols(u)
         to_y(w_half, w_y, W_Y, u).wait_recv()
         x_in = x_buf[:, :, cols].astype(F32).reshape(pair, PIECE)
-        x_mid[:, cols] = (x_in + y_sum(w_half[u], w_y[u]) + bias_of(bo_rows, u, PIECE)).astype(BF16).astype(F32)
+        x_new = (x_in + y_sum(w_half[u], w_y[u]) + bias_of(bo_rows, u, PIECE)).astype(BF16).astype(F32)
+        x_mid[:, cols] = x_new
+        hid[pair_rows(c), cols] = x_new
+        share_mid(u).start()
 
     gain = gain_ref[...].astype(F32)
     shift = shift_ref[...].astype(F32)
     d_model = x_mid.shape[1]
-    hid_copies = []
     for part in range(2):
-        src = slice(part * half, (part + 1) * half)
-        dst = pl.ds(pl.multiple_of(c * pair + part * half, 8), half)
-        rows = x_mid[src, :]
+        if part == 1:
+            @pl.loop(0, pieces)
+            def _(u):
+                share_mid(u).wait_recv()
+
+        where = pl.ds(pl.multiple_of((c if part == 0 else 1 - c) * pair, 16), pair)
+        rows = hid[where, :]
         mean = jnp.mean(rows, axis=-1, keepdims=True)
         cent = rows - mean
         rstd = lax.rsqrt(jnp.mean(cent * cent, axis=-1, keepdims=True) + LN_EPS)
         for n in range(d_model // LANES):
             cols = slice(n * LANES, (n + 1) * LANES)
-            hid[dst, cols] = (cent[:, cols] * rstd * gain[n:n + 1, :] + shift[n:n + 1, :]).astype(BF16).astype(F32)
-        copy = remote(hid.at[dst, :], hid.at[dst, :], (C_HID_A, C_HID_B)[part], sib)
-        copy.start()
-        hid_copies.append(copy)
-    for copy in hid_copies:
-        copy.wait_recv()
-    hid_b[...] = hid[...].astype(BF16)
+            hid_b[where, cols] = (cent[:, cols] * rstd * gain[n:n + 1, :] + shift[n:n + 1, :]).astype(BF16)
 
     together = 3
 
@@ -639,13 +643,14 @@
         stage(it, 11, do_forward)
         stage(it, 13, do_store)
 
-    for copy in swaps + hid_copies:
+    for copy in swaps:
         copy.wait_send()
 
     @pl.loop(0, pieces)
     def _(j):
         to_core(w_part, w_core, W_CORE, j).wait_send()
         to_y(w_half, w_y, W_Y, j).wait_send()
+        share_mid(j).wait_send()
         to_core(p_part, p_core, J_CORE, j).wait_send()
         to_y(p_half, p_y, J_Y, j).wait_send()
         for kind in (J_OWN_X, J_OWN_C, J_FWD_C):
@@ -695,10 +700,10 @@
         pltpu.VMEM((d_model // LANES, LANES), F32),
         pltpu.VMEM((2 * ff_own // LANES, LANES), F32),
         pltpu.VMEM((d_model // LANES, LANES), F32),
-        pltpu.SemaphoreType.DMA((6,)),
-        pltpu.SemaphoreType.DMA((6,)),
-        pltpu.SemaphoreType.DMA((7, pieces)),
-        pltpu.SemaphoreType.DMA((7, pieces)),
+        pltpu.SemaphoreType.DMA((4,)),
+        pltpu.SemaphoreType.DMA((4,)),
+        pltpu.SemaphoreType.DMA((8, pieces)),
+        pltpu.SemaphoreType.DMA((8, pieces)),
         pltpu.SemaphoreType.DMA((4,)),
         pltpu.SemaphoreType.DMA((chunks,)),
         pltpu.SemaphoreType.DMA,

time: 126 us -> 126 us (level)
  no operation moved by 1% of the time
where the time goes in v8:
time: 126 us; the launch traced here: 125 us
  Pallas kernels  118 us (94%)
  waiting for transfers between devices  2.4 us (2%)
  starting transfers between devices  2.33 us (2%)
    pallas_call x1, Pallas kernels, tail(): pl.pallas_call(functools.partial(tail_kernel, cfg), out_shape=pltpu.VMEM(...  67 us
    pallas_call x2, Pallas kernels, attend(): pl.pallas_call(functools.partial(attend_kernel, (steps, kvs, group, slots...  38.3 us
    pallas_call x1, Pallas kernels, front(): pl.pallas_call(functools.partial(front_kernel, (steps, kvs, group)), out_...  12.9 us
  transfers between devices with their start and end apart: 1, of which 1 were waited for; matrix products, arithmetic and copies ran while one was open for 0% of the time, Pallas kernels for 15%

profile of v8, /device:TPU:0, one launch (start us, length us, event | category | flops | bytes accessed | tf_op | source)
XLA Modules:
  0.0 125.3 jit_solution(10453763222362509952)
XLA Ops:
  0.6 0.5 multiply_power_fusion.freq_ref
  1.2 12.9 %front.1 = (bf16[48,72,128]{2,1,0:T(8,128)(2,1)}, bf16[48,16,128]{2,1,0:T(8,128)(2,1)}, bf16[48,16,128]{2,1,0:T(8,128)(2,1)}) custom-call(s32[48]{0:T(128)} %pos_ref.5, bf16[4,48,4608]{2,1,0:T(8,128)(2,1)} %x_hbm.3, f32[1,64]{1,0:T(1,128)} %multiply_power_fusion.freq_ref, bf16[36,128]{1,0:T(8,128)(2,1)} %bitcast.21, bf16[36,128]{1,0:T(8,128)(2,1)} %bitcast.22, ...), custom_call_target="tpu_custom_call" | custom-call | flops 2491416576 | bytes 12976128 | tf_op jit(solution)/shard_map/front/pallas_call | solution.py:134
  14.1 19.2 %attend_peer.1 = (bf16[48,2048,128]{2,1,0:T(8,128)(2,1)}, bf16[48,2048,128]{2,1,0:T(8,128)(2,1)}, f32[4,24,2432]{2,1,0:T(8,128)}) custom-call(s32[48]{0:T(128)} %pos_ref.5, bf16[48,72,128]{2,1,0:T(8,128)(2,1)} %get-tuple-element.12.q_hbm, bf16[48,16,128]{2,1,0:T(8,128)(2,1)} %get-tuple-element.13.kn_hbm, bf16[48,16,128]{2,1,0:T(8,128)(2,1)} %get-tuple-element.14.vn_hbm, ...), custom_call_target="tpu_custom_call" | custom-call | flops 20000000000 | bytes 50331648 | tf_op jit(solution)/shard_map/attend_peer/pallas_call | solution.py:343
  33.3 2.3 %collective-permute-start = (f32[4,24,2432]{2,1,0:T(8,128)}, f32[4,24,2432]{2,1,0:T(8,128)}, u32[]{:S(2)}, u32[]{:S(2)}) collective-permute-start(f32[4,24,2432]{2,1,0:T(8,128)} %get-tuple-element.18), channel_id=1, source_target_pairs={{0,2},{1,3},{2,0},{3,1},{4,6},{5,7},{6,4},{7,5}} | collective-permute-start | bytes 2801672 | tf_op jit(solution)/shard_map/ppermute | solution.py:748
  35.6 19.1 %attend_own.1 = (bf16[48,2048,128]{2,1,0:T(8,128)(2,1)}, bf16[48,2048,128]{2,1,0:T(8,128)(2,1)}, f32[4,24,2432]{2,1,0:T(8,128)}) custom-call(s32[48]{0:T(128)} %pos_ref.5, bf16[48,72,128]{2,1,0:T(8,128)(2,1)} %get-tuple-element.12.q_hbm, bf16[48,16,128]{2,1,0:T(8,128)(2,1)} %get-tuple-element.13.kn_hbm, ...), custom_call_target="tpu_custom_call", output_to_operand_aliasing={{0}: (6, {}), {1}: (7, {})} | custom-call | flops 20000000000 | bytes 50331648 | tf_op jit(solution)/shard_map/attend_own/pallas_call | solution.py:343
  54.7 2.4 %collective-permute-done.xin_hbm = f32[4,24,2432]{2,1,0:T(8,128)} collective-permute-done((f32[4,24,2432]{2,1,0:T(8,128)}, f32[4,24,2432]{2,1,0:T(8,128)}, u32[]{:S(2)}, u32[]{:S(2)}) %collective-permute-start) | collective-permute-done | bytes 933920 | tf_op jit(solution)/shard_map/ppermute | solution.py:748
  57.1 67.0 %tail.1 = bf16[4,48,4608]{2,1,0:T(8,128)(2,1)S(1)} custom-call(f32[4,24,2432]{2,1,0:T(8,128)} %get-tuple-element.17.own_hbm, f32[4,24,2432]{2,1,0:T(8,128)} %collective-permute-done.xin_hbm, bf16[4,48,4608]{2,1,0:T(8,128)(2,1)} %x_hbm.3, bf16[2304,4608]{1,0:T(8,128)(2,1)} %wo_hbm.1, bf16[4608,9216]{1,0:T(8,128)(2,1)} %wfc_hbm.1, ...), custom_call_target="tpu_custom_call" | custom-call | flops 9172942848 | bytes 100000000 | tf_op jit(solution)/shard_map/tail/pallas_call | solution.py:712
  124.1 1.2 copy.28
Async XLA Ops:
  33.3 23.9 %collective-permute-start = (f32[4,24,2432]{2,1,0:T(8,128)}, f32[4,24,2432]{2,1,0:T(8,128)}, u32[]{:S(2)}, u32[]{:S(2)}) collective-permute-start(f32[4,24,2432]{2,1,0:T(8,128)} %get-tuple-element.18), channel_id=1, source_target_pairs={{0,2},{1,3},{2,0},{3,1},{4,6},{5,7},{6,4},{7,5}} | collective-permute-start | bytes 2801672 | tf_op jit(solution)/shard_map/ppermute | solution.py:748
